TPU v7x, 32 devices: a whole 2x2x4 slice. The times are simulated.
32 devices in a mesh: rot: 2 (over y), py: 4 (over x, core), pz: 4 (over z).
Axes of the slice: x: 2, y: 2, z: 4, core: 2. Of those that a mesh axis runs over, the one named last changes fastest.
Arguments:
- receptor_grids: float32 [2, 128, 128, 128], P('rot', None, 'py', 'pz'), may hold values from -0.09375 to 0.09375
- ligand_cells: int32 [8, 2048], P('rot'), may hold values from 0 to 2097151
- atom_shape: float32 [2048], replicated, may hold values from 0.5 to 2
- atom_charges: float32 [2048], replicated, may hold values from -3 to 3
Outputs:
- correlation: float32 [8, 128, 128, 128], P('rot', 'py', 'pz')
- best_score: float32 [8], P('rot')
Inputs may be any that keep to these rules, and one draw needn't show every extreme that they name: Atom a of rotation r lies in cell (x, y, z) with ligand_cells[r, a] = x 128^2 + y * 128 + z; several atoms may share a cell.
All inputs are finite; a program needn't handle non-finite values.
Results may differ from a plain program's by a relative error of at most 0.000086.
Values sent between devices are 32-bit elements; how exact they have to be, the bound alone decides.
No kernel may reach another device: no remote copies, remote signals or barrier semaphores. Data moves between devices by JAX's collectives and lax.ppermute only.
A program may use at most 192 MiB of HBM per device.

v0:
```python
import math

import jax
import jax.numpy as jnp
from jax import lax
from jax.sharding import PartitionSpec as P

N = 128


exact_mode = lax.Precision.HIGHEST


def twiddle(length, inverse):
    counter = jnp.arange(length, dtype=jnp.int32)
    phases = counter[:, None] * counter[None, :] % length
    angles = phases.astype(jnp.float32) * (2.0 * math.pi / length)
    factor = 1.0 if inverse else -1.0
    return (jnp.cos(angles), factor * jnp.sin(angles))


def transform(real_part, imag_part, pattern, inverse):
    cosine, sine_table = twiddle(N, inverse)
    if imag_part is None:
        return (
            jnp.einsum(pattern, real_part, cosine, precision=exact_mode),
            jnp.einsum(pattern, real_part, sine_table, precision=exact_mode),
        )
    new_real = jnp.einsum(pattern, real_part, cosine, precision=exact_mode) - jnp.einsum(
        pattern, imag_part, sine_table, precision=exact_mode
    )
    new_imag = jnp.einsum(pattern, real_part, sine_table, precision=exact_mode) + jnp.einsum(
        pattern, imag_part, cosine, precision=exact_mode
    )
    return (new_real, new_imag)


def receptor_forward(grids):
    real_part, imag_part = transform(grids, None, "cxyz,xk->ckyz", False)
    real_part, imag_part = (
        lax.all_to_all(real_part, "pz", split_axis=1, concat_axis=3, tiled=True),
        lax.all_to_all(imag_part, "pz", split_axis=1, concat_axis=3, tiled=True),
    )
    real_part, imag_part = transform(real_part, imag_part, "cxyz,zk->cxyk", False)
    real_part, imag_part = (
        lax.all_to_all(real_part, "py", split_axis=3, concat_axis=2, tiled=True),
        lax.all_to_all(imag_part, "py", split_axis=3, concat_axis=2, tiled=True),
    )
    return transform(real_part, imag_part, "cxyz,yk->cxkz", False)


def inverse_transform(real_part, imag_part):
    real_part, imag_part = transform(real_part, imag_part, "bxyz,yk->bxkz", True)
    pieces = (
        lax.all_to_all(real_part, "py", split_axis=2, concat_axis=3, tiled=True),
        lax.all_to_all(imag_part, "py", split_axis=2, concat_axis=3, tiled=True),
    )
    real_part, imag_part = transform(pieces[0], pieces[1], "bxyz,zk->bxyk", True)
    pieces = (
        lax.all_to_all(real_part, "pz", split_axis=3, concat_axis=1, tiled=True),
        lax.all_to_all(imag_part, "pz", split_axis=3, concat_axis=1, tiled=True),
    )
    return transform(pieces[0], pieces[1], "bxyz,xk->byzk", True)


def on_device(receptor_grids, ligand_cells, atom_shape, atom_charges):
    planes = lax.all_gather(receptor_grids, "rot", axis=0, tiled=True)
    receptor_real, receptor_imag = receptor_forward(planes)
    x_block = N // lax.axis_size("pz")
    z_block = N // lax.axis_size("py")
    kx_values = lax.axis_index("pz") * x_block + jnp.arange(x_block, dtype=jnp.int32)
    kz_values = lax.axis_index("py") * z_block + jnp.arange(z_block, dtype=jnp.int32)
    ky_values = jnp.arange(N, dtype=jnp.int32)
    weights = jnp.stack((atom_shape, atom_charges), 1)
    step_angle = 2.0 * math.pi / N

    def rotation_product(atom_cells):
        coord_x = atom_cells // (N * N)
        coord_y = atom_cells // N % N
        coord_z = atom_cells % N
        angle_y = (coord_y[:, None] * ky_values[None, :] % N).astype(jnp.float32) * step_angle
        cos_y = jnp.cos(angle_y)
        sin_y = jnp.sin(angle_y)
        phase_xz = (
            coord_x[:, None, None] * kx_values[None, :, None]
            + coord_z[:, None, None] * kz_values[None, None, :]
        ) % N
        angle_xz = phase_xz.astype(jnp.float32) * step_angle
        cos_xz = (weights[:, :, None, None] * jnp.cos(angle_xz)[:, None]).reshape(
            atom_cells.shape[0], -1
        )
        sin_xz = (weights[:, :, None, None] * jnp.sin(angle_xz)[:, None]).reshape(
            atom_cells.shape[0], -1
        )
        conj_real = jnp.einsum("ay,ab->yb", cos_y, cos_xz, precision=exact_mode) - jnp.einsum(
            "ay,ab->yb", sin_y, sin_xz, precision=exact_mode
        )
        conj_imag = jnp.einsum("ay,ab->yb", cos_y, sin_xz, precision=exact_mode) + jnp.einsum(
            "ay,ab->yb", sin_y, cos_xz, precision=exact_mode
        )
        conj_real = conj_real.reshape(N, 2, x_block, z_block)
        conj_imag = conj_imag.reshape(N, 2, x_block, z_block)
        product_real = jnp.einsum(
            "ycxz,cxyz->xyz", conj_real, receptor_real, precision=exact_mode
        ) - jnp.einsum("ycxz,cxyz->xyz", conj_imag, receptor_imag, precision=exact_mode)
        product_imag = jnp.einsum(
            "ycxz,cxyz->xyz", conj_imag, receptor_real, precision=exact_mode
        ) + jnp.einsum("ycxz,cxyz->xyz", conj_real, receptor_imag, precision=exact_mode)
        return (product_real, product_imag)

    product_real, product_imag = lax.map(rotation_product, ligand_cells)
    rotations = ligand_cells.shape[0]
    scale = 1.0 / (N * N * N)
    pair_real = product_real.reshape((rotations // 2, 2) + product_real.shape[1:])
    pair_imag = product_imag.reshape((rotations // 2, 2) + product_imag.shape[1:])
    joined_real = pair_real[:, 0] - pair_imag[:, 1]
    joined_imag = pair_imag[:, 0] + pair_real[:, 1]
    even_maps, odd_maps = inverse_transform(joined_real, joined_imag)
    stacked = jnp.stack((even_maps, odd_maps), 1)
    correlation = stacked.reshape((rotations,) + even_maps.shape[1:]) * scale
    local_best = jnp.max(correlation, axis=(1, 2, 3))
    best_score = lax.pmax(local_best, ("py", "pz"))
    return (correlation, best_score)


def solution(mesh):
    placed = (P("rot", None, "py", "pz"), P("rot", None), P(), P())
    return jax.shard_map(
        on_device,
        mesh=mesh,
        in_specs=placed,
        out_specs=(P("rot", "py", "pz", None), P("rot")),
        check_vma=False,
    )
```

profile of v0, /device:TPU:0, one launch (start us, length us, event | category | flops | bytes accessed | tf_op | source)
XLA Modules:
  0.0 1082.8 jit_solution(7503352937062404224)
XLA Ops:
  7.9 25.7 %all-gather.2.cloned.1.call-done = f32[2,128,32,32]{1,3,2,0:T(8,128)} async-done(((f32[1,128,32,32]{1,3,2,0:T(8,128)}), f32[2,128,32,32]{1,3,2,0:T(8,128)}) %all-gather.2.cloned.1.call-update) | async-done | bytes 1048592 | tf_op jit(solution)/shard_map/all_gather | solution.py:67
  60.5 15.0 %all-to-all-done = f32[4,1,65536]{2,1,0:T(1,128)S(1)} async-done(((f32[4,1,65536]{2,1,0:T(1,128)}), f32[4,1,65536]{2,1,0:T(1,128)S(1)}, u32[]{:S(2)}, u32[]{:S(2)}) %all-to-all-start) | async-done | bytes 1048608 | tf_op jit(solution)/shard_map/all_to_all | solution.py:41
  86.8 8.1 copy.110
  111.5 8.1 copy.109
  205.4 643.8 %while.16 = (s32[]{:T(128)}, f32[4,32,128,32]{3,2,1,0:T(8,128)}, f32[4,32,128,32]{3,2,1,0:T(8,128)}, s32[4,2048]{1,0:T(4,128)}, f32[2048,2]{0,1:T(2,128)S(1)}, /...) while((s32[]{:T(128)}, f32[4,32,128,32]{3,2,1,0:T(8,128)}, ...), condition=%wide.region_1.2_spmd.clone, body=%wide.region_0.1_spmd.clone.sunk | while | flops 25824804864 | bytes 229754016 | solution.py:111
  206.6 33.8 %fusion.268 = (f32[2048,32,32]{0,2,1:T(8,128)S(1)}, f32[2048,32,32]{0,2,1:T(8,128)}) fusion(s32[2048,32]{0,1:T(8,128)S(1)} %broadcast_multiply_fusion.7, s32[2048,32]{0,1:T(8,128)S(1)} %broadcast_multiply_fusion.8), kind=kLoop, calls=%fused_computation.17.clone.1 | loop fusion | flops 29360128 | bytes 17301504 | tf_op jit(solution)/shard_map/while/body/eval_jaxpr/sin | solution.py:92
  240.4 11.4 %broadcast_multiply_fusion.9 = (f32[2048,2,32,32]{0,3,2,1:T(8,128)}, f32[2048,2,32,32]{0,3,2,1:T(8,128)S(1)}) fusion(f32[2048,32,32]{0,2,1:T(8,128)S(1)} %get-tuple-element.326, f32[2048,2]{0,1:T(2,128)S(1)} %get-tuple-element.361, f32[2048,32,32]{0,2,1:T(8,128)} %get-tuple-element.327), kind=kLoop, calls=%fused_computation.11.clone.1 | loop fusion | flops 8388608 | bytes 50348032 | tf_op jit(solution)/shard_map/while/body/eval_jaxpr/mul | solution.py:92
  251.8 26.1 %fusion.270 = f32[128,2048]{1,0:T(8,128)S(1)} fusion(f32[2048,2048]{0,1:T(8,128)} %bitcast.214, s32[2048]{0:T(1024)S(1)} %get-tuple-element.329), kind=kOutput, calls=%fused_computation.35.clone.1 | convolution fusion | flops 6446120960 | bytes 17833984 | tf_op jit(solution)/shard_map/while/body/eval_jaxpr/ay,ab->yb/dot_general | solution.py:98
  277.9 23.0 %convolution_add_fusion.7 = f32[128,2048]{1,0:T(8,128)S(1)} fusion(f32[128,2048]{1,0:T(8,128)S(1)} %fusion.270, f32[2048,2048]{0,1:T(8,128)S(1)} %bitcast.212, s32[2048]{0:T(1024)S(1)} %get-tuple-element.329), kind=kOutput, calls=%fused_computation.19.clone.1 | convolution fusion | flops 6446383104 | bytes 18882560 | tf_op jit(solution)/shard_map/while/body/eval_jaxpr/ay,ab->yb/dot_general | solution.py:98
  303.8 24.5 %fusion.269 = f32[128,2048]{1,0:T(8,128)S(1)} fusion(f32[2048,2048]{0,1:T(8,128)} %bitcast.213, s32[2048]{0:T(1024)S(1)} %get-tuple-element.329), kind=kOutput, calls=%fused_computation.36.clone.1 | convolution fusion | flops 6446120960 | bytes 17833984 | tf_op jit(solution)/shard_map/while/body/eval_jaxpr/ay,ab->yb/dot_general | solution.py:95
  328.3 24.5 %convolution_subtract_fusion.7 = f32[128,2048]{1,0:T(8,128)S(1)} fusion(f32[128,2048]{1,0:T(8,128)S(1)} %fusion.269, f32[2048,2048]{0,1:T(8,128)} %bitcast.215, s32[2048]{0:T(1024)S(1)} %get-tuple-element.329), kind=kOutput, calls=%fused_computation.20.clone.1 | convolution fusion | flops 6446383104 | bytes 18882560 | tf_op jit(solution)/shard_map/while/body/eval_jaxpr/ay,ab->yb/dot_general | solution.py:95
  355.7 7.9 multiply_reduce_fusion.5
  367.3 33.8 %fusion.268 = (f32[2048,32,32]{0,2,1:T(8,128)S(1)}, f32[2048,32,32]{0,2,1:T(8,128)}) fusion(s32[2048,32]{0,1:T(8,128)S(1)} %broadcast_multiply_fusion.7, s32[2048,32]{0,1:T(8,128)S(1)} %broadcast_multiply_fusion.8), kind=kLoop, calls=%fused_computation.17.clone.1 | loop fusion | flops 29360128 | bytes 17301504 | tf_op jit(solution)/shard_map/while/body/eval_jaxpr/sin | solution.py:92
  401.2 11.4 %broadcast_multiply_fusion.9 = (f32[2048,2,32,32]{0,3,2,1:T(8,128)}, f32[2048,2,32,32]{0,3,2,1:T(8,128)S(1)}) fusion(f32[2048,32,32]{0,2,1:T(8,128)S(1)} %get-tuple-element.326, f32[2048,2]{0,1:T(2,128)S(1)} %get-tuple-element.361, f32[2048,32,32]{0,2,1:T(8,128)} %get-tuple-element.327), kind=kLoop, calls=%fused_computation.11.clone.1 | loop fusion | flops 8388608 | bytes 50348032 | tf_op jit(solution)/shard_map/while/body/eval_jaxpr/mul | solution.py:92
  412.6 26.1 %fusion.270 = f32[128,2048]{1,0:T(8,128)S(1)} fusion(f32[2048,2048]{0,1:T(8,128)} %bitcast.214, s32[2048]{0:T(1024)S(1)} %get-tuple-element.329), kind=kOutput, calls=%fused_computation.35.clone.1 | convolution fusion | flops 6446120960 | bytes 17833984 | tf_op jit(solution)/shard_map/while/body/eval_jaxpr/ay,ab->yb/dot_general | solution.py:98
  438.7 23.0 %convolution_add_fusion.7 = f32[128,2048]{1,0:T(8,128)S(1)} fusion(f32[128,2048]{1,0:T(8,128)S(1)} %fusion.270, f32[2048,2048]{0,1:T(8,128)S(1)} %bitcast.212, s32[2048]{0:T(1024)S(1)} %get-tuple-element.329), kind=kOutput, calls=%fused_computation.19.clone.1 | convolution fusion | flops 6446383104 | bytes 18882560 | tf_op jit(solution)/shard_map/while/body/eval_jaxpr/ay,ab->yb/dot_general | solution.py:98
  464.6 24.5 %fusion.269 = f32[128,2048]{1,0:T(8,128)S(1)} fusion(f32[2048,2048]{0,1:T(8,128)} %bitcast.213, s32[2048]{0:T(1024)S(1)} %get-tuple-element.329), kind=kOutput, calls=%fused_computation.36.clone.1 | convolution fusion | flops 6446120960 | bytes 17833984 | tf_op jit(solution)/shard_map/while/body/eval_jaxpr/ay,ab->yb/dot_general | solution.py:95
  489.1 24.5 %convolution_subtract_fusion.7 = f32[128,2048]{1,0:T(8,128)S(1)} fusion(f32[128,2048]{1,0:T(8,128)S(1)} %fusion.269, f32[2048,2048]{0,1:T(8,128)} %bitcast.215, s32[2048]{0:T(1024)S(1)} %get-tuple-element.329), kind=kOutput, calls=%fused_computation.20.clone.1 | convolution fusion | flops 6446383104 | bytes 18882560 | tf_op jit(solution)/shard_map/while/body/eval_jaxpr/ay,ab->yb/dot_general | solution.py:95
  528.2 33.8 %fusion.268 = (f32[2048,32,32]{0,2,1:T(8,128)S(1)}, f32[2048,32,32]{0,2,1:T(8,128)}) fusion(s32[2048,32]{0,1:T(8,128)S(1)} %broadcast_multiply_fusion.7, s32[2048,32]{0,1:T(8,128)S(1)} %broadcast_multiply_fusion.8), kind=kLoop, calls=%fused_computation.17.clone.1 | loop fusion | flops 29360128 | bytes 17301504 | tf_op jit(solution)/shard_map/while/body/eval_jaxpr/sin | solution.py:92
  562.0 11.4 %broadcast_multiply_fusion.9 = (f32[2048,2,32,32]{0,3,2,1:T(8,128)}, f32[2048,2,32,32]{0,3,2,1:T(8,128)S(1)}) fusion(f32[2048,32,32]{0,2,1:T(8,128)S(1)} %get-tuple-element.326, f32[2048,2]{0,1:T(2,128)S(1)} %get-tuple-element.361, f32[2048,32,32]{0,2,1:T(8,128)} %get-tuple-element.327), kind=kLoop, calls=%fused_computation.11.clone.1 | loop fusion | flops 8388608 | bytes 50348032 | tf_op jit(solution)/shard_map/while/body/eval_jaxpr/mul | solution.py:92
  573.4 26.1 %fusion.270 = f32[128,2048]{1,0:T(8,128)S(1)} fusion(f32[2048,2048]{0,1:T(8,128)} %bitcast.214, s32[2048]{0:T(1024)S(1)} %get-tuple-element.329), kind=kOutput, calls=%fused_computation.35.clone.1 | convolution fusion | flops 6446120960 | bytes 17833984 | tf_op jit(solution)/shard_map/while/body/eval_jaxpr/ay,ab->yb/dot_general | solution.py:98
  599.5 23.0 %convolution_add_fusion.7 = f32[128,2048]{1,0:T(8,128)S(1)} fusion(f32[128,2048]{1,0:T(8,128)S(1)} %fusion.270, f32[2048,2048]{0,1:T(8,128)S(1)} %bitcast.212, s32[2048]{0:T(1024)S(1)} %get-tuple-element.329), kind=kOutput, calls=%fused_computation.19.clone.1 | convolution fusion | flops 6446383104 | bytes 18882560 | tf_op jit(solution)/shard_map/while/body/eval_jaxpr/ay,ab->yb/dot_general | solution.py:98
  625.4 24.5 %fusion.269 = f32[128,2048]{1,0:T(8,128)S(1)} fusion(f32[2048,2048]{0,1:T(8,128)} %bitcast.213, s32[2048]{0:T(1024)S(1)} %get-tuple-element.329), kind=kOutput, calls=%fused_computation.36.clone.1 | convolution fusion | flops 6446120960 | bytes 17833984 | tf_op jit(solution)/shard_map/while/body/eval_jaxpr/ay,ab->yb/dot_general | solution.py:95
  649.9 24.5 %convolution_subtract_fusion.7 = f32[128,2048]{1,0:T(8,128)S(1)} fusion(f32[128,2048]{1,0:T(8,128)S(1)} %fusion.269, f32[2048,2048]{0,1:T(8,128)} %bitcast.215, s32[2048]{0:T(1024)S(1)} %get-tuple-element.329), kind=kOutput, calls=%fused_computation.20.clone.1 | convolution fusion | flops 6446383104 | bytes 18882560 | tf_op jit(solution)/shard_map/while/body/eval_jaxpr/ay,ab->yb/dot_general | solution.py:95
  689.0 33.8 %fusion.268 = (f32[2048,32,32]{0,2,1:T(8,128)S(1)}, f32[2048,32,32]{0,2,1:T(8,128)}) fusion(s32[2048,32]{0,1:T(8,128)S(1)} %broadcast_multiply_fusion.7, s32[2048,32]{0,1:T(8,128)S(1)} %broadcast_multiply_fusion.8), kind=kLoop, calls=%fused_computation.17.clone.1 | loop fusion | flops 29360128 | bytes 17301504 | tf_op jit(solution)/shard_map/while/body/eval_jaxpr/sin | solution.py:92
  722.8 11.4 %broadcast_multiply_fusion.9 = (f32[2048,2,32,32]{0,3,2,1:T(8,128)}, f32[2048,2,32,32]{0,3,2,1:T(8,128)S(1)}) fusion(f32[2048,32,32]{0,2,1:T(8,128)S(1)} %get-tuple-element.326, f32[2048,2]{0,1:T(2,128)S(1)} %get-tuple-element.361, f32[2048,32,32]{0,2,1:T(8,128)} %get-tuple-element.327), kind=kLoop, calls=%fused_computation.11.clone.1 | loop fusion | flops 8388608 | bytes 50348032 | tf_op jit(solution)/shard_map/while/body/eval_jaxpr/mul | solution.py:92
  734.2 26.1 %fusion.270 = f32[128,2048]{1,0:T(8,128)S(1)} fusion(f32[2048,2048]{0,1:T(8,128)} %bitcast.214, s32[2048]{0:T(1024)S(1)} %get-tuple-element.329), kind=kOutput, calls=%fused_computation.35.clone.1 | convolution fusion | flops 6446120960 | bytes 17833984 | tf_op jit(solution)/shard_map/while/body/eval_jaxpr/ay,ab->yb/dot_general | solution.py:98
  760.3 23.0 %convolution_add_fusion.7 = f32[128,2048]{1,0:T(8,128)S(1)} fusion(f32[128,2048]{1,0:T(8,128)S(1)} %fusion.270, f32[2048,2048]{0,1:T(8,128)S(1)} %bitcast.212, s32[2048]{0:T(1024)S(1)} %get-tuple-element.329), kind=kOutput, calls=%fused_computation.19.clone.1 | convolution fusion | flops 6446383104 | bytes 18882560 | tf_op jit(solution)/shard_map/while/body/eval_jaxpr/ay,ab->yb/dot_general | solution.py:98
  786.2 24.5 %fusion.269 = f32[128,2048]{1,0:T(8,128)S(1)} fusion(f32[2048,2048]{0,1:T(8,128)} %bitcast.213, s32[2048]{0:T(1024)S(1)} %get-tuple-element.329), kind=kOutput, calls=%fused_computation.36.clone.1 | convolution fusion | flops 6446120960 | bytes 17833984 | tf_op jit(solution)/shard_map/while/body/eval_jaxpr/ay,ab->yb/dot_general | solution.py:95
  810.7 24.5 %convolution_subtract_fusion.7 = f32[128,2048]{1,0:T(8,128)S(1)} fusion(f32[128,2048]{1,0:T(8,128)S(1)} %fusion.269, f32[2048,2048]{0,1:T(8,128)} %bitcast.215, s32[2048]{0:T(1024)S(1)} %get-tuple-element.329), kind=kOutput, calls=%fused_computation.20.clone.1 | convolution fusion | flops 6446383104 | bytes 18882560 | tf_op jit(solution)/shard_map/while/body/eval_jaxpr/ay,ab->yb/dot_general | solution.py:95
  978.0 14.9 %all-to-all-done.6 = f32[4,1,65536]{2,1,0:T(1,128)S(1)} async-done(((f32[4,1,65536]{2,1,0:T(1,128)}), f32[4,1,65536]{2,1,0:T(1,128)S(1)}, u32[]{:S(2)}, u32[]{:S(2)}) %all-to-all-start.6) | async-done | bytes 1048608 | tf_op jit(solution)/shard_map/all_to_all | solution.py:60
  1045.4 30.3 %pmax.7 = f32[4]{0:T(128)} all-reduce(f32[4]{0:T(128)S(1)} %reduce_max.12), channel_id=1, replica_groups=mesh['rot'=2,'py'=4,'pz'=4] {'py','pz'}, use_global_device_ids=true, to_apply=%region_3.4 | all-reduce | flops 4 | bytes 32 | tf_op jit(solution)/shard_map/pmax | solution.py:122
  (161 shorter events, 384.4 us)
Async XLA Ops:
  7.2 26.4 %all-gather.2.cloned.1.call-start = ((), (), s32[]{:S(2)}) async-start(), calls=%async_computation.8 | async-start | bytes 1572864 | tf_op jit(solution)/shard_map/all_gather | solution.py:67
  40.4 9.5 copy-start.1
  45.4 30.2 %all-to-all-start = ((f32[4,1,65536]{2,1,0:T(1,128)}), f32[4,1,65536]{2,1,0:T(1,128)S(1)}, u32[]{:S(2)}, u32[]{:S(2)}) async-start(f32[4,1,65536]{2,1,0:T(1,128)} %reshape.243), calls=%async_computation | async-start | bytes 2097152 | tf_op jit(solution)/shard_map/all_to_all | solution.py:41
  75.5 28.9 %all-to-all-start.1 = ((f32[4,1,65536]{2,1,0:T(1,128)}), f32[4,1,65536]{2,1,0:T(1,128)S(1)}, u32[]{:S(2)}, u32[]{:S(2)}) async-start(f32[4,1,65536]{2,1,0:T(1,128)} %reshape.245), calls=%async_computation.1 | async-start | bytes 2097152 | tf_op jit(solution)/shard_map/all_to_all | solution.py:42
  135.5 17.9 %all-to-all-start.2 = ((f32[4,1,65536]{2,1,0:T(1,128)}), f32[4,1,65536]{2,1,0:T(1,128)S(1)}, u32[]{:S(2)}, u32[]{:S(2)}) async-start(f32[4,1,65536]{2,1,0:T(1,128)} %reshape.247), calls=%async_computation.2 | async-start | bytes 2097152 | tf_op jit(solution)/shard_map/all_to_all | solution.py:46
  145.9 11.2 %copy-start.2 = (f32[2048]{0:T(1024)S(1)}, f32[2048]{0:T(1024)}, u32[]{:S(2)}) copy-start(f32[2048]{0:T(1024)} %param.9) | copy-start | bytes 24580
  145.9 11.3 %copy-start.3 = (f32[2048]{0:T(1024)S(1)}, f32[2048]{0:T(1024)}, u32[]{:S(2)}) copy-start(f32[2048]{0:T(1024)} %param.8) | copy-start | bytes 24580
  153.4 25.3 %all-to-all-start.3 = ((f32[4,1,65536]{2,1,0:T(1,128)}), f32[4,1,65536]{2,1,0:T(1,128)S(1)}, u32[]{:S(2)}, u32[]{:S(2)}) async-start(f32[4,1,65536]{2,1,0:T(1,128)} %reshape.249), calls=%async_computation.3 | async-start | bytes 2097152 | tf_op jit(solution)/shard_map/all_to_all | solution.py:47
  251.8 26.1 %copy-start = (f32[2048,2,32,32]{0,3,2,1:T(8,128)}, f32[2048,2,32,32]{0,3,2,1:T(8,128)S(1)}, u32[]{:S(2)}) copy-start(f32[2048,2,32,32]{0,3,2,1:T(8,128)S(1)} %get-tuple-element.328) | copy-start | bytes 50331652 | tf_op jit(solution)/shard_map/while
  412.6 26.1 %copy-start = (f32[2048,2,32,32]{0,3,2,1:T(8,128)}, f32[2048,2,32,32]{0,3,2,1:T(8,128)S(1)}, u32[]{:S(2)}) copy-start(f32[2048,2,32,32]{0,3,2,1:T(8,128)S(1)} %get-tuple-element.328) | copy-start | bytes 50331652 | tf_op jit(solution)/shard_map/while
  573.4 26.1 %copy-start = (f32[2048,2,32,32]{0,3,2,1:T(8,128)}, f32[2048,2,32,32]{0,3,2,1:T(8,128)S(1)}, u32[]{:S(2)}) copy-start(f32[2048,2,32,32]{0,3,2,1:T(8,128)S(1)} %get-tuple-element.328) | copy-start | bytes 50331652 | tf_op jit(solution)/shard_map/while
  734.2 26.1 %copy-start = (f32[2048,2,32,32]{0,3,2,1:T(8,128)}, f32[2048,2,32,32]{0,3,2,1:T(8,128)S(1)}, u32[]{:S(2)}) copy-start(f32[2048,2,32,32]{0,3,2,1:T(8,128)S(1)} %get-tuple-element.328) | copy-start | bytes 50331652 | tf_op jit(solution)/shard_map/while
  891.7 18.8 %all-to-all-start.5 = ((f32[4,1,65536]{2,1,0:T(1,128)}), f32[4,1,65536]{2,1,0:T(1,128)}, u32[]{:S(2)}, u32[]{:S(2)}) async-start(f32[4,1,65536]{2,1,0:T(1,128)} %reshape.253), calls=%async_computation.5 | async-start | bytes 2097152 | tf_op jit(solution)/shard_map/all_to_all | solution.py:56
  910.5 22.5 %all-to-all-start.4 = ((f32[4,1,65536]{2,1,0:T(1,128)}), f32[4,1,65536]{2,1,0:T(1,128)S(1)}, u32[]{:S(2)}, u32[]{:S(2)}) async-start(f32[4,1,65536]{2,1,0:T(1,128)} %reshape.251), calls=%async_computation.4 | async-start | bytes 2097152 | tf_op jit(solution)/shard_map/all_to_all | solution.py:55
  962.7 30.1 %all-to-all-start.6 = ((f32[4,1,65536]{2,1,0:T(1,128)}), f32[4,1,65536]{2,1,0:T(1,128)S(1)}, u32[]{:S(2)}, u32[]{:S(2)}) async-start(f32[4,1,65536]{2,1,0:T(1,128)} %reshape.255), calls=%async_computation.6 | async-start | bytes 2097152 | tf_op jit(solution)/shard_map/all_to_all | solution.py:60
  992.9 30.1 %all-to-all-start.7 = ((f32[4,1,65536]{2,1,0:T(1,128)}), f32[4,1,65536]{2,1,0:T(1,128)}, u32[]{:S(2)}, u32[]{:S(2)}) async-start(f32[4,1,65536]{2,1,0:T(1,128)} %reshape.257), calls=%async_computation.7 | async-start | bytes 2097152 | tf_op jit(solution)/shard_map/all_to_all | solution.py:61
Sparse Core Ops, SparseCore 0:
  9.5 23.9 all-gather.1
where the time goes:
time: 1090 us; the launch traced here: 1080 us
  matrix products  428 us (39%)
  other arithmetic  256 us (23%)
  local copies, waits for them, and re-layouts  252 us (23%)
  waiting for transfers between devices  70.1 us (6%)
  starting transfers between devices  31.2 us (3%)
  blocking collectives  30.3 us (3%)
  between operations  14.7 us (1%)
    sin x4, other arithmetic, rotation_product(): jnp.sin(angle_xz)[:, None]  135 us
    dot_general x4, matrix products, rotation_product(): jnp.einsum('ay,ab->yb', cos_y, sin_xz, precision=exact_mode)  104 us
    dot_general x4, matrix products, rotation_product(): jnp.einsum('ay,ab->yb', cos_y, cos_xz, precision=exact_mode)  98 us
    dot_general x4, matrix products, rotation_product(): jnp.einsum('ay,ab->yb', sin_y, sin_xz, precision=exact_mode)  97.8 us
    dot_general x4, matrix products, rotation_product(): jnp.einsum('ay,ab->yb', sin_y, cos_xz, precision=exact_mode)  91.8 us
    unnamed x28, local copies, waits for them, and re-layouts  83.3 us
    mul x4, other arithmetic, rotation_product(): weights[:, :, None, None] * jnp.sin(angle_xz)[:, None]  45.7 us
    dot_general x4, other arithmetic, rotation_product(): jnp.einsum('ycxz,cxyz->xyz', conj_real, receptor_imag, precision=exact_mode)  31.6 us
  transfers between devices with their start and end apart: 9, of which 7 were waited for; matrix products, arithmetic and copies ran while one was open for 10% of the time, Pallas kernels for 0%

commit v1 on v0

v1 whole, which is shorter than its diff:
```python
import functools
import math

import jax
import jax.numpy as jnp
import numpy as np
from jax import lax
from jax.experimental import pallas as pl
from jax.experimental.pallas import tpu as pltpu
from jax.sharding import PartitionSpec as P

exact_mode = lax.Precision.HIGHEST
AXES = ("rot", "py", "pz")
LANES = 128
SUBLANES = 8


def split_constant(matrix):
    head = np.asarray(matrix, np.float64).astype(jnp.bfloat16)
    rest = (np.asarray(matrix, np.float64) - head.astype(np.float64)).astype(jnp.bfloat16)
    return head, rest


def plus_matrix(n):
    turns = np.outer(np.arange(n), np.arange(n)) % n
    cosine, sine = np.cos(turns * (2 * np.pi / n)), np.sin(turns * (2 * np.pi / n))
    return np.block([[cosine, sine], [-sine, cosine]])


def component_phases(n):
    places = np.arange(n)
    phases = np.zeros((n, n), np.int64)
    for slot in range(n // 2):
        phases[2 * slot] = slot * places % n
        phases[2 * slot + 1] = (n // 2) * places % n if slot == 0 else (slot * places - n // 4) % n
    return phases


def forward_x_matrix(n):
    return np.cos(component_phases(n) * (2 * np.pi / n))


def inverse_x_matrix(n):
    matrix = np.cos(component_phases(n) * (2 * np.pi / n))
    scale = np.full((n, 1), 2.0)
    scale[3::2] = -2.0
    scale[:2] = 1.0
    return matrix * scale / float(n) ** 3


def split(value):
    head = value.astype(jnp.bfloat16)
    rest = (value - head.astype(jnp.float32)).astype(jnp.bfloat16)
    return head, rest


def dot(a, b):
    return jnp.dot(a, b, preferred_element_type=jnp.float32)


def times_constant(value, head_ref, rest_ref):
    head, rest = split(value)
    return dot(head, head_ref[...]) + (dot(head, rest_ref[...]) + dot(rest, head_ref[...]))


def constant_times(head_ref, rest_ref, value):
    head, rest = split(value)
    return dot(head_ref[...], head) + (dot(rest_ref[...], head) + dot(head_ref[...], rest))


def swap_groups(pieces, width):
    return [
        jnp.concatenate([piece[..., q * width : (q + 1) * width] for piece in pieces], axis=-1)
        for q in range(len(pieces))
    ]


def forward_x_kernel(grid_ref, head_ref, rest_ref, out_ref, rows_ref):
    n, y_block, z_block = grid_ref.shape[1:]
    groups = LANES // z_block
    high = y_block // groups
    rows_ref[...] = jnp.concatenate(
        [grid_ref[0, :, g * high : (g + 1) * high, :] for g in range(groups)], axis=-1
    ).reshape(n * high, LANES)
    for row in range(high):
        values = rows_ref[pl.ds(row, n, stride=high), :]
        out_ref[pl.ds(row, n, stride=high), :] = constant_times(head_ref, rest_ref, values)


def spectrum(planes, n, zh, zr, yh, yr):
    count = len(planes)
    rows = jnp.concatenate([jnp.concatenate(pair, axis=1) for pair in planes], axis=0)
    rows = times_constant(rows, zh, zr)
    columns = jnp.concatenate(
        [
            jnp.concatenate([rows[i * n : (i + 1) * n, :n], rows[i * n : (i + 1) * n, n:]], axis=0)
            for i in range(count)
        ],
        axis=1,
    )
    return constant_times(yh, yr, columns)


def ligand_kernel(special_ref, values_ref, cell_ref, zh, zr, yh, yr, out_ref):
    n = zh.shape[0] // 2
    comps, atoms = values_ref.shape[-2:]
    half = n // 2
    special = special_ref[0, 0] > 0
    grids = []
    for rotation in range(2):
        cell = cell_ref[0, rotation : rotation + 1, :]
        y_low = (cell // n) % half
        place = cell % n + n * ((cell // (n * half)) % 2)
        head = values_ref[0, rotation].astype(jnp.bfloat16).astype(jnp.float32)
        rest = (values_ref[0, rotation] - head).astype(jnp.bfloat16).astype(jnp.float32)
        hit = lax.broadcasted_iota(jnp.int32, (half, atoms), 0) == y_low
        stacked = jnp.concatenate(
            [
                jnp.where(hit, part[c : c + 1, :], 0.0).astype(jnp.bfloat16)
                for part in (head, rest)
                for c in range(comps)
            ],
            axis=0,
        )
        one_hot = (
            lax.broadcasted_iota(jnp.int32, (2 * n, atoms), 0) == place
        ).astype(jnp.float32).astype(jnp.bfloat16)
        total = lax.dot_general(
            stacked, one_hot, (((1,), (1,)), ((), ())), preferred_element_type=jnp.float32
        )
        total = total[: comps * half] + total[comps * half :]
        grids.append(
            [
                jnp.concatenate(
                    [total[c * half : (c + 1) * half, :n], total[c * half : (c + 1) * half, n:]], axis=0
                )
                for c in range(comps)
            ]
        )
    planes = [[], []]
    for c in range(0, comps, 2):
        first, second = (grids[0][c], grids[0][c + 1]), (grids[1][c], grids[1][c + 1])
        if c < 4:
            first, second = (
                (first[0], jnp.where(special, second[0], first[1])),
                (jnp.where(special, first[1], second[0]), second[1]),
            )
        planes[0].append(first)
        planes[1].append(second)
    out_ref[0] = spectrum(planes[0] + planes[1], n, zh, zr, yh, yr)


def receptor_kernel(special_ref, blocks_ref, zh, zr, yh, yr, out_ref, *, channels, y_parts, z_parts):
    n = zh.shape[0] // 2
    width = n // z_parts
    comps = blocks_ref.shape[1] // SUBLANES
    special = special_ref[0, 0] > 0
    planes = []
    for channel in range(channels):
        parts = []
        for c in range(comps):
            rows = []
            for y_part in range(y_parts):
                first = (channel * y_parts + y_part) * z_parts
                pieces = [blocks_ref[first + i, c * SUBLANES : (c + 1) * SUBLANES, :] for i in range(z_parts)]
                rows += swap_groups(pieces, width)
            parts.append(jnp.concatenate(rows, axis=0))
        zero = jnp.zeros_like(parts[0])
        lone = jnp.where(special, zero, parts[1])
        planes.append((parts[0], lone))
        planes.append((jnp.where(special, parts[1], parts[0]), lone))
        for c in range(2, comps, 2):
            planes.append((parts[c], parts[c + 1]))
    out_ref[...] = spectrum(planes, n, zh, zr, yh, yr)


def product_kernel(special_ref, receptor_ref, ligand_ref, zh, zr, yh, yr, out_ref, *, channels, y_parts, z_parts):
    n = zh.shape[0] // 2
    width = n // z_parts
    groups = LANES // width
    slots = ligand_ref.shape[2] // (2 * channels * n)
    special = special_ref[0, 0] > 0

    def receptor(channel, slot, rotation):
        at = channel * (slots + 1) + (rotation if slot == 0 else slot + 1)
        return receptor_ref[:n, at * n : (at + 1) * n], receptor_ref[n:, at * n : (at + 1) * n]

    def ligand(channel, slot, rotation):
        at = (rotation * slots + slot) * channels + channel
        return ligand_ref[0, :n, at * n : (at + 1) * n], ligand_ref[0, n:, at * n : (at + 1) * n]

    columns = []
    for rotation in range(2):
        for slot in range(slots):
            real, imag = 0.0, 0.0
            for channel in range(channels):
                fr, fi = receptor(channel, slot, rotation)
                hr, hi = ligand(channel, slot, rotation)
                real = real + (fr * hr + fi * hi)
                imag = imag + (fr * hi - fi * hr)
            columns.append(jnp.concatenate([real, imag], axis=0))
    columns = constant_times(yh, yr, jnp.concatenate(columns, axis=1))
    rows = jnp.concatenate(
        [
            jnp.concatenate([columns[:n, i * n : (i + 1) * n], columns[n:, i * n : (i + 1) * n]], axis=1)
            for i in range(2 * slots)
        ],
        axis=0,
    )
    rows = times_constant(rows, zh, zr)
    maps = [
        [
            [rows[(rotation * slots + slot) * n : (rotation * slots + slot + 1) * n, p * n : (p + 1) * n] for p in range(2)]
            for slot in range(slots)
        ]
        for rotation in range(2)
    ]
    lone, other = maps[0][0][1], maps[1][0][0]
    maps[0][0][1] = jnp.where(special, other, lone)
    maps[1][0][0] = jnp.where(special, lone, other)
    for rotation in range(2):
        for slot in range(slots):
            for p in range(2):
                plane = maps[rotation][slot][p]
                row = (slot * 2 + p) * SUBLANES
                for y_part in range(y_parts):
                    pieces = [
                        plane[(y_part * groups + g) * SUBLANES : (y_part * groups + g + 1) * SUBLANES, :]
                        for g in range(groups)
                    ]
                    for z_part, block in enumerate(swap_groups(pieces, width)):
                        out_ref[(rotation * y_parts + y_part) * z_parts + z_part, row : row + SUBLANES, :] = block


def inverse_x_kernel(blocks_ref, head_ref, rest_ref, out_ref, best_ref):
    n = head_ref.shape[0]
    y_block, z_block = out_ref.shape[1:3]
    groups = LANES // z_block
    best = None
    for row in range(SUBLANES):
        values = blocks_ref[0, pl.ds(row, n, stride=SUBLANES), :]
        result = times_constant(values.T, head_ref, rest_ref)
        for g in range(groups):
            out_ref[0, g * SUBLANES + row] = result[g * z_block : (g + 1) * z_block, :]
        best = result if best is None else jnp.maximum(best, result)
    best_ref[0] = jnp.broadcast_to(jnp.max(best, axis=(0, 1), keepdims=True), (SUBLANES, LANES))


def whole():
    return pl.BlockSpec(memory_space=pltpu.VMEM)


def scalar():
    return pl.BlockSpec(memory_space=pltpu.SMEM)


def on_device(receptor_grids, ligand_cells, atom_shape, atom_charges, *, sizes):
    n = receptor_grids.shape[1]
    rots, y_parts, z_parts = (sizes[a] for a in AXES)
    devices = rots * y_parts * z_parts
    slots = n // 2 // devices
    comps = 2 * slots
    y_block, z_block = receptor_grids.shape[2:]
    rotations, atoms = ligand_cells.shape
    channels = 2
    planes = [jnp.asarray(m) for m in split_constant(plus_matrix(n))]
    planes += [m.T for m in (np.asarray(p) for p in split_constant(plus_matrix(n)))]
    planes = [jnp.asarray(m) for m in planes]
    f32 = jnp.float32

    other = lax.ppermute(ligand_cells, "rot", [(i, i ^ 1) for i in range(rots)])

    components = pl.pallas_call(
        forward_x_kernel,
        out_shape=jax.ShapeDtypeStruct((n * SUBLANES, LANES), f32),
        in_specs=[whole()] * 3,
        out_specs=whole(),
        scratch_shapes=[pltpu.VMEM((n * SUBLANES, LANES), f32)],
        name="forward_x",
    )(receptor_grids, *(jnp.asarray(m) for m in split_constant(forward_x_matrix(n))))
    blocks = lax.all_to_all(components.reshape(devices, comps * SUBLANES, LANES), AXES, 0, 0, tiled=True)

    mine = lax.axis_index("rot") == 0
    cells = jnp.stack(
        [jnp.where(mine, ligand_cells, other), jnp.where(mine, other, ligand_cells)], axis=1
    )
    device = lax.axis_index(AXES)
    coord_x = cells // (n * n)
    slot = device * slots + jnp.arange(slots, dtype=jnp.int32)
    turns = slot[:, None] * coord_x[:, :, None, None, :]
    quarter = jnp.where(
        slot[:, None] == 0, (n // 2) * coord_x[:, :, None, None, :], turns - n // 4
    )
    phase = jnp.concatenate([turns[..., None, :], quarter[..., None, :]], axis=-2) % n
    wave = jnp.cos(phase.astype(f32) * (2.0 * math.pi / n))
    weights = jnp.stack([atom_shape, atom_charges], 0)[:, None, :]
    wave = jnp.swapaxes(wave, 2, 3) if wave.shape[2] == 1 else wave
    wave = wave.reshape(rotations, rots, slots, 1, 2, atoms)
    values = (wave * weights).reshape(rotations, rots, slots * channels * 2, atoms)
    special = (device == 0).astype(jnp.int32).reshape(1, 1)

    width = 2 * slots * channels * n
    ligand = pl.pallas_call(
        ligand_kernel,
        grid=(rotations,),
        out_shape=jax.ShapeDtypeStruct((rotations, 2 * n, width), f32),
        in_specs=[
            scalar(),
            pl.BlockSpec((1, rots, slots * channels * 2, atoms), lambda i: (i, 0, 0, 0)),
            pl.BlockSpec((1, rots, atoms), lambda i: (i, 0, 0)),
        ]
        + [whole()] * 4,
        out_specs=pl.BlockSpec((1, 2 * n, width), lambda i: (i, 0, 0)),
        name="ligand",
    )(special, values, cells, *planes)

    receptor = pl.pallas_call(
        functools.partial(receptor_kernel, channels=channels, y_parts=y_parts, z_parts=z_parts),
        out_shape=jax.ShapeDtypeStruct((2 * n, channels * (slots + 1) * n), f32),
        in_specs=[scalar()] + [whole()] * 5,
        out_specs=whole(),
        name="receptor",
    )(special, blocks, *planes)

    rows = comps * SUBLANES
    sent = pl.pallas_call(
        functools.partial(product_kernel, channels=channels, y_parts=y_parts, z_parts=z_parts),
        grid=(rotations,),
        out_shape=jax.ShapeDtypeStruct((devices, rotations * rows, LANES), f32),
        in_specs=[scalar(), whole(), pl.BlockSpec((1, 2 * n, width), lambda i: (i, 0, 0))] + [whole()] * 4,
        out_specs=pl.BlockSpec((devices, rows, LANES), lambda i: (0, i, 0)),
        name="product",
    )(special, receptor, ligand, *planes)
    got = lax.all_to_all(sent, AXES, 0, 0, tiled=True)
    got = jnp.swapaxes(got.reshape(devices, rotations, rows, LANES), 0, 1).reshape(rotations, devices * rows, LANES)

    correlation, best = pl.pallas_call(
        inverse_x_kernel,
        grid=(rotations,),
        out_shape=[
            jax.ShapeDtypeStruct((rotations, y_block, z_block, n), f32),
            jax.ShapeDtypeStruct((rotations, SUBLANES, LANES), f32),
        ],
        in_specs=[pl.BlockSpec((1, devices * rows, LANES), lambda i: (i, 0, 0))] + [whole()] * 2,
        out_specs=[
            pl.BlockSpec((1, y_block, z_block, n), lambda i: (i, 0, 0, 0)),
            pl.BlockSpec((1, SUBLANES, LANES), lambda i: (i, 0, 0)),
        ],
        name="inverse_x",
    )(got, *(jnp.asarray(m) for m in split_constant(inverse_x_matrix(n))))
    best = best[:, 0, :]
    for axis in ("py", "pz"):
        step = 1
        while step < sizes[axis]:
            best = jnp.maximum(best, lax.ppermute(best, axis, [(i, i ^ step) for i in range(sizes[axis])]))
            step *= 2
    return correlation, best[:, 0]


def twiddle(length, inverse):
    counter = jnp.arange(length, dtype=jnp.int32)
    phases = counter[:, None] * counter[None, :] % length
    angles = phases.astype(jnp.float32) * (2.0 * math.pi / length)
    factor = 1.0 if inverse else -1.0
    return (jnp.cos(angles), factor * jnp.sin(angles))


def transform(real_part, imag_part, pattern, inverse, n):
    cosine, sine_table = twiddle(n, inverse)
    if imag_part is None:
        return (
            jnp.einsum(pattern, real_part, cosine, precision=exact_mode),
            jnp.einsum(pattern, real_part, sine_table, precision=exact_mode),
        )
    new_real = jnp.einsum(pattern, real_part, cosine, precision=exact_mode) - jnp.einsum(
        pattern, imag_part, sine_table, precision=exact_mode
    )
    new_imag = jnp.einsum(pattern, real_part, sine_table, precision=exact_mode) + jnp.einsum(
        pattern, imag_part, cosine, precision=exact_mode
    )
    return (new_real, new_imag)


def exchange(pair, axis, split_axis, concat_axis):
    return tuple(lax.all_to_all(p, axis, split_axis=split_axis, concat_axis=concat_axis, tiled=True) for p in pair)


def on_any_device(receptor_grids, ligand_cells, atom_shape, atom_charges, *, sizes):
    n = receptor_grids.shape[1]
    planes = lax.all_gather(receptor_grids, "rot", axis=0, tiled=True)
    pair = transform(planes, None, "cxyz,xk->ckyz", False, n)
    pair = transform(*exchange(pair, "pz", 1, 3), "cxyz,zk->cxyk", False, n)
    receptor_real, receptor_imag = transform(*exchange(pair, "py", 3, 2), "cxyz,yk->cxkz", False, n)
    x_block = n // sizes["pz"]
    z_block = n // sizes["py"]
    kx_values = lax.axis_index("pz") * x_block + jnp.arange(x_block, dtype=jnp.int32)
    kz_values = lax.axis_index("py") * z_block + jnp.arange(z_block, dtype=jnp.int32)
    ky_values = jnp.arange(n, dtype=jnp.int32)
    weights = jnp.stack((atom_shape, atom_charges), 1)
    step_angle = 2.0 * math.pi / n

    def rotation_product(atom_cells):
        coord_x = atom_cells // (n * n)
        coord_y = atom_cells // n % n
        coord_z = atom_cells % n
        angle_y = (coord_y[:, None] * ky_values[None, :] % n).astype(jnp.float32) * step_angle
        cos_y = jnp.cos(angle_y)
        sin_y = jnp.sin(angle_y)
        phase_xz = (
            coord_x[:, None, None] * kx_values[None, :, None]
            + coord_z[:, None, None] * kz_values[None, None, :]
        ) % n
        angle_xz = phase_xz.astype(jnp.float32) * step_angle
        cos_xz = (weights[:, :, None, None] * jnp.cos(angle_xz)[:, None]).reshape(atom_cells.shape[0], -1)
        sin_xz = (weights[:, :, None, None] * jnp.sin(angle_xz)[:, None]).reshape(atom_cells.shape[0], -1)
        meet = functools.partial(jnp.einsum, "ay,ab->yb", precision=exact_mode)
        conj_real = (meet(cos_y, cos_xz) - meet(sin_y, sin_xz)).reshape(n, 2, x_block, z_block)
        conj_imag = (meet(cos_y, sin_xz) + meet(sin_y, cos_xz)).reshape(n, 2, x_block, z_block)
        join = functools.partial(jnp.einsum, "ycxz,cxyz->xyz", precision=exact_mode)
        product_real = join(conj_real, receptor_real) - join(conj_imag, receptor_imag)
        product_imag = join(conj_imag, receptor_real) + join(conj_real, receptor_imag)
        return (product_real, product_imag)

    product_real, product_imag = lax.map(rotation_product, ligand_cells)
    rotations = ligand_cells.shape[0]
    pair_real = product_real.reshape((rotations // 2, 2) + product_real.shape[1:])
    pair_imag = product_imag.reshape((rotations // 2, 2) + product_imag.shape[1:])
    pair = (pair_real[:, 0] - pair_imag[:, 1], pair_imag[:, 0] + pair_real[:, 1])
    pair = transform(*pair, "bxyz,yk->bxkz", True, n)
    pair = transform(*exchange(pair, "py", 2, 3), "bxyz,zk->bxyk", True, n)
    even_maps, odd_maps = transform(*exchange(pair, "pz", 3, 1), "bxyz,xk->byzk", True, n)
    stacked = jnp.stack((even_maps, odd_maps), 1)
    correlation = stacked.reshape((rotations,) + even_maps.shape[1:]) * (1.0 / (n * n * n))
    best_score = lax.pmax(jnp.max(correlation, axis=(1, 2, 3)), ("py", "pz"))
    return (correlation, best_score)


def solution(mesh):
    sizes = dict(mesh.shape)

    def run(receptor_grids, ligand_cells, atom_shape, atom_charges):
        n = receptor_grids.shape[1]
        devices = math.prod(sizes[a] for a in AXES)
        fits = (
            sizes["rot"] == 2
            and n == LANES
            and (n // 2) % devices == 0
            and (n // sizes["py"]) * (n // sizes["pz"]) == SUBLANES * LANES
            and all(sizes[a] & (sizes[a] - 1) == 0 for a in AXES)
        )
        body = functools.partial(on_device if fits else on_any_device, sizes=sizes)
        placed = (P("rot", None, "py", "pz"), P("rot", None), P(), P())
        return jax.shard_map(
            body,
            mesh=mesh,
            in_specs=placed,
            out_specs=(P("rot", "py", "pz", None), P("rot")),
            check_vma=False,
        )(receptor_grids, ligand_cells, atom_shape, atom_charges)

    return run
```

time: 1090 us -> 128 us (0.12)
  matrix products: 428 us -> 0 us
  other arithmetic: 256 us -> 6 us
  local copies, waits for them, and re-layouts: 252 us -> 8.26 us
  waiting for transfers between devices: 70.1 us -> 8.15 us
  Pallas kernels: 0 us -> 37.1 us
  blocking collectives: 30.3 us -> 53.2 us
  starting transfers between devices: 31.2 us -> 13.9 us
  between operations: 14.7 us -> 0.8 us
    dot_general x36 -> x0, matrix products: 424 us -> none  [the longest x4 104 us: rotation_product(): jnp.einsum('ay,ab->yb', cos_y, sin_xz, precision=exact_mode)]
    sin x4 -> x0, other arithmetic: 135 us -> none  [rotation_product(): jnp.sin(angle_xz)[:, None]]
    all_to_all x17 -> x0, local copies, waits for them, and re-layouts: 87.6 us -> none  [the longest x3 12.6 us: receptor_forward(): lax.all_to_all(real_part, 'pz', split_axis=1, concat_axis=3, tiled=True)]
    unnamed x28 -> x9, local copies, waits for them, and re-layouts: 83.3 us -> 4.65 us
    all_to_all x0 -> x1, blocking collectives: none -> 53.2 us  [on_device(): got = lax.all_to_all(sent, AXES, 0, 0, tiled=True)]
    mul x12 -> x3, other arithmetic: 46.4 us -> 1.94 us  [the longest x1 0.84 us: on_device(): wave * weights]
    all_to_all x8 -> x1, waiting for transfers between devices: 43.7 us -> 0.01 us  [on_device(): lax.all_to_all(components.reshape(devices, comps * SUBLANES, LANES), AXES...]
    pallas_call x0 -> x5, Pallas kernels: none -> 37.1 us  [the longest x1 18 us: on_device(): pl.pallas_call(ligand_kernel, grid=(rotations,), out_shape=jax.ShapeDtype...]
  transfers between devices with their start and end apart: 9 -> 6, of which waited for: 7 -> 4; matrix products, arithmetic and copies ran while one was open for 10% -> 8% of each run, Pallas kernels for 0% -> 17%
where the time goes in v1:
time: 128 us; the launch traced here: 127 us
  blocking collectives  53.2 us (42%)
  Pallas kernels  37.1 us (29%)
  starting transfers between devices  13.9 us (11%)
  local copies, waits for them, and re-layouts  8.26 us (6%)
  waiting for transfers between devices  8.15 us (6%)
  other arithmetic  6 us (5%)
    all_to_all x1, blocking collectives, on_device(): got = lax.all_to_all(sent, AXES, 0, 0, tiled=True)  53.2 us
    pallas_call x1, Pallas kernels, on_device(): pl.pallas_call(ligand_kernel, grid=(rotations,), out_shape=jax.ShapeDtype...  18 us
    ppermute x4, waiting for transfers between devices, on_device(): lax.ppermute(best, axis, [(i, i ^ step) for i in range(sizes[axis])])  8.14 us
    pallas_call x1, Pallas kernels, on_device(): pl.pallas_call(functools.partial(product_kernel, channels=channels, y_par...  7.48 us
    ppermute x4, starting transfers between devices, on_device(): lax.ppermute(best, axis, [(i, i ^ step) for i in range(sizes[axis])])  5.98 us
    all_to_all x1, starting transfers between devices, on_device(): lax.all_to_all(components.reshape(devices, comps * SUBLANES, LANES), AXES...  4.88 us
    unnamed x9, local copies, waits for them, and re-layouts  4.65 us
    pallas_call x1, Pallas kernels, on_device(): pl.pallas_call(inverse_x_kernel, grid=(rotations,), out_shape=[jax.ShapeD...  4.6 us
  transfers between devices with their start and end apart: 6, of which 4 were waited for; matrix products, arithmetic and copies ran while one was open for 8% of the time, Pallas kernels for 17%

profile of v1, /device:TPU:0, one launch (start us, length us, event | category | flops | bytes accessed | tf_op | source)
XLA Modules:
  0.0 127.5 jit_solution(4528931327279698338)
XLA Ops:
  0.6 3.1 %collective-permute-start = (s32[4,2048]{1,0:T(4,128)}, s32[4,2048]{1,0:T(4,128)S(1)}, u32[]{:S(2)}, u32[]{:S(2)}) collective-permute-start(s32[4,2048]{1,0:T(4,128)} %param.13), channel_id=1, source_target_pairs={{0,16},{16,0},{1,17},{17,1},{2,18},{18,2},{3,19},{19,3},{4,20},{20... | collective-permute-start | bytes 98312 | tf_op jit(solution)/shard_map/ppermute | solution.py:271
  3.7 3.8 %copy.17.grid_ref = f32[1,128,32,32]{3,2,1,0:T(8,128)} copy(f32[1,128,32,32]{1,3,2,0:T(8,128)} %param.12) | data formatting | bytes 1048576 | tf_op args[0]
  7.5 3.3 %forward_x.1 = f32[1024,128]{1,0:T(8,128)} custom-call(f32[1,128,32,32]{3,2,1,0:T(8,128)} %copy.17.grid_ref, bf16[128,128]{1,0:T(8,128)(2,1)} %constant.78.clone.head_ref, bf16[128,128]{1,0:T(8,128)(2,1)} %constant.79.clone.rest_ref), custom_call_target="tpu_custom_call" | custom-call | tf_op jit(solution)/shard_map/forward_x/pallas_call | solution.py:273
  10.9 4.9 %all-to-all-start = ((f32[32,32,128]{2,1,0:T(8,128)}), f32[32,32,128]{2,1,0:T(8,128)S(1)}, u32[]{:S(2)}, u32[]{:S(2)}) async-start(f32[32,32,128]{2,1,0:T(8,128)} %bitcast.13), calls=%async_computation | async-start | bytes 1048576 | tf_op jit(solution)/shard_map/all_to_all | solution.py:281
  15.8 0.0 copy-done.2
  15.8 0.0 copy-done.3
  15.9 0.0 collective-permute-done
  16.0 0.0 copy-done.1
  16.1 0.8 broadcast_multiply_fusion.2
  16.9 0.3 broadcast_multiply_fusion.1
  17.2 4.0 %fusion.2 = f32[4,2,2,2,2048]{4,3,2,1,0:T(2,128)S(1)} fusion(s32[4,2,2,1,2048]{4,3,2,1,0:T(1,128)S(1)} %get-tuple-element.9, s32[4,2,2,1,2048]{4,3,2,1,0:T(1,128)S(1)} %get-tuple-element.8), kind=kLoop, calls=%fused_computation.5 | loop fusion | flops 917504 | bytes 524288 | tf_op jit(solution)/shard_map/cos | solution.py:295
  21.2 0.2 mul.99
  21.4 0.4 mul.100
  21.8 0.8 broadcast_multiply_fusion.values_ref
  22.6 18.0 %ligand.1.ligand_ref = f32[4,256,1024]{2,1,0:T(8,128)} custom-call(s32[1,1]{1,0:T(1,128)} %bitcast.special_ref, f32[4,2,8,2048]{3,2,1,0:T(8,128)} %broadcast_multiply_fusion.values_ref, s32[4,2,2048]{2,1,0:T(2,128)} %get-tuple-element.10.cell_ref, bf16[256,256]{1,0:T(8,128)(2,1)} %constant.74.clone.zh, bf16[256,256]{1,0:T(8,128)(2,1)} %constant.75.clone.zr, ...), custom_call_target="tpu_custom_call" | custom-call | tf_op jit(solution)/shard_map/ligand/pallas_call | solution.py:303
  40.6 0.0 all-to-all-done.blocks_ref
  40.6 0.8 copy-done
  41.4 3.7 %receptor.1.receptor_ref = f32[256,768]{1,0:T(8,128)} custom-call(s32[1,1]{1,0:T(1,128)} %bitcast.special_ref, f32[32,32,128]{2,1,0:T(8,128)} %copy-done, bf16[256,256]{1,0:T(8,128)(2,1)} %constant.74.clone.zh, bf16[256,256]{1,0:T(8,128)(2,1)} %constant.75.clone.zr, bf16[256,256]{1,0:T(8,128)(2,1)} %constant.76.clone.yh, bf16[256,256]{1,0:T(8,128)(2,1)} %constant.77.clone.yr), custom_call_target="tpu_custom_call" | custom-call | tf_op jit(solution)/shard_map/receptor/pallas_call | solution.py:317
  45.2 7.5 %product.1 = f32[32,128,128]{2,1,0:T(8,128)} custom-call(s32[1,1]{1,0:T(1,128)} %bitcast.special_ref, f32[256,768]{1,0:T(8,128)} %receptor.1.receptor_ref, f32[4,256,1024]{2,1,0:T(8,128)} %ligand.1.ligand_ref, bf16[256,256]{1,0:T(8,128)(2,1)} %constant.74.clone.zh, bf16[256,256]{1,0:T(8,128)(2,1)} %constant.75.clone.zr, bf16[256,256]{1,0:T(8,128)(2,1)} %constant.76.clone.yh, ...), custom_call_target="tpu_custom_call" | custom-call | tf_op jit(solution)/shard_map/product/pallas_call | solution.py:326
  52.6 53.2 %all_to_all.10 = f32[32,128,128]{2,1,0:T(8,128)S(1)} all-to-all(f32[32,128,128]{2,1,0:T(8,128)} %product.1), channel_id=1, replica_groups=mesh['rot'=2,'py'=4,'pz'=4] {'rot','py','pz'}, dimensions={0} | all-to-all | bytes 4194304 | tf_op jit(solution)/shard_map/all_to_all | solution.py:334
  105.9 1.5 %copy.19 = f32[32,4,32,128]{3,2,0,1:T(8,128)} copy(f32[32,4,32,128]{3,2,1,0:T(8,128)S(1)} %bitcast.12) | data formatting | bytes 4194304 | tf_op jit(solution)/shard_map/reshape | solution.py:335
  107.4 4.6 %inverse_x.1 = (f32[4,32,32,128]{3,2,1,0:T(8,128)}, f32[4,8,128]{2,1,0:T(8,128)}) custom-call(f32[4,1024,128]{2,1,0:T(8,128)} %bitcast.11, bf16[128,128]{1,0:T(8,128)(2,1)} %constant.80.clone.head_ref, bf16[128,128]{1,0:T(8,128)(2,1)} %constant.81.clone.rest_ref), custom_call_target="tpu_custom_call" | custom-call | tf_op jit(solution)/shard_map/inverse_x/pallas_call | solution.py:337
  112.0 0.7 slice.6
  112.7 1.7 %collective-permute-start.1 = (f32[4,128]{1,0:T(4,128)S(1)}, f32[4,128]{1,0:T(4,128)S(1)}, u32[]{:S(2)}, u32[]{:S(2)}) collective-permute-start(f32[4,128]{1,0:T(4,128)S(1)} %bitcast.14), channel_id=1, source_target_pairs={{0,4},{4,0},{8,12},{12,8},{1,5},{5,1},{9,13},{13,9},{2,6},{6,2},{1... | collective-permute-start | bytes 6152 | tf_op jit(solution)/shard_map/ppermute | solution.py:355
  114.4 0.8 collective-permute-done.1
  115.2 1.5 %collective-permute-start.2 = (f32[4,128]{1,0:T(4,128)S(1)}, f32[4,128]{1,0:T(4,128)S(1)}, u32[]{:S(2)}, u32[]{:S(2)}) collective-permute-start(f32[4,128]{1,0:T(4,128)S(1)} %max.12), channel_id=1, source_target_pairs={{0,8},{4,12},{8,0},{12,4},{1,9},{5,13},{9,1},{13,5},{2,10},{6,14},... | collective-permute-start | bytes 6152 | tf_op jit(solution)/shard_map/ppermute | solution.py:355
  116.7 2.1 %collective-permute-done.2 = f32[4,128]{1,0:T(4,128)S(1)} collective-permute-done((f32[4,128]{1,0:T(4,128)S(1)}, f32[4,128]{1,0:T(4,128)S(1)}, u32[]{:S(2)}, u32[]{:S(2)}) %collective-permute-start.2) | collective-permute-done | bytes 2080 | tf_op jit(solution)/shard_map/ppermute | solution.py:355
  118.8 1.8 %collective-permute-start.3 = (f32[4,128]{1,0:T(4,128)S(1)}, f32[4,128]{1,0:T(4,128)S(1)}, u32[]{:S(2)}, u32[]{:S(2)}) collective-permute-start(f32[4,128]{1,0:T(4,128)S(1)} %max.13), channel_id=1, source_target_pairs={{0,1},{1,0},{2,3},{3,2},{4,5},{5,4},{6,7},{7,6},{8,9},{9,8},{10,11... | collective-permute-start | bytes 6152 | tf_op jit(solution)/shard_map/ppermute | solution.py:355
  120.6 1.8 %collective-permute-done.3 = f32[4,128]{1,0:T(4,128)S(1)} collective-permute-done((f32[4,128]{1,0:T(4,128)S(1)}, f32[4,128]{1,0:T(4,128)S(1)}, u32[]{:S(2)}, u32[]{:S(2)}) %collective-permute-start.3) | collective-permute-done | bytes 2080 | tf_op jit(solution)/shard_map/ppermute | solution.py:355
  122.4 1.1 collective-permute-start.4
  123.4 3.4 %collective-permute-done.4 = f32[4,128]{1,0:T(4,128)S(1)} collective-permute-done((f32[4,128]{1,0:T(4,128)S(1)}, f32[4,128]{1,0:T(4,128)S(1)}, u32[]{:S(2)}, u32[]{:S(2)}) %collective-permute-start.4) | collective-permute-done | bytes 2080 | tf_op jit(solution)/shard_map/ppermute | solution.py:355
  126.9 0.6 slice_reduce_fusion
  (16 shorter events, 0.2 us)
Async XLA Ops:
  0.6 15.3 %collective-permute-start = (s32[4,2048]{1,0:T(4,128)}, s32[4,2048]{1,0:T(4,128)S(1)}, u32[]{:S(2)}, u32[]{:S(2)}) collective-permute-start(s32[4,2048]{1,0:T(4,128)} %param.13), channel_id=1, source_target_pairs={{0,16},{16,0},{1,17},{17,1},{2,18},{18,2},{3,19},{19,3},{4,20},{20... | collective-permute-start | bytes 98312 | tf_op jit(solution)/shard_map/ppermute | solution.py:271
  7.5 8.3 %copy-start.2 = (f32[2048]{0:T(1024)S(1)}, f32[2048]{0:T(1024)}, u32[]{:S(2)}) copy-start(f32[2048]{0:T(1024)} %param.15) | copy-start | bytes 24580
  7.5 8.3 %copy-start.3 = (f32[2048]{0:T(1024)S(1)}, f32[2048]{0:T(1024)}, u32[]{:S(2)}) copy-start(f32[2048]{0:T(1024)} %param.14) | copy-start | bytes 24580
  7.5 8.4 %copy-start.1 = (s32[4,2048]{1,0:T(4,128)S(1)}, s32[4,2048]{1,0:T(4,128)}, u32[]{:S(2)}) copy-start(s32[4,2048]{1,0:T(4,128)} %param.13) | copy-start | bytes 98308
  10.9 29.8 %all-to-all-start = ((f32[32,32,128]{2,1,0:T(8,128)}), f32[32,32,128]{2,1,0:T(8,128)S(1)}, u32[]{:S(2)}, u32[]{:S(2)}) async-start(f32[32,32,128]{2,1,0:T(8,128)} %bitcast.13), calls=%async_computation | async-start | bytes 1048576 | tf_op jit(solution)/shard_map/all_to_all | solution.py:281
  40.6 0.8 copy-start
  112.7 2.5 %collective-permute-start.1 = (f32[4,128]{1,0:T(4,128)S(1)}, f32[4,128]{1,0:T(4,128)S(1)}, u32[]{:S(2)}, u32[]{:S(2)}) collective-permute-start(f32[4,128]{1,0:T(4,128)S(1)} %bitcast.14), channel_id=1, source_target_pairs={{0,4},{4,0},{8,12},{12,8},{1,5},{5,1},{9,13},{13,9},{2,6},{6,2},{1... | collective-permute-start | bytes 6152 | tf_op jit(solution)/shard_map/ppermute | solution.py:355
  115.2 3.6 %collective-permute-start.2 = (f32[4,128]{1,0:T(4,128)S(1)}, f32[4,128]{1,0:T(4,128)S(1)}, u32[]{:S(2)}, u32[]{:S(2)}) collective-permute-start(f32[4,128]{1,0:T(4,128)S(1)} %max.12), channel_id=1, source_target_pairs={{0,8},{4,12},{8,0},{12,4},{1,9},{5,13},{9,1},{13,5},{2,10},{6,14},... | collective-permute-start | bytes 6152 | tf_op jit(solution)/shard_map/ppermute | solution.py:355
  118.8 3.6 %collective-permute-start.3 = (f32[4,128]{1,0:T(4,128)S(1)}, f32[4,128]{1,0:T(4,128)S(1)}, u32[]{:S(2)}, u32[]{:S(2)}) collective-permute-start(f32[4,128]{1,0:T(4,128)S(1)} %max.13), channel_id=1, source_target_pairs={{0,1},{1,0},{2,3},{3,2},{4,5},{5,4},{6,7},{7,6},{8,9},{9,8},{10,11... | collective-permute-start | bytes 6152 | tf_op jit(solution)/shard_map/ppermute | solution.py:355
  122.4 4.5 %collective-permute-start.4 = (f32[4,128]{1,0:T(4,128)S(1)}, f32[4,128]{1,0:T(4,128)S(1)}, u32[]{:S(2)}, u32[]{:S(2)}) collective-permute-start(f32[4,128]{1,0:T(4,128)S(1)} %max.14), channel_id=1, source_target_pairs={{0,2},{1,3},{2,0},{3,1},{4,6},{5,7},{6,4},{7,5},{8,10},{9,11},{10,... | collective-permute-start | bytes 6152 | tf_op jit(solution)/shard_map/ppermute | solution.py:355

commit v2 on v1

--- a/solution.py
+++ b/solution.py
@@ -58,76 +58,99 @@
     return jnp.dot(a, b, preferred_element_type=jnp.float32)
 
 
+def dot_rows(a, b):
+    return lax.dot_general(a, b, (((1,), (1,)), ((), ())), preferred_element_type=jnp.float32)
+
+
 def times_constant(value, head_ref, rest_ref):
     head, rest = split(value)
     return dot(head, head_ref[...]) + (dot(head, rest_ref[...]) + dot(rest, head_ref[...]))
 
 
-def constant_times(head_ref, rest_ref, value):
-    head, rest = split(value)
-    return dot(head_ref[...], head) + (dot(rest_ref[...], head) + dot(head_ref[...], rest))
+def constant_times(head_ref, rest_ref, values):
+    results = []
+    for i in range(0, len(values), 2):
+        pair = values[i : i + 2]
+        head, rest = split(jnp.concatenate(pair, axis=1))
+        result = dot(head_ref[...], head) + (dot(rest_ref[...], head) + dot(head_ref[...], rest))
+        width = pair[0].shape[1]
+        results += [result[:, j * width : (j + 1) * width] for j in range(len(pair))]
+    return results
 
 
 def swap_groups(pieces, width):
-    return [
-        jnp.concatenate([piece[..., q * width : (q + 1) * width] for piece in pieces], axis=-1)
-        for q in range(len(pieces))
-    ]
-
-
-def forward_x_kernel(grid_ref, head_ref, rest_ref, out_ref, rows_ref):
-    n, y_block, z_block = grid_ref.shape[1:]
+    pieces = list(pieces)
+    lane = lax.broadcasted_iota(jnp.int32, pieces[0].shape, 1)
+    bit = len(pieces) // 2
+    while bit:
+        low = lane // (bit * width) % 2 == 0
+        for i in range(len(pieces)):
+            if i & bit == 0:
+                first, second = pieces[i], pieces[i | bit]
+                pieces[i] = jnp.where(low, first, pltpu.roll(second, bit * width, 1))
+                pieces[i | bit] = jnp.where(low, pltpu.roll(first, LANES - bit * width, 1), second)
+        bit //= 2
+    return pieces
+
+
+def forward_x_kernel(grid_ref, head_ref, rest_ref, out_ref):
+    y_block, z_block, n = grid_ref.shape[1:]
     groups = LANES // z_block
     high = y_block // groups
-    rows_ref[...] = jnp.concatenate(
-        [grid_ref[0, :, g * high : (g + 1) * high, :] for g in range(groups)], axis=-1
-    ).reshape(n * high, LANES)
     for row in range(high):
-        values = rows_ref[pl.ds(row, n, stride=high), :]
-        out_ref[pl.ds(row, n, stride=high), :] = constant_times(head_ref, rest_ref, values)
+        values = jnp.concatenate([grid_ref[0, g * high + row] for g in range(groups)], axis=0)
+        head, rest = split(values)
+        out_ref[pl.ds(row, n, stride=high), :] = dot_rows(head_ref[...], head) + (
+            dot_rows(rest_ref[...], head) + dot_rows(head_ref[...], rest)
+        )
+
+
+def one_hot_rows(count, place):
+    rows = lax.broadcasted_iota(jnp.int32, (count, place.shape[1]), 0)
+    return jnp.where(rows == place, 1.0, 0.0).astype(jnp.bfloat16)
 
 
 def spectrum(planes, n, zh, zr, yh, yr):
-    count = len(planes)
-    rows = jnp.concatenate([jnp.concatenate(pair, axis=1) for pair in planes], axis=0)
-    rows = times_constant(rows, zh, zr)
-    columns = jnp.concatenate(
-        [
-            jnp.concatenate([rows[i * n : (i + 1) * n, :n], rows[i * n : (i + 1) * n, n:]], axis=0)
-            for i in range(count)
-        ],
-        axis=1,
-    )
-    return constant_times(yh, yr, columns)
-
-
-def ligand_kernel(special_ref, values_ref, cell_ref, zh, zr, yh, yr, out_ref):
+    columns = []
+    for i in range(0, len(planes), 2):
+        pairs = planes[i : i + 2]
+        rows = jnp.concatenate([jnp.concatenate(pair, axis=1) for pair in pairs], axis=0)
+        rows = times_constant(rows, zh, zr)
+        columns += [
+            jnp.concatenate([rows[j * n : (j + 1) * n, :n], rows[j * n : (j + 1) * n, n:]], axis=0)
+            for j in range(len(pairs))
+        ]
+    return jnp.concatenate(constant_times(yh, yr, columns), axis=1)
+
+
+def ligand_kernel(place_ref, own_ref, other_ref, shape_ref, charge_ref, table_ref, zh, zr, yh, yr, out_ref):
     n = zh.shape[0] // 2
-    comps, atoms = values_ref.shape[-2:]
     half = n // 2
-    special = special_ref[0, 0] > 0
+    atoms = own_ref.shape[1]
+    step = pl.program_id(0)
+    device = place_ref[0]
+    first_half = device < table_ref.shape[0] // 2
+    special = device == 0
+    own, other = own_ref[pl.ds(step, 1), :], other_ref[pl.ds(step, 1), :]
     grids = []
-    for rotation in range(2):
-        cell = cell_ref[0, rotation : rotation + 1, :]
-        y_low = (cell // n) % half
-        place = cell % n + n * ((cell // (n * half)) % 2)
-        head = values_ref[0, rotation].astype(jnp.bfloat16).astype(jnp.float32)
-        rest = (values_ref[0, rotation] - head).astype(jnp.bfloat16).astype(jnp.float32)
-        hit = lax.broadcasted_iota(jnp.int32, (half, atoms), 0) == y_low
+    for cell in (jnp.where(first_half, own, other), jnp.where(first_half, other, own)):
+        coord_x, coord_y, coord_z = cell // (n * n), cell // n % n, cell % n
+        wave = dot(table_ref[device], one_hot_rows(n, coord_x))
+        comps = wave.shape[0] // 4
+        wave = wave[:comps] + (wave[comps : 2 * comps] + wave[2 * comps : 3 * comps])
+        values = jnp.concatenate([wave * shape_ref[...], wave * charge_ref[...]], axis=0)
+        comps = values.shape[0]
+        head = values.astype(jnp.bfloat16).astype(jnp.float32)
+        hit = lax.broadcasted_iota(jnp.int32, (half, atoms), 0) == coord_y % half
         stacked = jnp.concatenate(
             [
                 jnp.where(hit, part[c : c + 1, :], 0.0).astype(jnp.bfloat16)
-                for part in (head, rest)
+                for part in (head, values - head)
                 for c in range(comps)
             ],
             axis=0,
         )
-        one_hot = (
-            lax.broadcasted_iota(jnp.int32, (2 * n, atoms), 0) == place
-        ).astype(jnp.float32).astype(jnp.bfloat16)
-        total = lax.dot_general(
-            stacked, one_hot, (((1,), (1,)), ((), ())), preferred_element_type=jnp.float32
-        )
+        total = dot_rows(stacked, one_hot_rows(2 * n, coord_z + n * (coord_y // half)))
         total = total[: comps * half] + total[comps * half :]
         grids.append(
             [
@@ -140,7 +163,7 @@
     planes = [[], []]
     for c in range(0, comps, 2):
         first, second = (grids[0][c], grids[0][c + 1]), (grids[1][c], grids[1][c + 1])
-        if c < 4:
+        if c % (comps // 2) == 0:
             first, second = (
                 (first[0], jnp.where(special, second[0], first[1])),
                 (jnp.where(special, first[1], second[0]), second[1]),
@@ -150,11 +173,10 @@
     out_ref[0] = spectrum(planes[0] + planes[1], n, zh, zr, yh, yr)
 
 
-def receptor_kernel(special_ref, blocks_ref, zh, zr, yh, yr, out_ref, *, channels, y_parts, z_parts):
+def receptor_spectrum(special, blocks_ref, zh, zr, yh, yr, channels, y_parts, z_parts):
     n = zh.shape[0] // 2
     width = n // z_parts
     comps = blocks_ref.shape[1] // SUBLANES
-    special = special_ref[0, 0] > 0
     planes = []
     for channel in range(channels):
         parts = []
@@ -171,22 +193,30 @@
         planes.append((jnp.where(special, parts[1], parts[0]), lone))
         for c in range(2, comps, 2):
             planes.append((parts[c], parts[c + 1]))
-    out_ref[...] = spectrum(planes, n, zh, zr, yh, yr)
-
-
-def product_kernel(special_ref, receptor_ref, ligand_ref, zh, zr, yh, yr, out_ref, *, channels, y_parts, z_parts):
+    return spectrum(planes, n, zh, zr, yh, yr)
+
+
+def product_kernel(
+    place_ref, blocks_ref, ligand_ref, zh, zr, yh, yr, out_ref, receptor_ref, *, channels, y_parts, z_parts
+):
     n = zh.shape[0] // 2
     width = n // z_parts
     groups = LANES // width
     slots = ligand_ref.shape[2] // (2 * channels * n)
-    special = special_ref[0, 0] > 0
+    special = place_ref[0] == 0
+
+    @pl.when(pl.program_id(0) == 0)
+    def _():
+        receptor_ref[...] = receptor_spectrum(
+            special, blocks_ref, zh, zr, yh, yr, channels, y_parts, z_parts
+        )
 
     def receptor(channel, slot, rotation):
         at = channel * (slots + 1) + (rotation if slot == 0 else slot + 1)
         return receptor_ref[:n, at * n : (at + 1) * n], receptor_ref[n:, at * n : (at + 1) * n]
 
     def ligand(channel, slot, rotation):
-        at = (rotation * slots + slot) * channels + channel
+        at = (rotation * channels + channel) * slots + slot
         return ligand_ref[0, :n, at * n : (at + 1) * n], ligand_ref[0, n:, at * n : (at + 1) * n]
 
     columns = []
@@ -199,14 +229,8 @@
                 real = real + (fr * hr + fi * hi)
                 imag = imag + (fr * hi - fi * hr)
             columns.append(jnp.concatenate([real, imag], axis=0))
-    columns = constant_times(yh, yr, jnp.concatenate(columns, axis=1))
-    rows = jnp.concatenate(
-        [
-            jnp.concatenate([columns[:n, i * n : (i + 1) * n], columns[n:, i * n : (i + 1) * n]], axis=1)
-            for i in range(2 * slots)
-        ],
-        axis=0,
-    )
+    columns = constant_times(yh, yr, columns)
+    rows = jnp.concatenate([jnp.concatenate([c[:n], c[n:]], axis=1) for c in columns], axis=0)
     rows = times_constant(rows, zh, zr)
     maps = [
         [
@@ -232,26 +256,34 @@
                         out_ref[(rotation * y_parts + y_part) * z_parts + z_part, row : row + SUBLANES, :] = block
 
 
-def inverse_x_kernel(blocks_ref, head_ref, rest_ref, out_ref, best_ref):
+def inverse_x_kernel(blocks_ref, head_ref, rest_ref, out_ref, best_ref, rows_ref):
     n = head_ref.shape[0]
     y_block, z_block = out_ref.shape[1:3]
     groups = LANES // z_block
+    rows_ref[...] = blocks_ref[...].reshape(rows_ref.shape)
     best = None
     for row in range(SUBLANES):
-        values = blocks_ref[0, pl.ds(row, n, stride=SUBLANES), :]
+        values = rows_ref[pl.ds(row, n, stride=SUBLANES), :]
         result = times_constant(values.T, head_ref, rest_ref)
         for g in range(groups):
             out_ref[0, g * SUBLANES + row] = result[g * z_block : (g + 1) * z_block, :]
         best = result if best is None else jnp.maximum(best, result)
-    best_ref[0] = jnp.broadcast_to(jnp.max(best, axis=(0, 1), keepdims=True), (SUBLANES, LANES))
+    best_ref[pl.program_id(0)] = jnp.max(best)
 
 
 def whole():
     return pl.BlockSpec(memory_space=pltpu.VMEM)
 
 
-def scalar():
+def scalars():
     return pl.BlockSpec(memory_space=pltpu.SMEM)
+
+
+def component_tables(n, comps):
+    matrix = forward_x_matrix(n).reshape(n // comps, comps, n)
+    head, rest = split_constant(matrix)
+    last = (matrix - head.astype(np.float64) - rest.astype(np.float64)).astype(jnp.bfloat16)
+    return np.concatenate([head, rest, last, np.zeros_like(head)], axis=1)
 
 
 def on_device(receptor_grids, ligand_cells, atom_shape, atom_charges, *, sizes):
@@ -260,14 +292,14 @@
     devices = rots * y_parts * z_parts
     slots = n // 2 // devices
     comps = 2 * slots
+    rows = comps * SUBLANES
     y_block, z_block = receptor_grids.shape[2:]
     rotations, atoms = ligand_cells.shape
     channels = 2
-    planes = [jnp.asarray(m) for m in split_constant(plus_matrix(n))]
-    planes += [m.T for m in (np.asarray(p) for p in split_constant(plus_matrix(n)))]
-    planes = [jnp.asarray(m) for m in planes]
     f32 = jnp.float32
-
+    matrices = split_constant(plus_matrix(n))
+    matrices = [jnp.asarray(m) for m in (*matrices, *(np.ascontiguousarray(m.T) for m in matrices))]
+    place = lax.axis_index(AXES).reshape(1)
     other = lax.ppermute(ligand_cells, "rot", [(i, i ^ 1) for i in range(rots)])
 
     components = pl.pallas_call(
@@ -275,86 +307,58 @@
         out_shape=jax.ShapeDtypeStruct((n * SUBLANES, LANES), f32),
         in_specs=[whole()] * 3,
         out_specs=whole(),
-        scratch_shapes=[pltpu.VMEM((n * SUBLANES, LANES), f32)],
         name="forward_x",
-    )(receptor_grids, *(jnp.asarray(m) for m in split_constant(forward_x_matrix(n))))
-    blocks = lax.all_to_all(components.reshape(devices, comps * SUBLANES, LANES), AXES, 0, 0, tiled=True)
-
-    mine = lax.axis_index("rot") == 0
-    cells = jnp.stack(
-        [jnp.where(mine, ligand_cells, other), jnp.where(mine, other, ligand_cells)], axis=1
-    )
-    device = lax.axis_index(AXES)
-    coord_x = cells // (n * n)
-    slot = device * slots + jnp.arange(slots, dtype=jnp.int32)
-    turns = slot[:, None] * coord_x[:, :, None, None, :]
-    quarter = jnp.where(
-        slot[:, None] == 0, (n // 2) * coord_x[:, :, None, None, :], turns - n // 4
-    )
-    phase = jnp.concatenate([turns[..., None, :], quarter[..., None, :]], axis=-2) % n
-    wave = jnp.cos(phase.astype(f32) * (2.0 * math.pi / n))
-    weights = jnp.stack([atom_shape, atom_charges], 0)[:, None, :]
-    wave = jnp.swapaxes(wave, 2, 3) if wave.shape[2] == 1 else wave
-    wave = wave.reshape(rotations, rots, slots, 1, 2, atoms)
-    values = (wave * weights).reshape(rotations, rots, slots * channels * 2, atoms)
-    special = (device == 0).astype(jnp.int32).reshape(1, 1)
+    )(jnp.transpose(receptor_grids, (0, 2, 3, 1)), *(jnp.asarray(m) for m in split_constant(forward_x_matrix(n))))
+    components, other = lax.optimization_barrier((components, other))
+    blocks = lax.all_to_all(components.reshape(devices, rows, LANES), AXES, 0, 0, tiled=True)
 
     width = 2 * slots * channels * n
     ligand = pl.pallas_call(
         ligand_kernel,
         grid=(rotations,),
         out_shape=jax.ShapeDtypeStruct((rotations, 2 * n, width), f32),
-        in_specs=[
-            scalar(),
-            pl.BlockSpec((1, rots, slots * channels * 2, atoms), lambda i: (i, 0, 0, 0)),
-            pl.BlockSpec((1, rots, atoms), lambda i: (i, 0, 0)),
-        ]
-        + [whole()] * 4,
+        in_specs=[scalars()] + [whole()] * 9,
         out_specs=pl.BlockSpec((1, 2 * n, width), lambda i: (i, 0, 0)),
         name="ligand",
-    )(special, values, cells, *planes)
-
-    receptor = pl.pallas_call(
-        functools.partial(receptor_kernel, channels=channels, y_parts=y_parts, z_parts=z_parts),
-        out_shape=jax.ShapeDtypeStruct((2 * n, channels * (slots + 1) * n), f32),
-        in_specs=[scalar()] + [whole()] * 5,
-        out_specs=whole(),
-        name="receptor",
-    )(special, blocks, *planes)
-
-    rows = comps * SUBLANES
+    )(
+        place,
+        ligand_cells,
+        other,
+        atom_shape.reshape(1, atoms),
+        atom_charges.reshape(1, atoms),
+        jnp.asarray(component_tables(n, comps)),
+        *matrices,
+    )
+
     sent = pl.pallas_call(
         functools.partial(product_kernel, channels=channels, y_parts=y_parts, z_parts=z_parts),
         grid=(rotations,),
         out_shape=jax.ShapeDtypeStruct((devices, rotations * rows, LANES), f32),
-        in_specs=[scalar(), whole(), pl.BlockSpec((1, 2 * n, width), lambda i: (i, 0, 0))] + [whole()] * 4,
+        in_specs=[scalars(), whole(), pl.BlockSpec((1, 2 * n, width), lambda i: (i, 0, 0))] + [whole()] * 4,
         out_specs=pl.BlockSpec((devices, rows, LANES), lambda i: (0, i, 0)),
+        scratch_shapes=[pltpu.VMEM((2 * n, channels * (slots + 1) * n), f32)],
         name="product",
-    )(special, receptor, ligand, *planes)
+    )(place, blocks, ligand, *matrices)
     got = lax.all_to_all(sent, AXES, 0, 0, tiled=True)
-    got = jnp.swapaxes(got.reshape(devices, rotations, rows, LANES), 0, 1).reshape(rotations, devices * rows, LANES)
 
     correlation, best = pl.pallas_call(
         inverse_x_kernel,
         grid=(rotations,),
         out_shape=[
             jax.ShapeDtypeStruct((rotations, y_block, z_block, n), f32),
-            jax.ShapeDtypeStruct((rotations, SUBLANES, LANES), f32),
+            jax.ShapeDtypeStruct((rotations,), f32),
         ],
-        in_specs=[pl.BlockSpec((1, devices * rows, LANES), lambda i: (i, 0, 0))] + [whole()] * 2,
-        out_specs=[
-            pl.BlockSpec((1, y_block, z_block, n), lambda i: (i, 0, 0, 0)),
-            pl.BlockSpec((1, SUBLANES, LANES), lambda i: (i, 0, 0)),
-        ],
+        in_specs=[pl.BlockSpec((devices, rows, LANES), lambda i: (0, i, 0))] + [whole()] * 2,
+        out_specs=[pl.BlockSpec((1, y_block, z_block, n), lambda i: (i, 0, 0, 0)), scalars()],
+        scratch_shapes=[pltpu.VMEM((devices * rows, LANES), f32)],
         name="inverse_x",
     )(got, *(jnp.asarray(m) for m in split_constant(inverse_x_matrix(n))))
-    best = best[:, 0, :]
     for axis in ("py", "pz"):
         step = 1
         while step < sizes[axis]:
             best = jnp.maximum(best, lax.ppermute(best, axis, [(i, i ^ step) for i in range(sizes[axis])]))
             step *= 2
-    return correlation, best[:, 0]
+    return correlation, best
 
 
 def twiddle(length, inverse):

time: 128 us -> 111 us (0.87)
  local copies, waits for them, and re-layouts: 8.26 us -> 0.81 us
  Pallas kernels: 37.1 us -> 31.3 us
  other arithmetic: 6 us -> 1.18 us
    cos x1 -> x0, other arithmetic: 3.99 us -> none  [on_device(): wave = jnp.cos(phase.astype(f32) * (2.0 * math.pi / n))]
    unnamed x9 -> x4, local copies, waits for them, and re-layouts: 4.65 us -> 0.81 us
    pallas_call x1 -> x0, Pallas kernels: 3.73 us -> none  [on_device(): pl.pallas_call(functools.partial(receptor_kernel, channels=channels, y_pa...]
    pallas_call x1, Pallas kernels: 18 us -> 15.9 us  [on_device(): pl.pallas_call(ligand_kernel, grid=(rotations,), out_shape=jax.ShapeDtype...]
    mul x3 -> x0, other arithmetic: 1.94 us -> none  [the longest x1 0.84 us: on_device(): wave * weights]
    reshape x1 -> x0, local copies, waits for them, and re-layouts: 1.53 us -> none  [on_device(): got.reshape(devices, rotations, rows, LANES)]
    slice x2 -> x0, local copies, waits for them, and re-layouts: 1.35 us -> none  [the longest x1 0.72 us: on_device(): best = best[:, 0, :]]
  transfers between devices with their start and end apart: 6 -> 6, of which waited for: 4 -> 4; matrix products, arithmetic and copies ran while one was open for 8% -> 0% of each run, Pallas kernels for 17% -> 17%
where the time goes in v2:
time: 111 us
  blocking collectives  53.3 us (48%)
  Pallas kernels  31.3 us (28%)
  starting transfers between devices  15 us (14%)
  waiting for transfers between devices  8.23 us (7%)
  other arithmetic  1.18 us (1%)
    all_to_all x1, blocking collectives, on_device(): got = lax.all_to_all(sent, AXES, 0, 0, tiled=True)  53.3 us
    pallas_call x1, Pallas kernels, on_device(): pl.pallas_call(ligand_kernel, grid=(rotations,), out_shape=jax.ShapeDtype...  15.9 us
    ppermute x4, waiting for transfers between devices, on_device(): lax.ppermute(best, axis, [(i, i ^ step) for i in range(sizes[axis])])  8.23 us
    pallas_call x1, Pallas kernels, on_device(): pl.pallas_call(functools.partial(product_kernel, channels=channels, y_par...  8.14 us
    ppermute x4, starting transfers between devices, on_device(): lax.ppermute(best, axis, [(i, i ^ step) for i in range(sizes[axis])])  5.98 us
    all_to_all x1, starting transfers between devices, on_device(): lax.all_to_all(components.reshape(devices, rows, LANES), AXES, 0, 0, tile...  5.93 us
    pallas_call x1, Pallas kernels, on_device(): pl.pallas_call(inverse_x_kernel, grid=(rotations,), out_shape=[jax.ShapeD...  4.72 us
    ppermute x1, starting transfers between devices, on_device(): other = lax.ppermute(ligand_cells, 'rot', [(i, i ^ 1) for i in range(rots)])  3.06 us
  transfers between devices with their start and end apart: 6, of which 4 were waited for; matrix products, arithmetic and copies ran while one was open for 0% of the time, Pallas kernels for 17%

profile of v2, /device:TPU:0, one launch (start us, length us, event | category | flops | bytes accessed | tf_op | source)
XLA Modules:
  0.0 110.5 jit_solution(12088366980623327424)
XLA Ops:
  0.6 3.1 %collective-permute-start = (s32[4,2048]{1,0:T(4,128)}, s32[4,2048]{1,0:T(4,128)S(1)}, u32[]{:S(2)}, u32[]{:S(2)}) collective-permute-start(s32[4,2048]{1,0:T(4,128)} %own_ref.1), channel_id=1, source_target_pairs={{0,16},{16,0},{1,17},{17,1},{2,18},{18,2},{3,19},{19,3},{4,20},{20... | collective-permute-start | bytes 98312 | tf_op jit(solution)/shard_map/ppermute | solution.py:303
  3.7 2.5 %forward_x.1 = f32[1024,128]{1,0:T(8,128)} custom-call(f32[1,32,32,128]{3,2,1,0:T(8,128)} %bitcast.6, bf16[128,128]{1,0:T(8,128)(2,1)} %constant.39.clone.head_ref, bf16[128,128]{1,0:T(8,128)(2,1)} %constant.40.clone.rest_ref), custom_call_target="tpu_custom_call" | custom-call | tf_op jit(solution)/shard_map/forward_x/pallas_call | solution.py:305
  6.2 0.0 collective-permute-done.other_ref
  6.2 0.0 copy-start.1
  6.2 5.9 %all-to-all-start = ((f32[32,32,128]{2,1,0:T(8,128)}), f32[32,32,128]{2,1,0:T(8,128)S(1)}, u32[]{:S(2)}, u32[]{:S(2)}) async-start(f32[32,32,128]{2,1,0:T(8,128)} %bitcast.5), calls=%async_computation | async-start | bytes 1048576 | tf_op jit(solution)/shard_map/all_to_all | solution.py:313
  12.2 0.0 copy-done.1
  12.2 15.9 %ligand.1.ligand_ref = f32[4,256,1024]{2,1,0:T(8,128)} custom-call(s32[1]{0:T(128)} %bitcast.place_ref, s32[4,2048]{1,0:T(4,128)} %own_ref.1, s32[4,2048]{1,0:T(4,128)} %copy-done.1, f32[1,2048]{1,0:T(1,128)} %bitcast.7, f32[1,2048]{1,0:T(1,128)} %bitcast.8, bf16[32,16,128]{2,1,0:T(8,128)(2,1)} %constant.41.clone.table_ref, ...), custom_call_target="tpu_custom_call" | custom-call | tf_op jit(solution)/shard_map/ligand/pallas_call | solution.py:316
  28.1 0.0 all-to-all-done.blocks_ref
  28.1 0.0 copy-start
  28.1 0.8 copy-done
  28.9 8.1 %product.1 = f32[32,128,128]{2,1,0:T(8,128)} custom-call(s32[1]{0:T(128)} %bitcast.place_ref, f32[32,32,128]{2,1,0:T(8,128)} %copy-done, f32[4,256,1024]{2,1,0:T(8,128)} %ligand.1.ligand_ref, bf16[256,256]{1,0:T(8,128)(2,1)} %constant.35.clone.zh, bf16[256,256]{1,0:T(8,128)(2,1)} %constant.36.clone.zr, bf16[256,256]{1,0:T(8,128)(2,1)} %constant.37.clone.yh, ...), custom_call_target="tpu_custom_call" | custom-call | tf_op jit(solution)/shard_map/product/pallas_call | solution.py:333
  37.0 53.3 %all_to_all.10.blocks_ref = f32[32,128,128]{2,1,0:T(8,128)} all-to-all(f32[32,128,128]{2,1,0:T(8,128)} %product.1), channel_id=1, replica_groups=mesh['rot'=2,'py'=4,'pz'=4] {'rot','py','pz'}, dimensions={0} | all-to-all | bytes 4194304 | tf_op jit(solution)/shard_map/all_to_all | solution.py:342
  90.4 4.7 %inverse_x.1 = (f32[4,32,32,128]{3,2,1,0:T(8,128)}, f32[4]{0:T(128)}) custom-call(f32[32,128,128]{2,1,0:T(8,128)} %all_to_all.10.blocks_ref, bf16[128,128]{1,0:T(8,128)(2,1)} %constant.42.clone.head_ref, bf16[128,128]{1,0:T(8,128)(2,1)} %constant.43.clone.rest_ref), custom_call_target="tpu_custom_call" | custom-call | tf_op jit(solution)/shard_map/inverse_x/pallas_call | solution.py:344
  95.1 1.7 %collective-permute-start.1 = (f32[4]{0:T(128)}, f32[4]{0:T(128)S(1)}, u32[]{:S(2)}, u32[]{:S(2)}) collective-permute-start(f32[4]{0:T(128)} %get-tuple-element.9), channel_id=1, source_target_pairs={{0,4},{4,0},{8,12},{12,8},{1,5},{5,1},{9,13},{13,9},{2,6},{6,2},{1... | collective-permute-start | bytes 56 | tf_op jit(solution)/shard_map/ppermute | solution.py:359
  96.8 1.0 collective-permute-done.1
  97.7 0.7 max.12
  98.4 1.5 %collective-permute-start.2 = (f32[4]{0:T(128)S(1)}, f32[4]{0:T(128)S(1)}, u32[]{:S(2)}, u32[]{:S(2)}) collective-permute-start(f32[4]{0:T(128)S(1)} %max.12), channel_id=1, source_target_pairs={{0,8},{4,12},{8,0},{12,4},{1,9},{5,13},{9,1},{13,5},{2,10},{6,14},... | collective-permute-start | bytes 56 | tf_op jit(solution)/shard_map/ppermute | solution.py:359
  99.9 2.1 %collective-permute-done.2 = f32[4]{0:T(128)S(1)} collective-permute-done((f32[4]{0:T(128)S(1)}, f32[4]{0:T(128)S(1)}, u32[]{:S(2)}, u32[]{:S(2)}) %collective-permute-start.2) | collective-permute-done | bytes 48 | tf_op jit(solution)/shard_map/ppermute | solution.py:359
  101.9 1.8 %collective-permute-start.3 = (f32[4]{0:T(128)S(1)}, f32[4]{0:T(128)S(1)}, u32[]{:S(2)}, u32[]{:S(2)}) collective-permute-start(f32[4]{0:T(128)S(1)} %max.13), channel_id=1, source_target_pairs={{0,1},{1,0},{2,3},{3,2},{4,5},{5,4},{6,7},{7,6},{8,9},{9,8},{10,11... | collective-permute-start | bytes 56 | tf_op jit(solution)/shard_map/ppermute | solution.py:359
  103.7 1.8 %collective-permute-done.3 = f32[4]{0:T(128)S(1)} collective-permute-done((f32[4]{0:T(128)S(1)}, f32[4]{0:T(128)S(1)}, u32[]{:S(2)}, u32[]{:S(2)}) %collective-permute-start.3) | collective-permute-done | bytes 48 | tf_op jit(solution)/shard_map/ppermute | solution.py:359
  105.5 1.1 collective-permute-start.4
  106.6 3.4 %collective-permute-done.4 = f32[4]{0:T(128)S(1)} collective-permute-done((f32[4]{0:T(128)S(1)}, f32[4]{0:T(128)S(1)}, u32[]{:S(2)}, u32[]{:S(2)}) %collective-permute-start.4) | collective-permute-done | bytes 48 | tf_op jit(solution)/shard_map/ppermute | solution.py:359
  110.0 0.5 max.15
  (2 shorter events, 0.0 us)
Async XLA Ops:
  0.6 5.6 %collective-permute-start = (s32[4,2048]{1,0:T(4,128)}, s32[4,2048]{1,0:T(4,128)S(1)}, u32[]{:S(2)}, u32[]{:S(2)}) collective-permute-start(s32[4,2048]{1,0:T(4,128)} %own_ref.1), channel_id=1, source_target_pairs={{0,16},{16,0},{1,17},{17,1},{2,18},{18,2},{3,19},{19,3},{4,20},{20... | collective-permute-start | bytes 98312 | tf_op jit(solution)/shard_map/ppermute | solution.py:303
  6.2 6.0 %copy-start.1 = (s32[4,2048]{1,0:T(4,128)}, s32[4,2048]{1,0:T(4,128)S(1)}, u32[]{:S(2)}) copy-start(s32[4,2048]{1,0:T(4,128)S(1)} %collective-permute-done.other_ref) | copy-start | bytes 98308
  6.2 21.9 %all-to-all-start = ((f32[32,32,128]{2,1,0:T(8,128)}), f32[32,32,128]{2,1,0:T(8,128)S(1)}, u32[]{:S(2)}, u32[]{:S(2)}) async-start(f32[32,32,128]{2,1,0:T(8,128)} %bitcast.5), calls=%async_computation | async-start | bytes 1048576 | tf_op jit(solution)/shard_map/all_to_all | solution.py:313
  28.1 0.8 copy-start
  95.1 2.6 %collective-permute-start.1 = (f32[4]{0:T(128)}, f32[4]{0:T(128)S(1)}, u32[]{:S(2)}, u32[]{:S(2)}) collective-permute-start(f32[4]{0:T(128)} %get-tuple-element.9), channel_id=1, source_target_pairs={{0,4},{4,0},{8,12},{12,8},{1,5},{5,1},{9,13},{13,9},{2,6},{6,2},{1... | collective-permute-start | bytes 56 | tf_op jit(solution)/shard_map/ppermute | solution.py:359
  98.4 3.6 %collective-permute-start.2 = (f32[4]{0:T(128)S(1)}, f32[4]{0:T(128)S(1)}, u32[]{:S(2)}, u32[]{:S(2)}) collective-permute-start(f32[4]{0:T(128)S(1)} %max.12), channel_id=1, source_target_pairs={{0,8},{4,12},{8,0},{12,4},{1,9},{5,13},{9,1},{13,5},{2,10},{6,14},... | collective-permute-start | bytes 56 | tf_op jit(solution)/shard_map/ppermute | solution.py:359
  101.9 3.6 %collective-permute-start.3 = (f32[4]{0:T(128)S(1)}, f32[4]{0:T(128)S(1)}, u32[]{:S(2)}, u32[]{:S(2)}) collective-permute-start(f32[4]{0:T(128)S(1)} %max.13), channel_id=1, source_target_pairs={{0,1},{1,0},{2,3},{3,2},{4,5},{5,4},{6,7},{7,6},{8,9},{9,8},{10,11... | collective-permute-start | bytes 56 | tf_op jit(solution)/shard_map/ppermute | solution.py:359
  105.5 4.5 %collective-permute-start.4 = (f32[4]{0:T(128)S(1)}, f32[4]{0:T(128)S(1)}, u32[]{:S(2)}, u32[]{:S(2)}) collective-permute-start(f32[4]{0:T(128)S(1)} %max.14), channel_id=1, source_target_pairs={{0,2},{1,3},{2,0},{3,1},{4,6},{5,7},{6,4},{7,5},{8,10},{9,11},{10,... | collective-permute-start | bytes 56 | tf_op jit(solution)/shard_map/ppermute | solution.py:359

commit v3 on v2

--- a/solution.py
+++ b/solution.py
@@ -13,6 +13,7 @@
 AXES = ("rot", "py", "pz")
 LANES = 128
 SUBLANES = 8
+VMEM_BYTES = 48 << 20
 
 
 def split_constant(matrix):
@@ -123,7 +124,7 @@
     return jnp.concatenate(constant_times(yh, yr, columns), axis=1)
 
 
-def ligand_kernel(place_ref, own_ref, other_ref, shape_ref, charge_ref, table_ref, zh, zr, yh, yr, out_ref):
+def ligand_kernel(place_ref, own_ref, other_ref, shape_ref, charge_ref, table_ref, zh, zr, yh, yr, out_ref, held_ref, sems):
     n = zh.shape[0] // 2
     half = n // 2
     atoms = own_ref.shape[1]
@@ -170,7 +171,13 @@
             )
         planes[0].append(first)
         planes[1].append(second)
-    out_ref[0] = spectrum(planes[0] + planes[1], n, zh, zr, yh, yr)
+    held_ref[step] = spectrum(planes[0] + planes[1], n, zh, zr, yh, yr)
+    pltpu.make_async_copy(held_ref.at[step], out_ref.at[step], sems.at[step]).start()
+
+    @pl.when(step == pl.num_programs(0) - 1)
+    def _():
+        for i in range(held_ref.shape[0]):
+            pltpu.make_async_copy(held_ref.at[i], out_ref.at[i], sems.at[i]).wait()
 
 
 def receptor_spectrum(special, blocks_ref, zh, zr, yh, yr, channels, y_parts, z_parts):
@@ -197,19 +204,24 @@
 
 
 def product_kernel(
-    place_ref, blocks_ref, ligand_ref, zh, zr, yh, yr, out_ref, receptor_ref, *, channels, y_parts, z_parts
+    place_ref, blocks_ref, far_ref, zh, zr, yh, yr, out_ref, receptor_ref, ligand_ref, sems, *, channels, y_parts, z_parts
 ):
     n = zh.shape[0] // 2
     width = n // z_parts
     groups = LANES // width
     slots = ligand_ref.shape[2] // (2 * channels * n)
     special = place_ref[0] == 0
-
-    @pl.when(pl.program_id(0) == 0)
+    step = pl.program_id(0)
+
+    @pl.when(step == 0)
     def _():
+        for i in range(ligand_ref.shape[0]):
+            pltpu.make_async_copy(far_ref.at[i], ligand_ref.at[i], sems.at[i]).start()
         receptor_ref[...] = receptor_spectrum(
             special, blocks_ref, zh, zr, yh, yr, channels, y_parts, z_parts
         )
+
+    pltpu.make_async_copy(far_ref.at[step], ligand_ref.at[step], sems.at[step]).wait()
 
     def receptor(channel, slot, rotation):
         at = channel * (slots + 1) + (rotation if slot == 0 else slot + 1)
@@ -217,7 +229,7 @@
 
     def ligand(channel, slot, rotation):
         at = (rotation * channels + channel) * slots + slot
-        return ligand_ref[0, :n, at * n : (at + 1) * n], ligand_ref[0, n:, at * n : (at + 1) * n]
+        return ligand_ref[step, :n, at * n : (at + 1) * n], ligand_ref[step, n:, at * n : (at + 1) * n]
 
     columns = []
     for rotation in range(2):
@@ -275,6 +287,14 @@
     return pl.BlockSpec(memory_space=pltpu.VMEM)
 
 
+def room(mebibytes):
+    return pltpu.CompilerParams(vmem_limit_bytes=mebibytes << 20)
+
+
+def far():
+    return pl.BlockSpec(memory_space=pltpu.HBM)
+
+
 def scalars():
     return pl.BlockSpec(memory_space=pltpu.SMEM)
 
@@ -307,18 +327,22 @@
         out_shape=jax.ShapeDtypeStruct((n * SUBLANES, LANES), f32),
         in_specs=[whole()] * 3,
         out_specs=whole(),
+        compiler_params=room(60),
         name="forward_x",
     )(jnp.transpose(receptor_grids, (0, 2, 3, 1)), *(jnp.asarray(m) for m in split_constant(forward_x_matrix(n))))
     components, other = lax.optimization_barrier((components, other))
     blocks = lax.all_to_all(components.reshape(devices, rows, LANES), AXES, 0, 0, tiled=True)
 
     width = 2 * slots * channels * n
+    slabs = max(rotations, VMEM_BYTES // (2 * n * width * 4))
     ligand = pl.pallas_call(
         ligand_kernel,
         grid=(rotations,),
-        out_shape=jax.ShapeDtypeStruct((rotations, 2 * n, width), f32),
+        out_shape=jax.ShapeDtypeStruct((slabs, 2 * n, width), f32),
         in_specs=[scalars()] + [whole()] * 9,
-        out_specs=pl.BlockSpec((1, 2 * n, width), lambda i: (i, 0, 0)),
+        out_specs=far(),
+        scratch_shapes=[pltpu.VMEM((rotations, 2 * n, width), f32), pltpu.SemaphoreType.DMA((rotations,))],
+        compiler_params=room(24),
         name="ligand",
     )(
         place,
@@ -334,9 +358,14 @@
         functools.partial(product_kernel, channels=channels, y_parts=y_parts, z_parts=z_parts),
         grid=(rotations,),
         out_shape=jax.ShapeDtypeStruct((devices, rotations * rows, LANES), f32),
-        in_specs=[scalars(), whole(), pl.BlockSpec((1, 2 * n, width), lambda i: (i, 0, 0))] + [whole()] * 4,
+        in_specs=[scalars(), whole(), far()] + [whole()] * 4,
         out_specs=pl.BlockSpec((devices, rows, LANES), lambda i: (0, i, 0)),
-        scratch_shapes=[pltpu.VMEM((2 * n, channels * (slots + 1) * n), f32)],
+        scratch_shapes=[
+            pltpu.VMEM((2 * n, channels * (slots + 1) * n), f32),
+            pltpu.VMEM((rotations, 2 * n, width), f32),
+            pltpu.SemaphoreType.DMA((rotations,)),
+        ],
+        compiler_params=room(16),
         name="product",
     )(place, blocks, ligand, *matrices)
     got = lax.all_to_all(sent, AXES, 0, 0, tiled=True)
@@ -351,6 +380,7 @@
         in_specs=[pl.BlockSpec((devices, rows, LANES), lambda i: (0, i, 0))] + [whole()] * 2,
         out_specs=[pl.BlockSpec((1, y_block, z_block, n), lambda i: (i, 0, 0, 0)), scalars()],
         scratch_shapes=[pltpu.VMEM((devices * rows, LANES), f32)],
+        compiler_params=room(8),
         name="inverse_x",
     )(got, *(jnp.asarray(m) for m in split_constant(inverse_x_matrix(n))))
     for axis in ("py", "pz"):

time: 111 us -> 104 us (0.937)
  Pallas kernels: 31.3 us -> 26.2 us
    pallas_call x1, Pallas kernels: 8.14 us -> 5.74 us  [on_device(): pl.pallas_call(functools.partial(product_kernel, channels=channels, y_par...]
    pallas_call x1, Pallas kernels: 4.72 us -> 3.32 us  [on_device(): pl.pallas_call(inverse_x_kernel, grid=(rotations,), out_shape=[jax.ShapeD...]
    pallas_call x1, Pallas kernels: 15.9 us -> 14.6 us  [on_device(): pl.pallas_call(ligand_kernel, grid=(rotations,), out_shape=jax.ShapeDtype...]
where the time goes in v3:
time: 104 us
  blocking collectives  53 us (51%)
  Pallas kernels  26.2 us (25%)
  starting transfers between devices  15 us (14%)
  waiting for transfers between devices  8.09 us (8%)
    all_to_all x1, blocking collectives, on_device(): got = lax.all_to_all(sent, AXES, 0, 0, tiled=True)  53 us
    pallas_call x1, Pallas kernels, on_device(): pl.pallas_call(ligand_kernel, grid=(rotations,), out_shape=jax.ShapeDtype...  14.6 us
    ppermute x4, waiting for transfers between devices, on_device(): lax.ppermute(best, axis, [(i, i ^ step) for i in range(sizes[axis])])  8.09 us
    ppermute x4, starting transfers between devices, on_device(): lax.ppermute(best, axis, [(i, i ^ step) for i in range(sizes[axis])])  6.02 us
    all_to_all x1, starting transfers between devices, on_device(): lax.all_to_all(components.reshape(devices, rows, LANES), AXES, 0, 0, tile...  5.93 us
    pallas_call x1, Pallas kernels, on_device(): pl.pallas_call(functools.partial(product_kernel, channels=channels, y_par...  5.74 us
    pallas_call x1, Pallas kernels, on_device(): pl.pallas_call(inverse_x_kernel, grid=(rotations,), out_shape=[jax.ShapeD...  3.32 us
    ppermute x1, starting transfers between devices, on_device(): other = lax.ppermute(ligand_cells, 'rot', [(i, i ^ 1) for i in range(rots)])  3.06 us
  transfers between devices with their start and end apart: 6, of which 4 were waited for; matrix products, arithmetic and copies ran while one was open for 0% of the time, Pallas kernels for 17%

profile of v3, /device:TPU:0, one launch (start us, length us, event | category | flops | bytes accessed | tf_op | source)
XLA Modules:
  0.0 103.8 jit_solution(16943265501482098149)
XLA Ops:
  0.6 0.0 copy-start
  0.6 0.0 copy-start.1
  0.7 0.0 copy-start.2
  0.7 0.0 copy-start.3
  0.7 0.0 copy-start.4
  0.7 0.0 copy-start.5
  0.7 0.0 copy-start.9
  0.7 0.0 copy-start.8
  0.7 3.1 %collective-permute-start = (s32[4,2048]{1,0:T(4,128)}, s32[4,2048]{1,0:T(4,128)S(1)}, u32[]{:S(2)}, u32[]{:S(2)}) collective-permute-start(s32[4,2048]{1,0:T(4,128)} %own_ref.1), channel_id=1, source_target_pairs={{0,16},{16,0},{1,17},{17,1},{2,18},{18,2},{3,19},{19,3},{4,20},{20... | collective-permute-start | bytes 98312 | tf_op jit(solution)/shard_map/ppermute | solution.py:323
  3.8 2.5 %forward_x.1 = f32[1024,128]{1,0:T(8,128)} custom-call(f32[1,32,32,128]{3,2,1,0:T(8,128)} %bitcast.8, bf16[128,128]{1,0:T(8,128)(2,1)} %constant.39.clone.head_ref, bf16[128,128]{1,0:T(8,128)(2,1)} %constant.40.clone.rest_ref), custom_call_target="tpu_custom_call" | custom-call | tf_op jit(solution)/shard_map/forward_x/pallas_call | solution.py:325
  6.3 0.0 collective-permute-done.other_ref
  6.3 5.9 %all-to-all-start = ((f32[32,32,128]{2,1,0:T(8,128)}), f32[32,32,128]{2,1,0:T(8,128)S(1)}, u32[]{:S(2)}, u32[]{:S(2)}) async-start(f32[32,32,128]{2,1,0:T(8,128)} %bitcast.7), calls=%async_computation | async-start | bytes 1048576 | tf_op jit(solution)/shard_map/all_to_all | solution.py:334
  12.3 0.0 copy-done
  12.3 0.0 copy-done.1
  12.3 0.0 copy-done.2
  12.3 14.6 %ligand.1.far_ref = f32[48,256,1024]{2,1,0:T(8,128)} custom-call(s32[1]{0:T(128)} %bitcast.place_ref, s32[4,2048]{1,0:T(4,128)S(1)} %copy-done.5, s32[4,2048]{1,0:T(4,128)S(1)} %collective-permute-done.other_ref, f32[1,2048]{1,0:T(1,128)S(1)} %bitcast.5, f32[1,2048]{1,0:T(1,128)S(1)} %bitcast.6, bf16[32,16,128]{2,1,0:T(8,128)(2,1)S(1)} %copy-done.4, ...), custom_call_target="tpu_custom_call" | custom-call | tf_op jit(solution)/shard_map/ligand/pallas_call | solution.py:338
  27.0 0.0 all-to-all-done.blocks_ref
  27.0 5.7 %product.1 = f32[32,128,128]{2,1,0:T(8,128)S(1)} custom-call(s32[1]{0:T(128)} %bitcast.place_ref, f32[32,32,128]{2,1,0:T(8,128)S(1)} %all-to-all-done.blocks_ref, f32[48,256,1024]{2,1,0:T(8,128)} %ligand.1.far_ref, bf16[256,256]{1,0:T(8,128)(2,1)S(1)} %copy-done.3, bf16[256,256]{1,0:T(8,128)(2,1)S(1)} %copy-done.2, bf16[256,256]{1,0:T(8,128)(2,1)S(1)} %copy-done.1, ...), custom_call_target="tpu_custom_call" | custom-call | tf_op jit(solution)/shard_map/product/pallas_call | solution.py:357
  32.7 0.0 copy-start.6
  32.8 0.0 copy-start.7
  32.8 53.0 %all_to_all.10.blocks_ref = f32[32,128,128]{2,1,0:T(8,128)S(1)} all-to-all(f32[32,128,128]{2,1,0:T(8,128)S(1)} %product.1), channel_id=1, replica_groups=mesh['rot'=2,'py'=4,'pz'=4] {'rot','py','pz'}, dimensions={0} | all-to-all | bytes 4194304 | tf_op jit(solution)/shard_map/all_to_all | solution.py:371
  85.8 0.0 copy-done.7
  85.8 3.3 %inverse_x.1 = (f32[4,32,32,128]{3,2,1,0:T(8,128)}, f32[4]{0:T(128)S(1)}) custom-call(f32[32,128,128]{2,1,0:T(8,128)S(1)} %all_to_all.10.blocks_ref, bf16[128,128]{1,0:T(8,128)(2,1)S(1)} %copy-done.7, bf16[128,128]{1,0:T(8,128)(2,1)S(1)} %copy-done.6), custom_call_target="tpu_custom_call" | custom-call | tf_op jit(solution)/shard_map/inverse_x/pallas_call | solution.py:373
  89.1 1.7 %collective-permute-start.1 = (f32[4]{0:T(128)S(1)}, f32[4]{0:T(128)S(1)}, u32[]{:S(2)}, u32[]{:S(2)}) collective-permute-start(f32[4]{0:T(128)S(1)} %get-tuple-element.9), channel_id=1, source_target_pairs={{0,4},{4,0},{8,12},{12,8},{1,5},{5,1},{9,13},{13,9},{2,6},{6,2},{1... | collective-permute-start | bytes 56 | tf_op jit(solution)/shard_map/ppermute | solution.py:389
  90.8 0.8 collective-permute-done.1
  91.6 1.5 %collective-permute-start.2 = (f32[4]{0:T(128)S(1)}, f32[4]{0:T(128)S(1)}, u32[]{:S(2)}, u32[]{:S(2)}) collective-permute-start(f32[4]{0:T(128)S(1)} %max.12), channel_id=1, source_target_pairs={{0,8},{4,12},{8,0},{12,4},{1,9},{5,13},{9,1},{13,5},{2,10},{6,14},... | collective-permute-start | bytes 56 | tf_op jit(solution)/shard_map/ppermute | solution.py:389
  93.1 2.1 %collective-permute-done.2 = f32[4]{0:T(128)S(1)} collective-permute-done((f32[4]{0:T(128)S(1)}, f32[4]{0:T(128)S(1)}, u32[]{:S(2)}, u32[]{:S(2)}) %collective-permute-start.2) | collective-permute-done | bytes 48 | tf_op jit(solution)/shard_map/ppermute | solution.py:389
  95.2 1.8 %collective-permute-start.3 = (f32[4]{0:T(128)S(1)}, f32[4]{0:T(128)S(1)}, u32[]{:S(2)}, u32[]{:S(2)}) collective-permute-start(f32[4]{0:T(128)S(1)} %max.13), channel_id=1, source_target_pairs={{0,1},{1,0},{2,3},{3,2},{4,5},{5,4},{6,7},{7,6},{8,9},{9,8},{10,11... | collective-permute-start | bytes 56 | tf_op jit(solution)/shard_map/ppermute | solution.py:389
  97.0 1.8 %collective-permute-done.3 = f32[4]{0:T(128)S(1)} collective-permute-done((f32[4]{0:T(128)S(1)}, f32[4]{0:T(128)S(1)}, u32[]{:S(2)}, u32[]{:S(2)}) %collective-permute-start.3) | collective-permute-done | bytes 48 | tf_op jit(solution)/shard_map/ppermute | solution.py:389
  98.8 1.1 %collective-permute-start.4 = (f32[4]{0:T(128)S(1)}, f32[4]{0:T(128)S(1)}, u32[]{:S(2)}, u32[]{:S(2)}) collective-permute-start(f32[4]{0:T(128)S(1)} %max.14), channel_id=1, source_target_pairs={{0,2},{1,3},{2,0},{3,1},{4,6},{5,7},{6,4},{7,5},{8,10},{9,11},{10,... | collective-permute-start | bytes 56 | tf_op jit(solution)/shard_map/ppermute | solution.py:389
  99.8 3.4 %collective-permute-done.4 = f32[4]{0:T(128)S(1)} collective-permute-done((f32[4]{0:T(128)S(1)}, f32[4]{0:T(128)S(1)}, u32[]{:S(2)}, u32[]{:S(2)}) %collective-permute-start.4) | collective-permute-done | bytes 48 | tf_op jit(solution)/shard_map/ppermute | solution.py:389
  103.2 0.5 max.15
  (9 shorter events, 0.0 us)
Async XLA Ops:
  0.6 11.6 %copy-start = (bf16[256,256]{1,0:T(8,128)(2,1)S(1)}, bf16[256,256]{1,0:T(8,128)(2,1)}, u32[]{:S(2)}) copy-start(bf16[256,256]{1,0:T(8,128)(2,1)} %constant.38.clone.yr) | copy-start | bytes 393220
  0.6 11.6 %copy-start.1 = (bf16[256,256]{1,0:T(8,128)(2,1)S(1)}, bf16[256,256]{1,0:T(8,128)(2,1)}, u32[]{:S(2)}) copy-start(bf16[256,256]{1,0:T(8,128)(2,1)} %constant.37.clone.yh) | copy-start | bytes 393220
  0.7 11.6 %copy-start.2 = (bf16[256,256]{1,0:T(8,128)(2,1)S(1)}, bf16[256,256]{1,0:T(8,128)(2,1)}, u32[]{:S(2)}) copy-start(bf16[256,256]{1,0:T(8,128)(2,1)} %constant.36.clone.zr) | copy-start | bytes 393220
  0.7 11.6 %copy-start.3 = (bf16[256,256]{1,0:T(8,128)(2,1)S(1)}, bf16[256,256]{1,0:T(8,128)(2,1)}, u32[]{:S(2)}) copy-start(bf16[256,256]{1,0:T(8,128)(2,1)} %constant.35.clone.zh) | copy-start | bytes 393220
  0.7 11.6 %copy-start.4 = (bf16[32,16,128]{2,1,0:T(8,128)(2,1)S(1)}, bf16[32,16,128]{2,1,0:T(8,128)(2,1)}, u32[]{:S(2)}) copy-start(bf16[32,16,128]{2,1,0:T(8,128)(2,1)} %constant.41.clone.table_ref) | copy-start | bytes 393220
  0.7 11.6 %copy-start.5 = (s32[4,2048]{1,0:T(4,128)S(1)}, s32[4,2048]{1,0:T(4,128)}, u32[]{:S(2)}) copy-start(s32[4,2048]{1,0:T(4,128)} %own_ref.1) | copy-start | bytes 98308
  0.7 11.6 %copy-start.9 = (f32[2048]{0:T(1024)S(1)}, f32[2048]{0:T(1024)}, u32[]{:S(2)}) copy-start(f32[2048]{0:T(1024)} %param.16) | copy-start | bytes 24580
  0.7 11.6 %copy-start.8 = (f32[2048]{0:T(1024)S(1)}, f32[2048]{0:T(1024)}, u32[]{:S(2)}) copy-start(f32[2048]{0:T(1024)} %param.15) | copy-start | bytes 24580
  0.7 5.6 %collective-permute-start = (s32[4,2048]{1,0:T(4,128)}, s32[4,2048]{1,0:T(4,128)S(1)}, u32[]{:S(2)}, u32[]{:S(2)}) collective-permute-start(s32[4,2048]{1,0:T(4,128)} %own_ref.1), channel_id=1, source_target_pairs={{0,16},{16,0},{1,17},{17,1},{2,18},{18,2},{3,19},{19,3},{4,20},{20... | collective-permute-start | bytes 98312 | tf_op jit(solution)/shard_map/ppermute | solution.py:323
  6.3 20.7 %all-to-all-start = ((f32[32,32,128]{2,1,0:T(8,128)}), f32[32,32,128]{2,1,0:T(8,128)S(1)}, u32[]{:S(2)}, u32[]{:S(2)}) async-start(f32[32,32,128]{2,1,0:T(8,128)} %bitcast.7), calls=%async_computation | async-start | bytes 1048576 | tf_op jit(solution)/shard_map/all_to_all | solution.py:334
  32.7 53.1 %copy-start.6 = (bf16[128,128]{1,0:T(8,128)(2,1)S(1)}, bf16[128,128]{1,0:T(8,128)(2,1)}, u32[]{:S(2)}) copy-start(bf16[128,128]{1,0:T(8,128)(2,1)} %constant.43.clone.rest_ref) | copy-start | bytes 98308
  32.8 53.1 %copy-start.7 = (bf16[128,128]{1,0:T(8,128)(2,1)S(1)}, bf16[128,128]{1,0:T(8,128)(2,1)}, u32[]{:S(2)}) copy-start(bf16[128,128]{1,0:T(8,128)(2,1)} %constant.42.clone.head_ref) | copy-start | bytes 98308
  89.1 2.5 %collective-permute-start.1 = (f32[4]{0:T(128)S(1)}, f32[4]{0:T(128)S(1)}, u32[]{:S(2)}, u32[]{:S(2)}) collective-permute-start(f32[4]{0:T(128)S(1)} %get-tuple-element.9), channel_id=1, source_target_pairs={{0,4},{4,0},{8,12},{12,8},{1,5},{5,1},{9,13},{13,9},{2,6},{6,2},{1... | collective-permute-start | bytes 56 | tf_op jit(solution)/shard_map/ppermute | solution.py:389
  91.6 3.6 %collective-permute-start.2 = (f32[4]{0:T(128)S(1)}, f32[4]{0:T(128)S(1)}, u32[]{:S(2)}, u32[]{:S(2)}) collective-permute-start(f32[4]{0:T(128)S(1)} %max.12), channel_id=1, source_target_pairs={{0,8},{4,12},{8,0},{12,4},{1,9},{5,13},{9,1},{13,5},{2,10},{6,14},... | collective-permute-start | bytes 56 | tf_op jit(solution)/shard_map/ppermute | solution.py:389
  95.2 3.6 %collective-permute-start.3 = (f32[4]{0:T(128)S(1)}, f32[4]{0:T(128)S(1)}, u32[]{:S(2)}, u32[]{:S(2)}) collective-permute-start(f32[4]{0:T(128)S(1)} %max.13), channel_id=1, source_target_pairs={{0,1},{1,0},{2,3},{3,2},{4,5},{5,4},{6,7},{7,6},{8,9},{9,8},{10,11... | collective-permute-start | bytes 56 | tf_op jit(solution)/shard_map/ppermute | solution.py:389
  98.8 4.5 %collective-permute-start.4 = (f32[4]{0:T(128)S(1)}, f32[4]{0:T(128)S(1)}, u32[]{:S(2)}, u32[]{:S(2)}) collective-permute-start(f32[4]{0:T(128)S(1)} %max.14), channel_id=1, source_target_pairs={{0,2},{1,3},{2,0},{3,1},{4,6},{5,7},{6,4},{7,5},{8,10},{9,11},{10,... | collective-permute-start | bytes 56 | tf_op jit(solution)/shard_map/ppermute | solution.py:389

commit v4 on v3

--- a/solution.py
+++ b/solution.py
@@ -121,10 +121,10 @@
             jnp.concatenate([rows[j * n : (j + 1) * n, :n], rows[j * n : (j + 1) * n, n:]], axis=0)
             for j in range(len(pairs))
         ]
-    return jnp.concatenate(constant_times(yh, yr, columns), axis=1)
-
-
-def ligand_kernel(place_ref, own_ref, other_ref, shape_ref, charge_ref, table_ref, zh, zr, yh, yr, out_ref, held_ref, sems):
+    return constant_times(yh, yr, columns)
+
+
+def ligand_kernel(place_ref, own_ref, other_ref, shape_ref, charge_ref, table_ref, zh, zr, yh, yr, far_ref, near_ref, held_ref, sems):
     n = zh.shape[0] // 2
     half = n // 2
     atoms = own_ref.shape[1]
@@ -171,13 +171,18 @@
             )
         planes[0].append(first)
         planes[1].append(second)
-    held_ref[step] = spectrum(planes[0] + planes[1], n, zh, zr, yh, yr)
-    pltpu.make_async_copy(held_ref.at[step], out_ref.at[step], sems.at[step]).start()
-
-    @pl.when(step == pl.num_programs(0) - 1)
+    near_ref[...] = jnp.concatenate(spectrum(planes[0] + planes[1], n, zh, zr, yh, yr), axis=1)
+    last = pl.num_programs(0) - 1
+
+    @pl.when(step < last)
+    def _():
+        held_ref[step] = near_ref[...]
+        pltpu.make_async_copy(held_ref.at[step], far_ref.at[step], sems.at[step]).start()
+
+    @pl.when(step == last)
     def _():
         for i in range(held_ref.shape[0]):
-            pltpu.make_async_copy(held_ref.at[i], out_ref.at[i], sems.at[i]).wait()
+            pltpu.make_async_copy(held_ref.at[i], far_ref.at[i], sems.at[i]).wait()
 
 
 def receptor_spectrum(special, blocks_ref, zh, zr, yh, yr, channels, y_parts, z_parts):
@@ -204,75 +209,62 @@
 
 
 def product_kernel(
-    place_ref, blocks_ref, far_ref, zh, zr, yh, yr, out_ref, receptor_ref, ligand_ref, sems, *, channels, y_parts, z_parts
+    place_ref, blocks_ref, far_ref, near_ref, zh, zr, yh, yr, out_ref, ligand_ref, sems, *, channels, y_parts, z_parts
 ):
     n = zh.shape[0] // 2
     width = n // z_parts
     groups = LANES // width
-    slots = ligand_ref.shape[2] // (2 * channels * n)
+    slots = near_ref.shape[1] // (2 * channels * n)
+    last = ligand_ref.shape[0]
     special = place_ref[0] == 0
-    step = pl.program_id(0)
-
-    @pl.when(step == 0)
-    def _():
-        for i in range(ligand_ref.shape[0]):
-            pltpu.make_async_copy(far_ref.at[i], ligand_ref.at[i], sems.at[i]).start()
-        receptor_ref[...] = receptor_spectrum(
-            special, blocks_ref, zh, zr, yh, yr, channels, y_parts, z_parts
-        )
-
-    pltpu.make_async_copy(far_ref.at[step], ligand_ref.at[step], sems.at[step]).wait()
-
-    def receptor(channel, slot, rotation):
-        at = channel * (slots + 1) + (rotation if slot == 0 else slot + 1)
-        return receptor_ref[:n, at * n : (at + 1) * n], receptor_ref[n:, at * n : (at + 1) * n]
-
-    def ligand(channel, slot, rotation):
-        at = (rotation * channels + channel) * slots + slot
-        return ligand_ref[step, :n, at * n : (at + 1) * n], ligand_ref[step, n:, at * n : (at + 1) * n]
-
-    columns = []
-    for rotation in range(2):
-        for slot in range(slots):
-            real, imag = 0.0, 0.0
-            for channel in range(channels):
-                fr, fi = receptor(channel, slot, rotation)
-                hr, hi = ligand(channel, slot, rotation)
-                real = real + (fr * hr + fi * hi)
-                imag = imag + (fr * hi - fi * hr)
-            columns.append(jnp.concatenate([real, imag], axis=0))
-    columns = constant_times(yh, yr, columns)
-    rows = jnp.concatenate([jnp.concatenate([c[:n], c[n:]], axis=1) for c in columns], axis=0)
-    rows = times_constant(rows, zh, zr)
-    maps = [
-        [
-            [rows[(rotation * slots + slot) * n : (rotation * slots + slot + 1) * n, p * n : (p + 1) * n] for p in range(2)]
-            for slot in range(slots)
-        ]
-        for rotation in range(2)
-    ]
-    lone, other = maps[0][0][1], maps[1][0][0]
-    maps[0][0][1] = jnp.where(special, other, lone)
-    maps[1][0][0] = jnp.where(special, lone, other)
-    for rotation in range(2):
-        for slot in range(slots):
-            for p in range(2):
-                plane = maps[rotation][slot][p]
-                row = (slot * 2 + p) * SUBLANES
-                for y_part in range(y_parts):
-                    pieces = [
-                        plane[(y_part * groups + g) * SUBLANES : (y_part * groups + g + 1) * SUBLANES, :]
-                        for g in range(groups)
-                    ]
-                    for z_part, block in enumerate(swap_groups(pieces, width)):
-                        out_ref[(rotation * y_parts + y_part) * z_parts + z_part, row : row + SUBLANES, :] = block
+    copies = [pltpu.make_async_copy(far_ref.at[i], ligand_ref.at[i], sems.at[i]) for i in range(last)]
+    for copy in copies:
+        copy.start()
+    receptor = receptor_spectrum(special, blocks_ref, zh, zr, yh, yr, channels, y_parts, z_parts)
+    for copy in copies:
+        copy.wait()
+
+    for step in range(last + 1):
+        ligand = near_ref if step == last else ligand_ref.at[step]
+        columns = []
+        for rotation in range(2):
+            for slot in range(slots):
+                real, imag = 0.0, 0.0
+                for channel in range(channels):
+                    f = receptor[channel * (slots + 1) + (rotation if slot == 0 else slot + 1)]
+                    at = ((rotation * channels + channel) * slots + slot) * n
+                    fr, fi = f[:n], f[n:]
+                    hr, hi = ligand[:n, at : at + n], ligand[n:, at : at + n]
+                    real = real + (fr * hr + fi * hi)
+                    imag = imag + (fr * hi - fi * hr)
+                columns.append(jnp.concatenate([real, imag], axis=0))
+        columns = constant_times(yh, yr, columns)
+        rows = jnp.concatenate([jnp.concatenate([c[:n], c[n:]], axis=1) for c in columns], axis=0)
+        rows = times_constant(rows, zh, zr)
+        maps = []
+        for i in range(2 * slots):
+            both = rows[i * n : (i + 1) * n]
+            maps += [both[:, :n], both[:, n:]]
+        lone, other = maps[1], maps[2 * slots]
+        maps[1], maps[2 * slots] = jnp.where(special, other, lone), jnp.where(special, lone, other)
+        for i, plane in enumerate(maps):
+            rotation, component = divmod(i, 2 * slots)
+            row = (step * 2 * slots + component) * SUBLANES
+            for y_part in range(y_parts):
+                first = y_part * groups
+                pieces = [plane[(first + g) * SUBLANES : (first + g + 1) * SUBLANES] for g in range(groups)]
+                for z_part, block in enumerate(swap_groups(pieces, width)):
+                    out_ref[(rotation * y_parts + y_part) * z_parts + z_part, row : row + SUBLANES] = block
 
 
 def inverse_x_kernel(blocks_ref, head_ref, rest_ref, out_ref, best_ref, rows_ref):
     n = head_ref.shape[0]
-    y_block, z_block = out_ref.shape[1:3]
+    _, z_block = out_ref.shape[1:3]
     groups = LANES // z_block
-    rows_ref[...] = blocks_ref[...].reshape(rows_ref.shape)
+    step = pl.program_id(0)
+    count = rows_ref.shape[0] // blocks_ref.shape[0]
+    first = pl.multiple_of(step * count, SUBLANES)
+    rows_ref[...] = blocks_ref[:, pl.ds(first, count), :].reshape(rows_ref.shape)
     best = None
     for row in range(SUBLANES):
         values = rows_ref[pl.ds(row, n, stride=SUBLANES), :]
@@ -280,7 +272,7 @@
         for g in range(groups):
             out_ref[0, g * SUBLANES + row] = result[g * z_block : (g + 1) * z_block, :]
         best = result if best is None else jnp.maximum(best, result)
-    best_ref[pl.program_id(0)] = jnp.max(best)
+    best_ref[step] = jnp.max(best)
 
 
 def whole():
@@ -320,7 +312,6 @@
     matrices = split_constant(plus_matrix(n))
     matrices = [jnp.asarray(m) for m in (*matrices, *(np.ascontiguousarray(m.T) for m in matrices))]
     place = lax.axis_index(AXES).reshape(1)
-    other = lax.ppermute(ligand_cells, "rot", [(i, i ^ 1) for i in range(rots)])
 
     components = pl.pallas_call(
         forward_x_kernel,
@@ -330,18 +321,22 @@
         compiler_params=room(60),
         name="forward_x",
     )(jnp.transpose(receptor_grids, (0, 2, 3, 1)), *(jnp.asarray(m) for m in split_constant(forward_x_matrix(n))))
-    components, other = lax.optimization_barrier((components, other))
+    components, cells = lax.optimization_barrier((components, ligand_cells))
+    other = lax.ppermute(cells, "rot", [(i, i ^ 1) for i in range(rots)])
     blocks = lax.all_to_all(components.reshape(devices, rows, LANES), AXES, 0, 0, tiled=True)
 
     width = 2 * slots * channels * n
     slabs = max(rotations, VMEM_BYTES // (2 * n * width * 4))
-    ligand = pl.pallas_call(
+    far_ligand, near_ligand = pl.pallas_call(
         ligand_kernel,
         grid=(rotations,),
-        out_shape=jax.ShapeDtypeStruct((slabs, 2 * n, width), f32),
+        out_shape=[
+            jax.ShapeDtypeStruct((slabs, 2 * n, width), f32),
+            jax.ShapeDtypeStruct((2 * n, width), f32),
+        ],
         in_specs=[scalars()] + [whole()] * 9,
-        out_specs=far(),
-        scratch_shapes=[pltpu.VMEM((rotations, 2 * n, width), f32), pltpu.SemaphoreType.DMA((rotations,))],
+        out_specs=[far(), whole()],
+        scratch_shapes=[pltpu.VMEM((rotations - 1, 2 * n, width), f32), pltpu.SemaphoreType.DMA((rotations - 1,))],
         compiler_params=room(24),
         name="ligand",
     )(
@@ -356,18 +351,13 @@
 
     sent = pl.pallas_call(
         functools.partial(product_kernel, channels=channels, y_parts=y_parts, z_parts=z_parts),
-        grid=(rotations,),
         out_shape=jax.ShapeDtypeStruct((devices, rotations * rows, LANES), f32),
-        in_specs=[scalars(), whole(), far()] + [whole()] * 4,
-        out_specs=pl.BlockSpec((devices, rows, LANES), lambda i: (0, i, 0)),
-        scratch_shapes=[
-            pltpu.VMEM((2 * n, channels * (slots + 1) * n), f32),
-            pltpu.VMEM((rotations, 2 * n, width), f32),
-            pltpu.SemaphoreType.DMA((rotations,)),
-        ],
+        in_specs=[scalars(), whole(), far()] + [whole()] * 5,
+        out_specs=whole(),
+        scratch_shapes=[pltpu.VMEM((rotations - 1, 2 * n, width), f32), pltpu.SemaphoreType.DMA((rotations - 1,))],
         compiler_params=room(16),
         name="product",
-    )(place, blocks, ligand, *matrices)
+    )(place, blocks, far_ligand, near_ligand, *matrices)
     got = lax.all_to_all(sent, AXES, 0, 0, tiled=True)
 
     correlation, best = pl.pallas_call(
@@ -377,7 +367,7 @@
             jax.ShapeDtypeStruct((rotations, y_block, z_block, n), f32),
             jax.ShapeDtypeStruct((rotations,), f32),
         ],
-        in_specs=[pl.BlockSpec((devices, rows, LANES), lambda i: (0, i, 0))] + [whole()] * 2,
+        in_specs=[whole()] * 3,
         out_specs=[pl.BlockSpec((1, y_block, z_block, n), lambda i: (i, 0, 0, 0)), scalars()],
         scratch_shapes=[pltpu.VMEM((devices * rows, LANES), f32)],
         compiler_params=room(8),
@@ -471,6 +461,7 @@
 
 def solution(mesh):
     sizes = dict(mesh.shape)
+    placed = (P("rot", None, "py", "pz"), P("rot", None), P(), P())
 
     def run(receptor_grids, ligand_cells, atom_shape, atom_charges):
         n = receptor_grids.shape[1]
@@ -482,14 +473,13 @@
             and (n // sizes["py"]) * (n // sizes["pz"]) == SUBLANES * LANES
             and all(sizes[a] & (sizes[a] - 1) == 0 for a in AXES)
         )
-        body = functools.partial(on_device if fits else on_any_device, sizes=sizes)
-        placed = (P("rot", None, "py", "pz"), P("rot", None), P(), P())
-        return jax.shard_map(
-            body,
+        step = jax.shard_map(
+            functools.partial(on_device if fits else on_any_device, sizes=sizes),
             mesh=mesh,
             in_specs=placed,
             out_specs=(P("rot", "py", "pz", None), P("rot")),
             check_vma=False,
-        )(receptor_grids, ligand_cells, atom_shape, atom_charges)
+        )
+        return step(receptor_grids, ligand_cells, atom_shape, atom_charges)
 
     return run

time: 104 us -> 106 us (1.019)
  waiting for transfers between devices: 8.09 us -> 12.4 us
  Pallas kernels: 26.2 us -> 24.3 us
    ppermute x1, waiting for transfers between devices: 0.01 us -> 4.33 us  [on_device(): other = lax.ppermute(cells, 'rot', [(i, i ^ 1) for i in range(rots)])]
    all_to_all x1, starting transfers between devices: 5.93 us -> 7.32 us  [on_device(): lax.all_to_all(components.reshape(devices, rows, LANES), AXES, 0, 0, tile...]
    ppermute x1, starting transfers between devices: 3.06 us -> 1.83 us  [on_device(): other = lax.ppermute(cells, 'rot', [(i, i ^ 1) for i in range(rots)])]
  transfers between devices with their start and end apart: 6 -> 6, of which waited for: 4 -> 5; matrix products, arithmetic and copies ran while one was open for 0% -> 0% of each run, Pallas kernels for 17% -> 13%
where the time goes in v4:
time: 106 us
  blocking collectives  52.6 us (50%)
  Pallas kernels  24.3 us (23%)
  starting transfers between devices  15.2 us (14%)
  waiting for transfers between devices  12.4 us (12%)
    all_to_all x1, blocking collectives, on_device(): got = lax.all_to_all(sent, AXES, 0, 0, tiled=True)  52.6 us
    pallas_call x1, Pallas kernels, on_device(): pl.pallas_call(ligand_kernel, grid=(rotations,), out_shape=[jax.ShapeDtyp...  13.8 us
    ppermute x4, waiting for transfers between devices, on_device(): lax.ppermute(best, axis, [(i, i ^ step) for i in range(sizes[axis])])  8.08 us
    all_to_all x1, starting transfers between devices, on_device(): lax.all_to_all(components.reshape(devices, rows, LANES), AXES, 0, 0, tile...  7.32 us
    ppermute x4, starting transfers between devices, on_device(): lax.ppermute(best, axis, [(i, i ^ step) for i in range(sizes[axis])])  6.02 us
    pallas_call x1, Pallas kernels, on_device(): pl.pallas_call(functools.partial(product_kernel, channels=channels, y_par...  4.72 us
    ppermute x1, waiting for transfers between devices, on_device(): other = lax.ppermute(cells, 'rot', [(i, i ^ 1) for i in range(rots)])  4.33 us
    pallas_call x1, Pallas kernels, on_device(): pl.pallas_call(inverse_x_kernel, grid=(rotations,), out_shape=[jax.ShapeD...  3.17 us
  transfers between devices with their start and end apart: 6, of which 5 were waited for; matrix products, arithmetic and copies ran while one was open for 0% of the time, Pallas kernels for 13%

profile of v4, /device:TPU:0, one launch (start us, length us, event | category | flops | bytes accessed | tf_op | source)
XLA Modules:
  0.0 105.9 jit_solution(16827431130340952065)
XLA Ops:
  0.6 0.0 copy-start
  0.6 0.0 copy-start.1
  0.7 0.0 copy-start.2
  0.7 0.0 copy-start.3
  0.7 0.0 copy-start.4
  0.7 0.0 copy-start.7
  0.7 0.0 copy-start.9
  0.7 0.0 copy-start.8
  0.7 2.6 %forward_x.1 = f32[1024,128]{1,0:T(8,128)} custom-call(f32[1,32,32,128]{3,2,1,0:T(8,128)} %bitcast.8, bf16[128,128]{1,0:T(8,128)(2,1)} %constant.39.clone.head_ref, bf16[128,128]{1,0:T(8,128)(2,1)} %constant.40.clone.rest_ref), custom_call_target="tpu_custom_call" | custom-call | tf_op jit(solution)/shard_map/forward_x/pallas_call | solution.py:316
  3.4 7.3 %all-to-all-start = ((f32[32,32,128]{2,1,0:T(8,128)}), f32[32,32,128]{2,1,0:T(8,128)S(1)}, u32[]{:S(2)}, u32[]{:S(2)}) async-start(f32[32,32,128]{2,1,0:T(8,128)} %bitcast.7), calls=%async_computation | async-start | bytes 1048576 | tf_op jit(solution)/shard_map/all_to_all | solution.py:326
  10.7 0.0 copy-done.7
  10.7 1.8 %collective-permute-start = (s32[4,2048]{1,0:T(4,128)S(1)}, s32[4,2048]{1,0:T(4,128)S(1)}, u32[]{:S(2)}, u32[]{:S(2)}) collective-permute-start(s32[4,2048]{1,0:T(4,128)S(1)} %copy-done.7), channel_id=1, source_target_pairs={{0,16},{16,0},{1,17},{17,1},{2,18},{18,2},{3,19},{19,3},{4,20},{20... | collective-permute-start | bytes 98312 | tf_op jit(solution)/shard_map/ppermute | solution.py:325
  12.5 4.3 %collective-permute-done.other_ref = s32[4,2048]{1,0:T(4,128)S(1)} collective-permute-done((s32[4,2048]{1,0:T(4,128)S(1)}, s32[4,2048]{1,0:T(4,128)S(1)}, u32[]{:S(2)}, u32[]{:S(2)}) %collective-permute-start) | collective-permute-done | bytes 32800 | tf_op jit(solution)/shard_map/ppermute | solution.py:325
  16.9 0.0 copy-done
  16.9 0.0 copy-done.1
  16.9 13.8 %ligand.1 = (f32[48,256,1024]{2,1,0:T(8,128)}, f32[256,1024]{1,0:T(8,128)S(1)}) custom-call(s32[1]{0:T(128)} %bitcast.place_ref, s32[4,2048]{1,0:T(4,128)S(1)} %copy-done.7, s32[4,2048]{1,0:T(4,128)S(1)} %collective-permute-done.other_ref, f32[1,2048]{1,0:T(1,128)S(1)} %bitcast.5, f32[1,2048]{1,0:T(1,128)S(1)} %bitcast.6, ...), custom_call_target="tpu_custom_call" | custom-call | tf_op jit(solution)/shard_map/ligand/pallas_call | solution.py:330
  30.7 0.0 all-to-all-done.blocks_ref
  30.7 4.7 %product.1 = f32[32,128,128]{2,1,0:T(8,128)S(1)} custom-call(s32[1]{0:T(128)} %bitcast.place_ref, f32[32,32,128]{2,1,0:T(8,128)S(1)} %all-to-all-done.blocks_ref, f32[48,256,1024]{2,1,0:T(8,128)} %get-tuple-element.10.far_ref, f32[256,1024]{1,0:T(8,128)S(1)} %get-tuple-element.11.near_ref, bf16[256,256]{1,0:T(8,128)(2,1)S(1)} %copy-done.3, ...), custom_call_target="tpu_custom_call" | custom-call | tf_op jit(solution)/shard_map/product/pallas_call | solution.py:352
  35.4 0.0 copy-start.5
  35.5 0.0 copy-start.6
  35.5 52.6 %all_to_all.10.blocks_ref = f32[32,128,128]{2,1,0:T(8,128)S(1)} all-to-all(f32[32,128,128]{2,1,0:T(8,128)S(1)} %product.1), channel_id=1, replica_groups=mesh['rot'=2,'py'=4,'pz'=4] {'rot','py','pz'}, dimensions={0} | all-to-all | bytes 4194304 | tf_op jit(solution)/shard_map/all_to_all | solution.py:361
  88.1 0.0 copy-done.5
  88.1 3.2 %inverse_x.1 = (f32[4,32,32,128]{3,2,1,0:T(8,128)}, f32[4]{0:T(128)S(1)}) custom-call(f32[32,128,128]{2,1,0:T(8,128)S(1)} %all_to_all.10.blocks_ref, bf16[128,128]{1,0:T(8,128)(2,1)S(1)} %copy-done.6, bf16[128,128]{1,0:T(8,128)(2,1)S(1)} %copy-done.5), custom_call_target="tpu_custom_call" | custom-call | tf_op jit(solution)/shard_map/inverse_x/pallas_call | solution.py:363
  91.3 1.7 %collective-permute-start.1 = (f32[4]{0:T(128)S(1)}, f32[4]{0:T(128)S(1)}, u32[]{:S(2)}, u32[]{:S(2)}) collective-permute-start(f32[4]{0:T(128)S(1)} %get-tuple-element.13), channel_id=1, source_target_pairs={{0,4},{4,0},{8,12},{12,8},{1,5},{5,1},{9,13},{13,9},{2,6},{6,2},{1... | collective-permute-start | bytes 56 | tf_op jit(solution)/shard_map/ppermute | solution.py:379
  93.0 0.8 collective-permute-done.1
  93.8 1.5 %collective-permute-start.2 = (f32[4]{0:T(128)S(1)}, f32[4]{0:T(128)S(1)}, u32[]{:S(2)}, u32[]{:S(2)}) collective-permute-start(f32[4]{0:T(128)S(1)} %max.12), channel_id=1, source_target_pairs={{0,8},{4,12},{8,0},{12,4},{1,9},{5,13},{9,1},{13,5},{2,10},{6,14},... | collective-permute-start | bytes 56 | tf_op jit(solution)/shard_map/ppermute | solution.py:379
  95.3 2.1 %collective-permute-done.2 = f32[4]{0:T(128)S(1)} collective-permute-done((f32[4]{0:T(128)S(1)}, f32[4]{0:T(128)S(1)}, u32[]{:S(2)}, u32[]{:S(2)}) %collective-permute-start.2) | collective-permute-done | bytes 48 | tf_op jit(solution)/shard_map/ppermute | solution.py:379
  97.4 1.8 %collective-permute-start.3 = (f32[4]{0:T(128)S(1)}, f32[4]{0:T(128)S(1)}, u32[]{:S(2)}, u32[]{:S(2)}) collective-permute-start(f32[4]{0:T(128)S(1)} %max.13), channel_id=1, source_target_pairs={{0,1},{1,0},{2,3},{3,2},{4,5},{5,4},{6,7},{7,6},{8,9},{9,8},{10,11... | collective-permute-start | bytes 56 | tf_op jit(solution)/shard_map/ppermute | solution.py:379
  99.2 1.8 %collective-permute-done.3 = f32[4]{0:T(128)S(1)} collective-permute-done((f32[4]{0:T(128)S(1)}, f32[4]{0:T(128)S(1)}, u32[]{:S(2)}, u32[]{:S(2)}) %collective-permute-start.3) | collective-permute-done | bytes 48 | tf_op jit(solution)/shard_map/ppermute | solution.py:379
  100.9 1.1 collective-permute-start.4
  102.0 3.4 %collective-permute-done.4 = f32[4]{0:T(128)S(1)} collective-permute-done((f32[4]{0:T(128)S(1)}, f32[4]{0:T(128)S(1)}, u32[]{:S(2)}, u32[]{:S(2)}) %collective-permute-start.4) | collective-permute-done | bytes 48 | tf_op jit(solution)/shard_map/ppermute | solution.py:379
  105.4 0.5 max.15
  (9 shorter events, 0.0 us)
Async XLA Ops:
  0.6 16.2 %copy-start = (bf16[256,256]{1,0:T(8,128)(2,1)S(1)}, bf16[256,256]{1,0:T(8,128)(2,1)}, u32[]{:S(2)}) copy-start(bf16[256,256]{1,0:T(8,128)(2,1)} %constant.38.clone.yr) | copy-start | bytes 393220
  0.6 16.2 %copy-start.1 = (bf16[256,256]{1,0:T(8,128)(2,1)S(1)}, bf16[256,256]{1,0:T(8,128)(2,1)}, u32[]{:S(2)}) copy-start(bf16[256,256]{1,0:T(8,128)(2,1)} %constant.37.clone.yh) | copy-start | bytes 393220
  0.7 16.2 %copy-start.2 = (bf16[256,256]{1,0:T(8,128)(2,1)S(1)}, bf16[256,256]{1,0:T(8,128)(2,1)}, u32[]{:S(2)}) copy-start(bf16[256,256]{1,0:T(8,128)(2,1)} %constant.36.clone.zr) | copy-start | bytes 393220
  0.7 16.2 %copy-start.3 = (bf16[256,256]{1,0:T(8,128)(2,1)S(1)}, bf16[256,256]{1,0:T(8,128)(2,1)}, u32[]{:S(2)}) copy-start(bf16[256,256]{1,0:T(8,128)(2,1)} %constant.35.clone.zh) | copy-start | bytes 393220
  0.7 16.2 %copy-start.4 = (bf16[32,16,128]{2,1,0:T(8,128)(2,1)S(1)}, bf16[32,16,128]{2,1,0:T(8,128)(2,1)}, u32[]{:S(2)}) copy-start(bf16[32,16,128]{2,1,0:T(8,128)(2,1)} %constant.41.clone.table_ref) | copy-start | bytes 393220
  0.7 10.0 %copy-start.7 = (s32[4,2048]{1,0:T(4,128)S(1)}, s32[4,2048]{1,0:T(4,128)}, u32[]{:S(2)}) copy-start(s32[4,2048]{1,0:T(4,128)} %own_ref.1) | copy-start | bytes 98308
  0.7 16.2 %copy-start.9 = (f32[2048]{0:T(1024)S(1)}, f32[2048]{0:T(1024)}, u32[]{:S(2)}) copy-start(f32[2048]{0:T(1024)} %param.16) | copy-start | bytes 24580
  0.7 16.2 %copy-start.8 = (f32[2048]{0:T(1024)S(1)}, f32[2048]{0:T(1024)}, u32[]{:S(2)}) copy-start(f32[2048]{0:T(1024)} %param.15) | copy-start | bytes 24580
  3.4 27.4 %all-to-all-start = ((f32[32,32,128]{2,1,0:T(8,128)}), f32[32,32,128]{2,1,0:T(8,128)S(1)}, u32[]{:S(2)}, u32[]{:S(2)}) async-start(f32[32,32,128]{2,1,0:T(8,128)} %bitcast.7), calls=%async_computation | async-start | bytes 1048576 | tf_op jit(solution)/shard_map/all_to_all | solution.py:326
  10.7 6.2 %collective-permute-start = (s32[4,2048]{1,0:T(4,128)S(1)}, s32[4,2048]{1,0:T(4,128)S(1)}, u32[]{:S(2)}, u32[]{:S(2)}) collective-permute-start(s32[4,2048]{1,0:T(4,128)S(1)} %copy-done.7), channel_id=1, source_target_pairs={{0,16},{16,0},{1,17},{17,1},{2,18},{18,2},{3,19},{19,3},{4,20},{20... | collective-permute-start | bytes 98312 | tf_op jit(solution)/shard_map/ppermute | solution.py:325
  35.4 52.7 %copy-start.5 = (bf16[128,128]{1,0:T(8,128)(2,1)S(1)}, bf16[128,128]{1,0:T(8,128)(2,1)}, u32[]{:S(2)}) copy-start(bf16[128,128]{1,0:T(8,128)(2,1)} %constant.43.clone.rest_ref) | copy-start | bytes 98308
  35.5 52.7 %copy-start.6 = (bf16[128,128]{1,0:T(8,128)(2,1)S(1)}, bf16[128,128]{1,0:T(8,128)(2,1)}, u32[]{:S(2)}) copy-start(bf16[128,128]{1,0:T(8,128)(2,1)} %constant.42.clone.head_ref) | copy-start | bytes 98308
  91.3 2.5 %collective-permute-start.1 = (f32[4]{0:T(128)S(1)}, f32[4]{0:T(128)S(1)}, u32[]{:S(2)}, u32[]{:S(2)}) collective-permute-start(f32[4]{0:T(128)S(1)} %get-tuple-element.13), channel_id=1, source_target_pairs={{0,4},{4,0},{8,12},{12,8},{1,5},{5,1},{9,13},{13,9},{2,6},{6,2},{1... | collective-permute-start | bytes 56 | tf_op jit(solution)/shard_map/ppermute | solution.py:379
  93.8 3.6 %collective-permute-start.2 = (f32[4]{0:T(128)S(1)}, f32[4]{0:T(128)S(1)}, u32[]{:S(2)}, u32[]{:S(2)}) collective-permute-start(f32[4]{0:T(128)S(1)} %max.12), channel_id=1, source_target_pairs={{0,8},{4,12},{8,0},{12,4},{1,9},{5,13},{9,1},{13,5},{2,10},{6,14},... | collective-permute-start | bytes 56 | tf_op jit(solution)/shard_map/ppermute | solution.py:379
  97.4 3.6 %collective-permute-start.3 = (f32[4]{0:T(128)S(1)}, f32[4]{0:T(128)S(1)}, u32[]{:S(2)}, u32[]{:S(2)}) collective-permute-start(f32[4]{0:T(128)S(1)} %max.13), channel_id=1, source_target_pairs={{0,1},{1,0},{2,3},{3,2},{4,5},{5,4},{6,7},{7,6},{8,9},{9,8},{10,11... | collective-permute-start | bytes 56 | tf_op jit(solution)/shard_map/ppermute | solution.py:379
  100.9 4.5 %collective-permute-start.4 = (f32[4]{0:T(128)S(1)}, f32[4]{0:T(128)S(1)}, u32[]{:S(2)}, u32[]{:S(2)}) collective-permute-start(f32[4]{0:T(128)S(1)} %max.14), channel_id=1, source_target_pairs={{0,2},{1,3},{2,0},{3,1},{4,6},{5,7},{6,4},{7,5},{8,10},{9,11},{10,... | collective-permute-start | bytes 56 | tf_op jit(solution)/shard_map/ppermute | solution.py:379

commit v5 on v4

--- a/solution.py
+++ b/solution.py
@@ -65,15 +65,19 @@
 
 def times_constant(value, head_ref, rest_ref):
     head, rest = split(value)
-    return dot(head, head_ref[...]) + (dot(head, rest_ref[...]) + dot(rest, head_ref[...]))
-
-
-def constant_times(head_ref, rest_ref, values):
+    count = value.shape[0]
+    both = dot(jnp.concatenate([head, rest], axis=0), head_ref[...])
+    return both[:count] + (dot(head, rest_ref[...]) + both[count:])
+
+
+def constant_times(both_ref, values):
+    count = both_ref.shape[0] // 2
     results = []
     for i in range(0, len(values), 2):
         pair = values[i : i + 2]
         head, rest = split(jnp.concatenate(pair, axis=1))
-        result = dot(head_ref[...], head) + (dot(rest_ref[...], head) + dot(head_ref[...], rest))
+        both = dot(both_ref[...], head)
+        result = both[:count] + (both[count:] + dot(both_ref[:count], rest))
         width = pair[0].shape[1]
         results += [result[:, j * width : (j + 1) * width] for j in range(len(pair))]
     return results
@@ -111,20 +115,20 @@
     return jnp.where(rows == place, 1.0, 0.0).astype(jnp.bfloat16)
 
 
-def spectrum(planes, n, zh, zr, yh, yr):
+def spectrum(planes, n, zh, zr, yb, at_once):
     columns = []
-    for i in range(0, len(planes), 2):
-        pairs = planes[i : i + 2]
+    for i in range(0, len(planes), at_once):
+        pairs = planes[i : i + at_once]
         rows = jnp.concatenate([jnp.concatenate(pair, axis=1) for pair in pairs], axis=0)
         rows = times_constant(rows, zh, zr)
         columns += [
             jnp.concatenate([rows[j * n : (j + 1) * n, :n], rows[j * n : (j + 1) * n, n:]], axis=0)
             for j in range(len(pairs))
         ]
-    return constant_times(yh, yr, columns)
-
-
-def ligand_kernel(place_ref, own_ref, other_ref, shape_ref, charge_ref, table_ref, zh, zr, yh, yr, far_ref, near_ref, held_ref, sems):
+    return constant_times(yb, columns)
+
+
+def ligand_kernel(place_ref, own_ref, other_ref, shape_ref, charge_ref, table_ref, zh, zr, yb, far_ref, near_ref, held_ref, sems):
     n = zh.shape[0] // 2
     half = n // 2
     atoms = own_ref.shape[1]
@@ -171,7 +175,7 @@
             )
         planes[0].append(first)
         planes[1].append(second)
-    near_ref[...] = jnp.concatenate(spectrum(planes[0] + planes[1], n, zh, zr, yh, yr), axis=1)
+    near_ref[...] = jnp.concatenate(spectrum(planes[0] + planes[1], n, zh, zr, yb, 2), axis=1)
     last = pl.num_programs(0) - 1
 
     @pl.when(step < last)
@@ -185,7 +189,7 @@
             pltpu.make_async_copy(held_ref.at[i], far_ref.at[i], sems.at[i]).wait()
 
 
-def receptor_spectrum(special, blocks_ref, zh, zr, yh, yr, channels, y_parts, z_parts):
+def receptor_spectrum(special, blocks_ref, zh, zr, yb, channels, y_parts, z_parts):
     n = zh.shape[0] // 2
     width = n // z_parts
     comps = blocks_ref.shape[1] // SUBLANES
@@ -205,11 +209,11 @@
         planes.append((jnp.where(special, parts[1], parts[0]), lone))
         for c in range(2, comps, 2):
             planes.append((parts[c], parts[c + 1]))
-    return spectrum(planes, n, zh, zr, yh, yr)
+    return spectrum(planes, n, zh, zr, yb, 4)
 
 
 def product_kernel(
-    place_ref, blocks_ref, far_ref, near_ref, zh, zr, yh, yr, out_ref, ligand_ref, sems, *, channels, y_parts, z_parts
+    place_ref, blocks_ref, far_ref, near_ref, zh, zr, yb, out_ref, ligand_ref, sems, *, channels, y_parts, z_parts
 ):
     n = zh.shape[0] // 2
     width = n // z_parts
@@ -220,7 +224,7 @@
     copies = [pltpu.make_async_copy(far_ref.at[i], ligand_ref.at[i], sems.at[i]) for i in range(last)]
     for copy in copies:
         copy.start()
-    receptor = receptor_spectrum(special, blocks_ref, zh, zr, yh, yr, channels, y_parts, z_parts)
+    receptor = receptor_spectrum(special, blocks_ref, zh, zr, yb, channels, y_parts, z_parts)
     for copy in copies:
         copy.wait()
 
@@ -238,7 +242,7 @@
                     real = real + (fr * hr + fi * hi)
                     imag = imag + (fr * hi - fi * hr)
                 columns.append(jnp.concatenate([real, imag], axis=0))
-        columns = constant_times(yh, yr, columns)
+        columns = constant_times(yb, columns)
         rows = jnp.concatenate([jnp.concatenate([c[:n], c[n:]], axis=1) for c in columns], axis=0)
         rows = times_constant(rows, zh, zr)
         maps = []
@@ -257,22 +261,25 @@
                     out_ref[(rotation * y_parts + y_part) * z_parts + z_part, row : row + SUBLANES] = block
 
 
-def inverse_x_kernel(blocks_ref, head_ref, rest_ref, out_ref, best_ref, rows_ref):
-    n = head_ref.shape[0]
-    _, z_block = out_ref.shape[1:3]
+def inverse_x_kernel(blocks_ref, matrix_ref, out_ref, best_ref, rows_ref, held_ref, sems):
+    rotations, _, z_block, n = held_ref.shape
     groups = LANES // z_block
-    step = pl.program_id(0)
-    count = rows_ref.shape[0] // blocks_ref.shape[0]
-    first = pl.multiple_of(step * count, SUBLANES)
-    rows_ref[...] = blocks_ref[:, pl.ds(first, count), :].reshape(rows_ref.shape)
-    best = None
-    for row in range(SUBLANES):
-        values = rows_ref[pl.ds(row, n, stride=SUBLANES), :]
-        result = times_constant(values.T, head_ref, rest_ref)
-        for g in range(groups):
-            out_ref[0, g * SUBLANES + row] = result[g * z_block : (g + 1) * z_block, :]
-        best = result if best is None else jnp.maximum(best, result)
-    best_ref[step] = jnp.max(best)
+    count = rows_ref.shape[1] // blocks_ref.shape[0]
+    copies = [pltpu.make_async_copy(held_ref.at[i], out_ref.at[i], sems.at[i]) for i in range(rotations)]
+    for i, copy in enumerate(copies):
+        rows_ref[i] = blocks_ref[:, i * count : (i + 1) * count, :].reshape(rows_ref.shape[1:])
+        best = None
+        for row in range(SUBLANES):
+            values = rows_ref[i, pl.ds(row, n, stride=SUBLANES), :]
+            result = dot(jnp.concatenate(split(values.T), axis=1), matrix_ref[...])
+            result = result[:, :n] + result[:, n:]
+            for g in range(groups):
+                held_ref[i, g * SUBLANES + row] = result[g * z_block : (g + 1) * z_block, :]
+            best = result if best is None else jnp.maximum(best, result)
+        copy.start()
+        best_ref[i] = jnp.max(best)
+    for copy in copies:
+        copy.wait()
 
 
 def whole():
@@ -310,7 +317,7 @@
     channels = 2
     f32 = jnp.float32
     matrices = split_constant(plus_matrix(n))
-    matrices = [jnp.asarray(m) for m in (*matrices, *(np.ascontiguousarray(m.T) for m in matrices))]
+    matrices = [jnp.asarray(m) for m in (*matrices, np.concatenate([m.T for m in matrices], axis=0))]
     place = lax.axis_index(AXES).reshape(1)
 
     components = pl.pallas_call(
@@ -334,7 +341,7 @@
             jax.ShapeDtypeStruct((slabs, 2 * n, width), f32),
             jax.ShapeDtypeStruct((2 * n, width), f32),
         ],
-        in_specs=[scalars()] + [whole()] * 9,
+        in_specs=[scalars()] + [whole()] * 8,
         out_specs=[far(), whole()],
         scratch_shapes=[pltpu.VMEM((rotations - 1, 2 * n, width), f32), pltpu.SemaphoreType.DMA((rotations - 1,))],
         compiler_params=room(24),
@@ -352,27 +359,31 @@
     sent = pl.pallas_call(
         functools.partial(product_kernel, channels=channels, y_parts=y_parts, z_parts=z_parts),
         out_shape=jax.ShapeDtypeStruct((devices, rotations * rows, LANES), f32),
-        in_specs=[scalars(), whole(), far()] + [whole()] * 5,
+        in_specs=[scalars(), whole(), far()] + [whole()] * 4,
         out_specs=whole(),
         scratch_shapes=[pltpu.VMEM((rotations - 1, 2 * n, width), f32), pltpu.SemaphoreType.DMA((rotations - 1,))],
         compiler_params=room(16),
         name="product",
     )(place, blocks, far_ligand, near_ligand, *matrices)
+    head, rest = split_constant(inverse_x_matrix(n))
     got = lax.all_to_all(sent, AXES, 0, 0, tiled=True)
 
     correlation, best = pl.pallas_call(
         inverse_x_kernel,
-        grid=(rotations,),
         out_shape=[
             jax.ShapeDtypeStruct((rotations, y_block, z_block, n), f32),
             jax.ShapeDtypeStruct((rotations,), f32),
         ],
-        in_specs=[whole()] * 3,
-        out_specs=[pl.BlockSpec((1, y_block, z_block, n), lambda i: (i, 0, 0, 0)), scalars()],
-        scratch_shapes=[pltpu.VMEM((devices * rows, LANES), f32)],
-        compiler_params=room(8),
+        in_specs=[whole()] * 2,
+        out_specs=[far(), scalars()],
+        scratch_shapes=[
+            pltpu.VMEM((rotations, devices * rows, LANES), f32),
+            pltpu.VMEM((rotations, y_block, z_block, n), f32),
+            pltpu.SemaphoreType.DMA((rotations,)),
+        ],
+        compiler_params=room(12),
         name="inverse_x",
-    )(got, *(jnp.asarray(m) for m in split_constant(inverse_x_matrix(n))))
+    )(got, jnp.asarray(np.block([[head, rest], [head, np.zeros_like(head)]])))
     for axis in ("py", "pz"):
         step = 1
         while step < sizes[axis]:

time: 106 us -> 105 us (level)
  no operation moved by 1% of the time
where the time goes in v5:
time: 105 us
  blocking collectives  52.6 us (50%)
  Pallas kernels  23.4 us (22%)
  starting transfers between devices  15.2 us (14%)
  waiting for transfers between devices  12.4 us (12%)
    all_to_all x1, blocking collectives, on_device(): got = lax.all_to_all(sent, AXES, 0, 0, tiled=True)  52.6 us
    pallas_call x1, Pallas kernels, on_device(): pl.pallas_call(ligand_kernel, grid=(rotations,), out_shape=[jax.ShapeDtyp...  13.8 us
    ppermute x4, waiting for transfers between devices, on_device(): lax.ppermute(best, axis, [(i, i ^ step) for i in range(sizes[axis])])  8.08 us
    all_to_all x1, starting transfers between devices, on_device(): lax.all_to_all(components.reshape(devices, rows, LANES), AXES, 0, 0, tile...  7.32 us
    ppermute x4, starting transfers between devices, on_device(): lax.ppermute(best, axis, [(i, i ^ step) for i in range(sizes[axis])])  6.05 us
    pallas_call x1, Pallas kernels, on_device(): pl.pallas_call(functools.partial(product_kernel, channels=channels, y_par...  4.63 us
    ppermute x1, waiting for transfers between devices, on_device(): other = lax.ppermute(cells, 'rot', [(i, i ^ 1) for i in range(rots)])  4.33 us
    pallas_call x1, Pallas kernels, on_device(): pl.pallas_call(forward_x_kernel, out_shape=jax.ShapeDtypeStruct((n * SUBL...  2.58 us
  transfers between devices with their start and end apart: 6, of which 5 were waited for; matrix products, arithmetic and copies ran while one was open for 0% of the time, Pallas kernels for 13%

profile of v5, /device:TPU:0, one launch (start us, length us, event | category | flops | bytes accessed | tf_op | source)
XLA Modules:
  0.0 105.0 jit_solution(4820575725411275416)
XLA Ops:
  0.6 0.0 copy-start
  0.6 0.0 copy-start.1
  0.7 0.0 copy-start.2
  0.7 0.0 copy-start.4
  0.7 0.0 copy-start.5
  0.7 0.0 copy-start.7
  0.7 0.0 copy-start.6
  0.7 2.6 %forward_x.1 = f32[1024,128]{1,0:T(8,128)} custom-call(f32[1,32,32,128]{3,2,1,0:T(8,128)} %bitcast.8, bf16[128,128]{1,0:T(8,128)(2,1)} %constant.34.clone.head_ref, bf16[128,128]{1,0:T(8,128)(2,1)} %constant.35.clone.rest_ref), custom_call_target="tpu_custom_call" | custom-call | tf_op jit(solution)/shard_map/forward_x/pallas_call | solution.py:323
  3.3 7.3 %all-to-all-start = ((f32[32,32,128]{2,1,0:T(8,128)}), f32[32,32,128]{2,1,0:T(8,128)S(1)}, u32[]{:S(2)}, u32[]{:S(2)}) async-start(f32[32,32,128]{2,1,0:T(8,128)} %bitcast.7), calls=%async_computation | async-start | bytes 1048576 | tf_op jit(solution)/shard_map/all_to_all | solution.py:333
  10.6 0.0 copy-done.5
  10.6 1.8 %collective-permute-start = (s32[4,2048]{1,0:T(4,128)S(1)}, s32[4,2048]{1,0:T(4,128)S(1)}, u32[]{:S(2)}, u32[]{:S(2)}) collective-permute-start(s32[4,2048]{1,0:T(4,128)S(1)} %copy-done.5), channel_id=1, source_target_pairs={{0,16},{16,0},{1,17},{17,1},{2,18},{18,2},{3,19},{19,3},{4,20},{20... | collective-permute-start | bytes 98312 | tf_op jit(solution)/shard_map/ppermute | solution.py:332
  12.5 4.3 %collective-permute-done.other_ref = s32[4,2048]{1,0:T(4,128)S(1)} collective-permute-done((s32[4,2048]{1,0:T(4,128)S(1)}, s32[4,2048]{1,0:T(4,128)S(1)}, u32[]{:S(2)}, u32[]{:S(2)}) %collective-permute-start) | collective-permute-done | bytes 32800 | tf_op jit(solution)/shard_map/ppermute | solution.py:332
  16.8 0.0 copy-done
  16.8 0.0 copy-done.1
  16.8 0.0 copy-done.2
  16.8 0.0 copy-done.4
  16.8 0.0 copy-done.7
  16.8 13.8 %ligand.1 = (f32[48,256,1024]{2,1,0:T(8,128)}, f32[256,1024]{1,0:T(8,128)S(1)}) custom-call(s32[1]{0:T(128)} %bitcast.place_ref, s32[4,2048]{1,0:T(4,128)S(1)} %copy-done.5, s32[4,2048]{1,0:T(4,128)S(1)} %collective-permute-done.other_ref, f32[1,2048]{1,0:T(1,128)S(1)} %bitcast.5, f32[1,2048]{1,0:T(1,128)S(1)} %bitcast.6, ...), custom_call_target="tpu_custom_call" | custom-call | tf_op jit(solution)/shard_map/ligand/pallas_call | solution.py:337
  30.6 0.0 all-to-all-done.blocks_ref
  30.7 4.6 %product.1 = f32[32,128,128]{2,1,0:T(8,128)S(1)} custom-call(s32[1]{0:T(128)} %bitcast.place_ref, f32[32,32,128]{2,1,0:T(8,128)S(1)} %all-to-all-done.blocks_ref, f32[48,256,1024]{2,1,0:T(8,128)} %get-tuple-element.10.far_ref, f32[256,1024]{1,0:T(8,128)S(1)} %get-tuple-element.11.near_ref, bf16[256,256]{1,0:T(8,128)(2,1)S(1)} %copy-done.2, ...), custom_call_target="tpu_custom_call" | custom-call | tf_op jit(solution)/shard_map/product/pallas_call | solution.py:359
  35.3 0.0 copy-start.3
  35.3 52.6 %all_to_all.10.blocks_ref = f32[32,128,128]{2,1,0:T(8,128)S(1)} all-to-all(f32[32,128,128]{2,1,0:T(8,128)S(1)} %product.1), channel_id=1, replica_groups=mesh['rot'=2,'py'=4,'pz'=4] {'rot','py','pz'}, dimensions={0} | all-to-all | bytes 4194304 | tf_op jit(solution)/shard_map/all_to_all | solution.py:369
  87.9 2.4 %inverse_x.1 = (f32[4,32,32,128]{3,2,1,0:T(8,128)}, f32[4]{0:T(128)S(1)}) custom-call(f32[32,128,128]{2,1,0:T(8,128)S(1)} %all_to_all.10.blocks_ref, bf16[256,256]{1,0:T(8,128)(2,1)S(1)} %copy-done.3), custom_call_target="tpu_custom_call" | custom-call | tf_op jit(solution)/shard_map/inverse_x/pallas_call | solution.py:371
  90.3 1.7 %collective-permute-start.1 = (f32[4]{0:T(128)S(1)}, f32[4]{0:T(128)S(1)}, u32[]{:S(2)}, u32[]{:S(2)}) collective-permute-start(f32[4]{0:T(128)S(1)} %get-tuple-element.13), channel_id=1, source_target_pairs={{0,4},{4,0},{8,12},{12,8},{1,5},{5,1},{9,13},{13,9},{2,6},{6,2},{1... | collective-permute-start | bytes 56 | tf_op jit(solution)/shard_map/ppermute | solution.py:390
  92.0 0.8 collective-permute-done.1
  92.9 1.5 %collective-permute-start.2 = (f32[4]{0:T(128)S(1)}, f32[4]{0:T(128)S(1)}, u32[]{:S(2)}, u32[]{:S(2)}) collective-permute-start(f32[4]{0:T(128)S(1)} %max.12), channel_id=1, source_target_pairs={{0,8},{4,12},{8,0},{12,4},{1,9},{5,13},{9,1},{13,5},{2,10},{6,14},... | collective-permute-start | bytes 56 | tf_op jit(solution)/shard_map/ppermute | solution.py:390
  94.3 2.1 %collective-permute-done.2 = f32[4]{0:T(128)S(1)} collective-permute-done((f32[4]{0:T(128)S(1)}, f32[4]{0:T(128)S(1)}, u32[]{:S(2)}, u32[]{:S(2)}) %collective-permute-start.2) | collective-permute-done | bytes 48 | tf_op jit(solution)/shard_map/ppermute | solution.py:390
  96.4 1.8 %collective-permute-start.3 = (f32[4]{0:T(128)S(1)}, f32[4]{0:T(128)S(1)}, u32[]{:S(2)}, u32[]{:S(2)}) collective-permute-start(f32[4]{0:T(128)S(1)} %max.13), channel_id=1, source_target_pairs={{0,1},{1,0},{2,3},{3,2},{4,5},{5,4},{6,7},{7,6},{8,9},{9,8},{10,11... | collective-permute-start | bytes 56 | tf_op jit(solution)/shard_map/ppermute | solution.py:390
  98.2 1.8 %collective-permute-done.3 = f32[4]{0:T(128)S(1)} collective-permute-done((f32[4]{0:T(128)S(1)}, f32[4]{0:T(128)S(1)}, u32[]{:S(2)}, u32[]{:S(2)}) %collective-permute-start.3) | collective-permute-done | bytes 48 | tf_op jit(solution)/shard_map/ppermute | solution.py:390
  100.0 1.1 %collective-permute-start.4 = (f32[4]{0:T(128)S(1)}, f32[4]{0:T(128)S(1)}, u32[]{:S(2)}, u32[]{:S(2)}) collective-permute-start(f32[4]{0:T(128)S(1)} %max.14), channel_id=1, source_target_pairs={{0,2},{1,3},{2,0},{3,1},{4,6},{5,7},{6,4},{7,5},{8,10},{9,11},{10,... | collective-permute-start | bytes 56 | tf_op jit(solution)/shard_map/ppermute | solution.py:390
  101.1 3.4 %collective-permute-done.4 = f32[4]{0:T(128)S(1)} collective-permute-done((f32[4]{0:T(128)S(1)}, f32[4]{0:T(128)S(1)}, u32[]{:S(2)}, u32[]{:S(2)}) %collective-permute-start.4) | collective-permute-done | bytes 48 | tf_op jit(solution)/shard_map/ppermute | solution.py:390
  104.5 0.5 max.15
  (5 shorter events, 0.0 us)
Async XLA Ops:
  0.6 16.2 %copy-start = (bf16[512,256]{1,0:T(8,128)(2,1)S(1)}, bf16[512,256]{1,0:T(8,128)(2,1)}, u32[]{:S(2)}) copy-start(bf16[512,256]{1,0:T(8,128)(2,1)} %constant.33.clone.yb) | copy-start | bytes 786436
  0.6 16.1 %copy-start.1 = (bf16[256,256]{1,0:T(8,128)(2,1)S(1)}, bf16[256,256]{1,0:T(8,128)(2,1)}, u32[]{:S(2)}) copy-start(bf16[256,256]{1,0:T(8,128)(2,1)} %constant.32.clone.zr) | copy-start | bytes 393220
  0.7 16.1 %copy-start.2 = (bf16[256,256]{1,0:T(8,128)(2,1)S(1)}, bf16[256,256]{1,0:T(8,128)(2,1)}, u32[]{:S(2)}) copy-start(bf16[256,256]{1,0:T(8,128)(2,1)} %constant.31.clone.zh) | copy-start | bytes 393220
  0.7 16.1 %copy-start.4 = (bf16[32,16,128]{2,1,0:T(8,128)(2,1)S(1)}, bf16[32,16,128]{2,1,0:T(8,128)(2,1)}, u32[]{:S(2)}) copy-start(bf16[32,16,128]{2,1,0:T(8,128)(2,1)} %constant.36.clone.table_ref) | copy-start | bytes 393220
  0.7 9.9 %copy-start.5 = (s32[4,2048]{1,0:T(4,128)S(1)}, s32[4,2048]{1,0:T(4,128)}, u32[]{:S(2)}) copy-start(s32[4,2048]{1,0:T(4,128)} %own_ref.1) | copy-start | bytes 98308
  0.7 16.1 %copy-start.7 = (f32[2048]{0:T(1024)S(1)}, f32[2048]{0:T(1024)}, u32[]{:S(2)}) copy-start(f32[2048]{0:T(1024)} %param.14) | copy-start | bytes 24580
  0.7 16.1 %copy-start.6 = (f32[2048]{0:T(1024)S(1)}, f32[2048]{0:T(1024)}, u32[]{:S(2)}) copy-start(f32[2048]{0:T(1024)} %param.13) | copy-start | bytes 24580
  3.3 27.4 %all-to-all-start = ((f32[32,32,128]{2,1,0:T(8,128)}), f32[32,32,128]{2,1,0:T(8,128)S(1)}, u32[]{:S(2)}, u32[]{:S(2)}) async-start(f32[32,32,128]{2,1,0:T(8,128)} %bitcast.7), calls=%async_computation | async-start | bytes 1048576 | tf_op jit(solution)/shard_map/all_to_all | solution.py:333
  10.6 6.2 %collective-permute-start = (s32[4,2048]{1,0:T(4,128)S(1)}, s32[4,2048]{1,0:T(4,128)S(1)}, u32[]{:S(2)}, u32[]{:S(2)}) collective-permute-start(s32[4,2048]{1,0:T(4,128)S(1)} %copy-done.5), channel_id=1, source_target_pairs={{0,16},{16,0},{1,17},{17,1},{2,18},{18,2},{3,19},{19,3},{4,20},{20... | collective-permute-start | bytes 98312 | tf_op jit(solution)/shard_map/ppermute | solution.py:332
  35.3 52.7 %copy-start.3 = (bf16[256,256]{1,0:T(8,128)(2,1)S(1)}, bf16[256,256]{1,0:T(8,128)(2,1)}, u32[]{:S(2)}) copy-start(bf16[256,256]{1,0:T(8,128)(2,1)} %constant.37.clone.matrix_ref) | copy-start | bytes 393220
  90.3 2.5 %collective-permute-start.1 = (f32[4]{0:T(128)S(1)}, f32[4]{0:T(128)S(1)}, u32[]{:S(2)}, u32[]{:S(2)}) collective-permute-start(f32[4]{0:T(128)S(1)} %get-tuple-element.13), channel_id=1, source_target_pairs={{0,4},{4,0},{8,12},{12,8},{1,5},{5,1},{9,13},{13,9},{2,6},{6,2},{1... | collective-permute-start | bytes 56 | tf_op jit(solution)/shard_map/ppermute | solution.py:390
  92.9 3.6 %collective-permute-start.2 = (f32[4]{0:T(128)S(1)}, f32[4]{0:T(128)S(1)}, u32[]{:S(2)}, u32[]{:S(2)}) collective-permute-start(f32[4]{0:T(128)S(1)} %max.12), channel_id=1, source_target_pairs={{0,8},{4,12},{8,0},{12,4},{1,9},{5,13},{9,1},{13,5},{2,10},{6,14},... | collective-permute-start | bytes 56 | tf_op jit(solution)/shard_map/ppermute | solution.py:390
  96.4 3.6 %collective-permute-start.3 = (f32[4]{0:T(128)S(1)}, f32[4]{0:T(128)S(1)}, u32[]{:S(2)}, u32[]{:S(2)}) collective-permute-start(f32[4]{0:T(128)S(1)} %max.13), channel_id=1, source_target_pairs={{0,1},{1,0},{2,3},{3,2},{4,5},{5,4},{6,7},{7,6},{8,9},{9,8},{10,11... | collective-permute-start | bytes 56 | tf_op jit(solution)/shard_map/ppermute | solution.py:390
  100.0 4.5 %collective-permute-start.4 = (f32[4]{0:T(128)S(1)}, f32[4]{0:T(128)S(1)}, u32[]{:S(2)}, u32[]{:S(2)}) collective-permute-start(f32[4]{0:T(128)S(1)} %max.14), channel_id=1, source_target_pairs={{0,2},{1,3},{2,0},{3,1},{4,6},{5,7},{6,4},{7,5},{8,10},{9,11},{10,... | collective-permute-start | bytes 56 | tf_op jit(solution)/shard_map/ppermute | solution.py:390

commit v6 on v5

--- a/solution.py
+++ b/solution.py
@@ -128,47 +128,58 @@
     return constant_times(yb, columns)
 
 
-def ligand_kernel(place_ref, own_ref, other_ref, shape_ref, charge_ref, table_ref, zh, zr, yb, far_ref, near_ref, held_ref, sems):
+def cosine(turns, n):
+    folded = (jnp.abs((turns + n // 2) % n - n // 2) - n // 4).astype(jnp.float32) * (2.0 * math.pi / n)
+    square = folded * folded
+    total = jnp.zeros_like(folded)
+    for power in (13, 11, 9, 7, 5, 3, 1):
+        total = total * square + (-1.0) ** ((power + 1) // 2) / math.factorial(power)
+    return total * folded
+
+
+def ligand_kernel(place_ref, cells_ref, shape_ref, charge_ref, zh, zr, yb, far_ref, near_ref, held_ref, sems):
     n = zh.shape[0] // 2
     half = n // 2
-    atoms = own_ref.shape[1]
+    atoms = cells_ref.shape[1]
+    comps = near_ref.shape[1] // (2 * n)
     step = pl.program_id(0)
-    device = place_ref[0]
-    first_half = device < table_ref.shape[0] // 2
-    special = device == 0
-    own, other = own_ref[pl.ds(step, 1), :], other_ref[pl.ds(step, 1), :]
+    row = lax.broadcasted_iota(jnp.int32, (comps, 1), 0)
+    slot = place_ref[0] * (comps // 2) + row // 2
+    second = row % 2 == 1
+    times = jnp.where(second & (slot == 0), half, slot)
+    shift = jnp.where(second & (slot != 0), n - n // 4, 0)
+    special = place_ref[0] == 0
     grids = []
-    for cell in (jnp.where(first_half, own, other), jnp.where(first_half, other, own)):
+    for rotation in range(2):
+        cell = cells_ref[pl.ds(2 * step + rotation, 1), :]
         coord_x, coord_y, coord_z = cell // (n * n), cell // n % n, cell % n
-        wave = dot(table_ref[device], one_hot_rows(n, coord_x))
-        comps = wave.shape[0] // 4
-        wave = wave[:comps] + (wave[comps : 2 * comps] + wave[2 * comps : 3 * comps])
+        wave = cosine(times * coord_x + shift, n)
         values = jnp.concatenate([wave * shape_ref[...], wave * charge_ref[...]], axis=0)
-        comps = values.shape[0]
+        count = values.shape[0]
         head = values.astype(jnp.bfloat16).astype(jnp.float32)
         hit = lax.broadcasted_iota(jnp.int32, (half, atoms), 0) == coord_y % half
         stacked = jnp.concatenate(
             [
                 jnp.where(hit, part[c : c + 1, :], 0.0).astype(jnp.bfloat16)
                 for part in (head, values - head)
-                for c in range(comps)
+                for c in range(count)
             ],
             axis=0,
         )
         total = dot_rows(stacked, one_hot_rows(2 * n, coord_z + n * (coord_y // half)))
-        total = total[: comps * half] + total[comps * half :]
+        total = total[: count * half] + total[count * half :]
         grids.append(
             [
                 jnp.concatenate(
                     [total[c * half : (c + 1) * half, :n], total[c * half : (c + 1) * half, n:]], axis=0
                 )
-                for c in range(comps)
+                for c in range(count)
             ]
         )
     planes = [[], []]
-    for c in range(0, comps, 2):
+    for c in range(0, count, 2):
         first, second = (grids[0][c], grids[0][c + 1]), (grids[1][c], grids[1][c + 1])
-        if c % (comps // 2) == 0:
+        if c % comps == 0:
             first, second = (
                 (first[0], jnp.where(special, second[0], first[1])),
                 (jnp.where(special, first[1], second[0]), second[1]),
@@ -213,26 +224,49 @@
 
 
 def product_kernel(
-    place_ref, blocks_ref, far_ref, near_ref, zh, zr, yb, out_ref, ligand_ref, sems, *, channels, y_parts, z_parts
+    place_ref,
+    blocks_ref,
+    far_own_ref,
+    near_own_ref,
+    far_other_ref,
+    near_other_ref,
+    zh,
+    zr,
+    yb,
+    out_ref,
+    ligand_ref,
+    sems,
+    *,
+    channels,
+    y_parts,
+    z_parts,
 ):
     n = zh.shape[0] // 2
     width = n // z_parts
     groups = LANES // width
-    slots = near_ref.shape[1] // (2 * channels * n)
-    last = ligand_ref.shape[0]
+    slots = near_own_ref.shape[1] // (2 * channels * n)
+    pairs = ligand_ref.shape[1] + 1
     special = place_ref[0] == 0
-    copies = [pltpu.make_async_copy(far_ref.at[i], ligand_ref.at[i], sems.at[i]) for i in range(last)]
+    copies = [
+        pltpu.make_async_copy(far.at[i], ligand_ref.at[k, i], sems.at[k, i])
+        for k, far in enumerate((far_own_ref, far_other_ref))
+        for i in range(pairs - 1)
+    ]
     for copy in copies:
         copy.start()
     receptor = receptor_spectrum(special, blocks_ref, zh, zr, yb, channels, y_parts, z_parts)
     for copy in copies:
         copy.wait()
-
-    for step in range(last + 1):
-        ligand = near_ref if step == last else ligand_ref.at[step]
-        columns = []
-        for rotation in range(2):
-            for slot in range(slots):
+    own = place_ref[0] // (y_parts * z_parts)
+
+    for step in range(2 * pairs):
+        k, pair = divmod(step, pairs)
+        near_ref = (near_own_ref, near_other_ref)[k]
+        ligand = near_ref if pair == pairs - 1 else ligand_ref.at[k, pair]
+        device = (1 - own if k else own) * y_parts * z_parts
+        for slot in range(slots):
+            columns = []
+            for rotation in range(2):
                 real, imag = 0.0, 0.0
                 for channel in range(channels):
                     f = receptor[channel * (slots + 1) + (rotation if slot == 0 else slot + 1)]
@@ -242,23 +276,20 @@
                     real = real + (fr * hr + fi * hi)
                     imag = imag + (fr * hi - fi * hr)
                 columns.append(jnp.concatenate([real, imag], axis=0))
-        columns = constant_times(yb, columns)
-        rows = jnp.concatenate([jnp.concatenate([c[:n], c[n:]], axis=1) for c in columns], axis=0)
-        rows = times_constant(rows, zh, zr)
-        maps = []
-        for i in range(2 * slots):
-            both = rows[i * n : (i + 1) * n]
-            maps += [both[:, :n], both[:, n:]]
-        lone, other = maps[1], maps[2 * slots]
-        maps[1], maps[2 * slots] = jnp.where(special, other, lone), jnp.where(special, lone, other)
-        for i, plane in enumerate(maps):
-            rotation, component = divmod(i, 2 * slots)
-            row = (step * 2 * slots + component) * SUBLANES
-            for y_part in range(y_parts):
-                first = y_part * groups
-                pieces = [plane[(first + g) * SUBLANES : (first + g + 1) * SUBLANES] for g in range(groups)]
-                for z_part, block in enumerate(swap_groups(pieces, width)):
-                    out_ref[(rotation * y_parts + y_part) * z_parts + z_part, row : row + SUBLANES] = block
+            columns = constant_times(yb, columns)
+            rows = jnp.concatenate([jnp.concatenate([c[:n], c[n:]], axis=1) for c in columns], axis=0)
+            rows = times_constant(rows, zh, zr)
+            maps = [rows[:n, :n], rows[:n, n:], rows[n:, :n], rows[n:, n:]]
+            if slot == 0:
+                maps[1], maps[2] = jnp.where(special, maps[2], maps[1]), jnp.where(special, maps[1], maps[2])
+            for i, plane in enumerate(maps):
+                rotation, part = divmod(i, 2)
+                row = (((2 * pair + rotation) * slots + slot) * 2 + part) * SUBLANES
+                for y_part in range(y_parts):
+                    first = y_part * groups
+                    pieces = [plane[(first + g) * SUBLANES : (first + g + 1) * SUBLANES] for g in range(groups)]
+                    for z_part, block in enumerate(swap_groups(pieces, width)):
+                        out_ref[device + y_part * z_parts + z_part, row : row + SUBLANES] = block
 
 
 def inverse_x_kernel(blocks_ref, matrix_ref, out_ref, best_ref, rows_ref, held_ref, sems):
@@ -298,13 +329,6 @@
     return pl.BlockSpec(memory_space=pltpu.SMEM)
 
 
-def component_tables(n, comps):
-    matrix = forward_x_matrix(n).reshape(n // comps, comps, n)
-    head, rest = split_constant(matrix)
-    last = (matrix - head.astype(np.float64) - rest.astype(np.float64)).astype(jnp.bfloat16)
-    return np.concatenate([head, rest, last, np.zeros_like(head)], axis=1)
-
-
 def on_device(receptor_grids, ligand_cells, atom_shape, atom_charges, *, sizes):
     n = receptor_grids.shape[1]
     rots, y_parts, z_parts = (sizes[a] for a in AXES)
@@ -333,38 +357,33 @@
     blocks = lax.all_to_all(components.reshape(devices, rows, LANES), AXES, 0, 0, tiled=True)
 
     width = 2 * slots * channels * n
-    slabs = max(rotations, VMEM_BYTES // (2 * n * width * 4))
-    far_ligand, near_ligand = pl.pallas_call(
+    pairs = rotations // 2
+    slabs = max(pairs, VMEM_BYTES // (2 * n * width * 4))
+    ligand = pl.pallas_call(
         ligand_kernel,
-        grid=(rotations,),
+        grid=(pairs,),
         out_shape=[
             jax.ShapeDtypeStruct((slabs, 2 * n, width), f32),
             jax.ShapeDtypeStruct((2 * n, width), f32),
         ],
-        in_specs=[scalars()] + [whole()] * 8,
+        in_specs=[scalars()] + [whole()] * 6,
         out_specs=[far(), whole()],
-        scratch_shapes=[pltpu.VMEM((rotations - 1, 2 * n, width), f32), pltpu.SemaphoreType.DMA((rotations - 1,))],
+        scratch_shapes=[pltpu.VMEM((pairs - 1, 2 * n, width), f32), pltpu.SemaphoreType.DMA((pairs - 1,))],
         compiler_params=room(24),
         name="ligand",
-    )(
-        place,
-        ligand_cells,
-        other,
-        atom_shape.reshape(1, atoms),
-        atom_charges.reshape(1, atoms),
-        jnp.asarray(component_tables(n, comps)),
-        *matrices,
     )
+    weights = (atom_shape.reshape(1, atoms), atom_charges.reshape(1, atoms))
+    spectra = (*ligand(place, ligand_cells, *weights, *matrices), *ligand(place, other, *weights, *matrices))
 
     sent = pl.pallas_call(
         functools.partial(product_kernel, channels=channels, y_parts=y_parts, z_parts=z_parts),
         out_shape=jax.ShapeDtypeStruct((devices, rotations * rows, LANES), f32),
-        in_specs=[scalars(), whole(), far()] + [whole()] * 4,
+        in_specs=[scalars(), whole(), far(), whole(), far()] + [whole()] * 4,
         out_specs=whole(),
-        scratch_shapes=[pltpu.VMEM((rotations - 1, 2 * n, width), f32), pltpu.SemaphoreType.DMA((rotations - 1,))],
+        scratch_shapes=[pltpu.VMEM((2, pairs - 1, 2 * n, width), f32), pltpu.SemaphoreType.DMA((2, pairs - 1))],
         compiler_params=room(16),
         name="product",
-    )(place, blocks, far_ligand, near_ligand, *matrices)
+    )(place, blocks, *spectra, *matrices)
     head, rest = split_constant(inverse_x_matrix(n))
     got = lax.all_to_all(sent, AXES, 0, 0, tiled=True)
 
@@ -480,6 +499,7 @@
         fits = (
             sizes["rot"] == 2
             and n == LANES
+            and ligand_cells.shape[0] % 4 == 0
             and (n // 2) % devices == 0
             and (n // sizes["py"]) * (n // sizes["pz"]) == SUBLANES * LANES
             and all(sizes[a] & (sizes[a] - 1) == 0 for a in AXES)

time: 105 us -> 99.4 us (0.947)
  waiting for transfers between devices: 12.4 us -> 8.1 us
    ppermute x1, waiting for transfers between devices: 4.33 us -> 0.01 us  [on_device(): other = lax.ppermute(cells, 'rot', [(i, i ^ 1) for i in range(rots)])]
    pallas_call x1 -> x2, Pallas kernels: 13.8 us -> 13.2 us  [the longest x1 6.62 us: on_device(): ligand(place, ligand_cells, *weights, *matrices)]
  transfers between devices with their start and end apart: 6 -> 6, of which waited for: 5 -> 4; matrix products, arithmetic and copies ran while one was open for 0% -> 0% of each run, Pallas kernels for 13% -> 13%
where the time goes in v6:
time: 99.4 us; the launch traced here: 99.1 us
  blocking collectives  51.8 us (52%)
  Pallas kernels  22.6 us (23%)
  starting transfers between devices  15.2 us (15%)
  waiting for transfers between devices  8.1 us (8%)
    all_to_all x1, blocking collectives, on_device(): got = lax.all_to_all(sent, AXES, 0, 0, tiled=True)  51.8 us
    ppermute x4, waiting for transfers between devices, on_device(): lax.ppermute(best, axis, [(i, i ^ step) for i in range(sizes[axis])])  8.1 us
    all_to_all x1, starting transfers between devices, on_device(): lax.all_to_all(components.reshape(devices, rows, LANES), AXES, 0, 0, tile...  7.32 us
    pallas_call x1, Pallas kernels, on_device(): ligand(place, ligand_cells, *weights, *matrices)  6.62 us
    pallas_call x1, Pallas kernels, on_device(): ligand(place, other, *weights, *matrices)  6.62 us
    ppermute x4, starting transfers between devices, on_device(): lax.ppermute(best, axis, [(i, i ^ step) for i in range(sizes[axis])])  6.05 us
    pallas_call x1, Pallas kernels, on_device(): pl.pallas_call(functools.partial(product_kernel, channels=channels, y_par...  4.42 us
    pallas_call x1, Pallas kernels, on_device(): pl.pallas_call(forward_x_kernel, out_shape=jax.ShapeDtypeStruct((n * SUBL...  2.57 us
  transfers between devices with their start and end apart: 6, of which 4 were waited for; matrix products, arithmetic and copies ran while one was open for 0% of the time, Pallas kernels for 13%

profile of v6, /device:TPU:0, one launch (start us, length us, event | category | flops | bytes accessed | tf_op | source)
XLA Modules:
  0.0 99.1 jit_solution(5732632196549950345)
XLA Ops:
  0.6 0.0 copy-start
  0.6 0.0 copy-start.1
  0.7 0.0 copy-start.2
  0.7 0.0 copy-start.4
  0.7 0.0 copy-start.6
  0.7 0.0 copy-start.5
  0.7 2.6 %forward_x.1 = f32[1024,128]{1,0:T(8,128)} custom-call(f32[1,32,32,128]{3,2,1,0:T(8,128)} %bitcast.10, bf16[128,128]{1,0:T(8,128)(2,1)} %constant.32.clone.head_ref, bf16[128,128]{1,0:T(8,128)(2,1)} %constant.33.clone.rest_ref), custom_call_target="tpu_custom_call" | custom-call | tf_op jit(solution)/shard_map/forward_x/pallas_call | solution.py:347
  3.3 7.3 %all-to-all-start = ((f32[32,32,128]{2,1,0:T(8,128)}), f32[32,32,128]{2,1,0:T(8,128)S(1)}, u32[]{:S(2)}, u32[]{:S(2)}) async-start(f32[32,32,128]{2,1,0:T(8,128)} %bitcast.9), calls=%async_computation | async-start | bytes 1048576 | tf_op jit(solution)/shard_map/all_to_all | solution.py:357
  10.6 0.0 copy-done.4
  10.6 1.8 %collective-permute-start = (s32[4,2048]{1,0:T(4,128)S(1)}, s32[4,2048]{1,0:T(4,128)S(1)}, u32[]{:S(2)}, u32[]{:S(2)}) collective-permute-start(s32[4,2048]{1,0:T(4,128)S(1)} %copy-done.4), channel_id=1, source_target_pairs={{0,16},{16,0},{1,17},{17,1},{2,18},{18,2},{3,19},{19,3},{4,20},{20... | collective-permute-start | bytes 98312 | tf_op jit(solution)/shard_map/ppermute | solution.py:356
  12.4 0.0 copy-done
  12.4 0.0 copy-done.1
  12.5 0.0 copy-done.2
  12.5 0.0 copy-done.6
  12.5 0.0 copy-done.5
  12.5 6.6 %ligand.2 = (f32[48,256,1024]{2,1,0:T(8,128)}, f32[256,1024]{1,0:T(8,128)S(1)}) custom-call(s32[1]{0:T(128)} %bitcast.place_ref, s32[4,2048]{1,0:T(4,128)S(1)} %copy-done.4, f32[1,2048]{1,0:T(1,128)S(1)} %bitcast.5, f32[1,2048]{1,0:T(1,128)S(1)} %bitcast.7, bf16[256,256]{1,0:T(8,128)(2,1)S(1)} %copy-done.2, bf16[256,256]{1,0:T(8,128)(2,1)S(1)} %copy-done.1, ...), custom_call_target="tpu_custom_call" | custom-call | tf_op jit(solution)/shard_map/ligand/pallas_call | solution.py:376
  19.1 0.0 collective-permute-done.cells_ref
  19.1 6.6 %ligand.3 = (f32[48,256,1024]{2,1,0:T(8,128)}, f32[256,1024]{1,0:T(8,128)S(1)}) custom-call(s32[1]{0:T(128)} %bitcast.place_ref, s32[4,2048]{1,0:T(4,128)S(1)} %collective-permute-done.cells_ref, f32[1,2048]{1,0:T(1,128)S(1)} %bitcast.6, f32[1,2048]{1,0:T(1,128)S(1)} %bitcast.8, bf16[256,256]{1,0:T(8,128)(2,1)S(1)} %copy-done.2, ...), custom_call_target="tpu_custom_call" | custom-call | tf_op jit(solution)/shard_map/ligand/pallas_call | solution.py:376
  25.7 0.0 all-to-all-done.blocks_ref
  25.7 4.4 %product.1 = f32[32,128,128]{2,1,0:T(8,128)S(1)} custom-call(s32[1]{0:T(128)} %bitcast.place_ref, f32[32,32,128]{2,1,0:T(8,128)S(1)} %all-to-all-done.blocks_ref, f32[48,256,1024]{2,1,0:T(8,128)} %get-tuple-element.11.far_own_ref, f32[256,1024]{1,0:T(8,128)S(1)} %get-tuple-element.12.near_own_ref, f32[48,256,1024]{2,1,0:T(8,128)} %get-tuple-element.14.far_other_ref, ...), custom_call_target="tpu_custom_call" | custom-call | tf_op jit(solution)/shard_map/product/pallas_call | solution.py:378
  30.2 0.0 copy-start.3
  30.2 51.8 %all_to_all.10.blocks_ref = f32[32,128,128]{2,1,0:T(8,128)S(1)} all-to-all(f32[32,128,128]{2,1,0:T(8,128)S(1)} %product.1), channel_id=1, replica_groups=mesh['rot'=2,'py'=4,'pz'=4] {'rot','py','pz'}, dimensions={0} | all-to-all | bytes 4194304 | tf_op jit(solution)/shard_map/all_to_all | solution.py:388
  82.0 2.4 %inverse_x.1 = (f32[4,32,32,128]{3,2,1,0:T(8,128)}, f32[4]{0:T(128)S(1)}) custom-call(f32[32,128,128]{2,1,0:T(8,128)S(1)} %all_to_all.10.blocks_ref, bf16[256,256]{1,0:T(8,128)(2,1)S(1)} %copy-done.3), custom_call_target="tpu_custom_call" | custom-call | tf_op jit(solution)/shard_map/inverse_x/pallas_call | solution.py:390
  84.4 1.7 %collective-permute-start.1 = (f32[4]{0:T(128)S(1)}, f32[4]{0:T(128)S(1)}, u32[]{:S(2)}, u32[]{:S(2)}) collective-permute-start(f32[4]{0:T(128)S(1)} %get-tuple-element.17), channel_id=1, source_target_pairs={{0,4},{4,0},{8,12},{12,8},{1,5},{5,1},{9,13},{13,9},{2,6},{6,2},{1... | collective-permute-start | bytes 56 | tf_op jit(solution)/shard_map/ppermute | solution.py:409
  86.1 0.8 collective-permute-done.1
  87.0 1.5 %collective-permute-start.2 = (f32[4]{0:T(128)S(1)}, f32[4]{0:T(128)S(1)}, u32[]{:S(2)}, u32[]{:S(2)}) collective-permute-start(f32[4]{0:T(128)S(1)} %max.12), channel_id=1, source_target_pairs={{0,8},{4,12},{8,0},{12,4},{1,9},{5,13},{9,1},{13,5},{2,10},{6,14},... | collective-permute-start | bytes 56 | tf_op jit(solution)/shard_map/ppermute | solution.py:409
  88.4 2.1 %collective-permute-done.2 = f32[4]{0:T(128)S(1)} collective-permute-done((f32[4]{0:T(128)S(1)}, f32[4]{0:T(128)S(1)}, u32[]{:S(2)}, u32[]{:S(2)}) %collective-permute-start.2) | collective-permute-done | bytes 48 | tf_op jit(solution)/shard_map/ppermute | solution.py:409
  90.5 1.8 %collective-permute-start.3 = (f32[4]{0:T(128)S(1)}, f32[4]{0:T(128)S(1)}, u32[]{:S(2)}, u32[]{:S(2)}) collective-permute-start(f32[4]{0:T(128)S(1)} %max.13), channel_id=1, source_target_pairs={{0,1},{1,0},{2,3},{3,2},{4,5},{5,4},{6,7},{7,6},{8,9},{9,8},{10,11... | collective-permute-start | bytes 56 | tf_op jit(solution)/shard_map/ppermute | solution.py:409
  92.3 1.8 %collective-permute-done.3 = f32[4]{0:T(128)S(1)} collective-permute-done((f32[4]{0:T(128)S(1)}, f32[4]{0:T(128)S(1)}, u32[]{:S(2)}, u32[]{:S(2)}) %collective-permute-start.3) | collective-permute-done | bytes 48 | tf_op jit(solution)/shard_map/ppermute | solution.py:409
  94.1 1.1 %collective-permute-start.4 = (f32[4]{0:T(128)S(1)}, f32[4]{0:T(128)S(1)}, u32[]{:S(2)}, u32[]{:S(2)}) collective-permute-start(f32[4]{0:T(128)S(1)} %max.14), channel_id=1, source_target_pairs={{0,2},{1,3},{2,0},{3,1},{4,6},{5,7},{6,4},{7,5},{8,10},{9,11},{10,... | collective-permute-start | bytes 56 | tf_op jit(solution)/shard_map/ppermute | solution.py:409
  95.1 3.4 %collective-permute-done.4 = f32[4]{0:T(128)S(1)} collective-permute-done((f32[4]{0:T(128)S(1)}, f32[4]{0:T(128)S(1)}, u32[]{:S(2)}, u32[]{:S(2)}) %collective-permute-start.4) | collective-permute-done | bytes 48 | tf_op jit(solution)/shard_map/ppermute | solution.py:409
  98.6 0.5 max.15
  (4 shorter events, 0.0 us)
Async XLA Ops:
  0.6 11.8 %copy-start = (bf16[512,256]{1,0:T(8,128)(2,1)S(1)}, bf16[512,256]{1,0:T(8,128)(2,1)}, u32[]{:S(2)}) copy-start(bf16[512,256]{1,0:T(8,128)(2,1)} %constant.31.clone.yb) | copy-start | bytes 786436
  0.6 11.8 %copy-start.1 = (bf16[256,256]{1,0:T(8,128)(2,1)S(1)}, bf16[256,256]{1,0:T(8,128)(2,1)}, u32[]{:S(2)}) copy-start(bf16[256,256]{1,0:T(8,128)(2,1)} %constant.30.clone.zr) | copy-start | bytes 393220
  0.7 11.8 %copy-start.2 = (bf16[256,256]{1,0:T(8,128)(2,1)S(1)}, bf16[256,256]{1,0:T(8,128)(2,1)}, u32[]{:S(2)}) copy-start(bf16[256,256]{1,0:T(8,128)(2,1)} %constant.29.clone.zh) | copy-start | bytes 393220
  0.7 9.9 %copy-start.4 = (s32[4,2048]{1,0:T(4,128)S(1)}, s32[4,2048]{1,0:T(4,128)}, u32[]{:S(2)}) copy-start(s32[4,2048]{1,0:T(4,128)} %cells_ref.1) | copy-start | bytes 98308
  0.7 11.8 %copy-start.6 = (f32[2048]{0:T(1024)S(1)}, f32[2048]{0:T(1024)}, u32[]{:S(2)}) copy-start(f32[2048]{0:T(1024)} %param.13) | copy-start | bytes 24580
  0.7 11.8 %copy-start.5 = (f32[2048]{0:T(1024)S(1)}, f32[2048]{0:T(1024)}, u32[]{:S(2)}) copy-start(f32[2048]{0:T(1024)} %param.12) | copy-start | bytes 24580
  3.3 22.5 %all-to-all-start = ((f32[32,32,128]{2,1,0:T(8,128)}), f32[32,32,128]{2,1,0:T(8,128)S(1)}, u32[]{:S(2)}, u32[]{:S(2)}) async-start(f32[32,32,128]{2,1,0:T(8,128)} %bitcast.9), calls=%async_computation | async-start | bytes 1048576 | tf_op jit(solution)/shard_map/all_to_all | solution.py:357
  10.6 8.5 %collective-permute-start = (s32[4,2048]{1,0:T(4,128)S(1)}, s32[4,2048]{1,0:T(4,128)S(1)}, u32[]{:S(2)}, u32[]{:S(2)}) collective-permute-start(s32[4,2048]{1,0:T(4,128)S(1)} %copy-done.4), channel_id=1, source_target_pairs={{0,16},{16,0},{1,17},{17,1},{2,18},{18,2},{3,19},{19,3},{4,20},{20... | collective-permute-start | bytes 98312 | tf_op jit(solution)/shard_map/ppermute | solution.py:356
  30.2 51.9 %copy-start.3 = (bf16[256,256]{1,0:T(8,128)(2,1)S(1)}, bf16[256,256]{1,0:T(8,128)(2,1)}, u32[]{:S(2)}) copy-start(bf16[256,256]{1,0:T(8,128)(2,1)} %constant.34.clone.matrix_ref) | copy-start | bytes 393220
  84.4 2.5 %collective-permute-start.1 = (f32[4]{0:T(128)S(1)}, f32[4]{0:T(128)S(1)}, u32[]{:S(2)}, u32[]{:S(2)}) collective-permute-start(f32[4]{0:T(128)S(1)} %get-tuple-element.17), channel_id=1, source_target_pairs={{0,4},{4,0},{8,12},{12,8},{1,5},{5,1},{9,13},{13,9},{2,6},{6,2},{1... | collective-permute-start | bytes 56 | tf_op jit(solution)/shard_map/ppermute | solution.py:409
  87.0 3.6 %collective-permute-start.2 = (f32[4]{0:T(128)S(1)}, f32[4]{0:T(128)S(1)}, u32[]{:S(2)}, u32[]{:S(2)}) collective-permute-start(f32[4]{0:T(128)S(1)} %max.12), channel_id=1, source_target_pairs={{0,8},{4,12},{8,0},{12,4},{1,9},{5,13},{9,1},{13,5},{2,10},{6,14},... | collective-permute-start | bytes 56 | tf_op jit(solution)/shard_map/ppermute | solution.py:409
  90.5 3.6 %collective-permute-start.3 = (f32[4]{0:T(128)S(1)}, f32[4]{0:T(128)S(1)}, u32[]{:S(2)}, u32[]{:S(2)}) collective-permute-start(f32[4]{0:T(128)S(1)} %max.13), channel_id=1, source_target_pairs={{0,1},{1,0},{2,3},{3,2},{4,5},{5,4},{6,7},{7,6},{8,9},{9,8},{10,11... | collective-permute-start | bytes 56 | tf_op jit(solution)/shard_map/ppermute | solution.py:409
  94.1 4.5 %collective-permute-start.4 = (f32[4]{0:T(128)S(1)}, f32[4]{0:T(128)S(1)}, u32[]{:S(2)}, u32[]{:S(2)}) collective-permute-start(f32[4]{0:T(128)S(1)} %max.14), channel_id=1, source_target_pairs={{0,2},{1,3},{2,0},{3,1},{4,6},{5,7},{6,4},{7,5},{8,10},{9,11},{10,... | collective-permute-start | bytes 56 | tf_op jit(solution)/shard_map/ppermute | solution.py:409

commit v7 on v6

--- a/solution.py
+++ b/solution.py
@@ -98,16 +98,15 @@
     return pieces
 
 
-def forward_x_kernel(grid_ref, head_ref, rest_ref, out_ref):
+def forward_x_kernel(grid_ref, both_ref, out_ref):
     y_block, z_block, n = grid_ref.shape[1:]
     groups = LANES // z_block
     high = y_block // groups
     for row in range(high):
         values = jnp.concatenate([grid_ref[0, g * high + row] for g in range(groups)], axis=0)
         head, rest = split(values)
-        out_ref[pl.ds(row, n, stride=high), :] = dot_rows(head_ref[...], head) + (
-            dot_rows(rest_ref[...], head) + dot_rows(head_ref[...], rest)
-        )
+        both = dot_rows(both_ref[...], head)
+        out_ref[pl.ds(row, n, stride=high), :] = both[:n] + (both[n:] + dot_rows(both_ref[:n], rest))
 
 
 def one_hot_rows(count, place):
@@ -142,62 +141,60 @@
     half = n // 2
     atoms = cells_ref.shape[1]
     comps = near_ref.shape[1] // (2 * n)
-    step = pl.program_id(0)
+    last = held_ref.shape[0]
+    copies = [pltpu.make_async_copy(held_ref.at[i], far_ref.at[i], sems.at[i]) for i in range(last)]
     row = lax.broadcasted_iota(jnp.int32, (comps, 1), 0)
     slot = place_ref[0] * (comps // 2) + row // 2
     second = row % 2 == 1
     times = jnp.where(second & (slot == 0), half, slot)
     shift = jnp.where(second & (slot != 0), n - n // 4, 0)
     special = place_ref[0] == 0
-    grids = []
-    for rotation in range(2):
-        cell = cells_ref[pl.ds(2 * step + rotation, 1), :]
-        coord_x, coord_y, coord_z = cell // (n * n), cell // n % n, cell % n
-        wave = cosine(times * coord_x + shift, n)
-        values = jnp.concatenate([wave * shape_ref[...], wave * charge_ref[...]], axis=0)
-        count = values.shape[0]
-        head = values.astype(jnp.bfloat16).astype(jnp.float32)
-        hit = lax.broadcasted_iota(jnp.int32, (half, atoms), 0) == coord_y % half
-        stacked = jnp.concatenate(
-            [
-                jnp.where(hit, part[c : c + 1, :], 0.0).astype(jnp.bfloat16)
-                for part in (head, values - head)
-                for c in range(count)
-            ],
-            axis=0,
-        )
-        total = dot_rows(stacked, one_hot_rows(2 * n, coord_z + n * (coord_y // half)))
-        total = total[: count * half] + total[count * half :]
-        grids.append(
-            [
-                jnp.concatenate(
-                    [total[c * half : (c + 1) * half, :n], total[c * half : (c + 1) * half, n:]], axis=0
+    for step in range(last + 1):
+        grids = []
+        for rotation in range(2):
+            cell = cells_ref[2 * step + rotation : 2 * step + rotation + 1, :]
+            coord_x, coord_y, coord_z = cell // (n * n), cell // n % n, cell % n
+            wave = cosine(times * coord_x + shift, n)
+            values = jnp.concatenate([wave * shape_ref[...], wave * charge_ref[...]], axis=0)
+            count = values.shape[0]
+            head = values.astype(jnp.bfloat16).astype(jnp.float32)
+            hit = lax.broadcasted_iota(jnp.int32, (half, atoms), 0) == coord_y % half
+            stacked = jnp.concatenate(
+                [
+                    jnp.where(hit, part[c : c + 1, :], 0.0).astype(jnp.bfloat16)
+                    for part in (head, values - head)
+                    for c in range(count)
+                ],
+                axis=0,
+            )
+            total = dot_rows(stacked, one_hot_rows(2 * n, coord_z + n * (coord_y // half)))
+            total = total[: count * half] + total[count * half :]
+            grids.append(
+                [
+                    jnp.concatenate(
+                        [total[c * half : (c + 1) * half, :n], total[c * half : (c + 1) * half, n:]], axis=0
+                    )
+                    for c in range(count)
+                ]
+            )
+        planes = [[], []]
+        for c in range(0, count, 2):
+            first, second = (grids[0][c], grids[0][c + 1]), (grids[1][c], grids[1][c + 1])
+            if c % comps == 0:
+                first, second = (
+                    (first[0], jnp.where(special, second[0], first[1])),
+                    (jnp.where(special, first[1], second[0]), second[1]),
                 )
-                for c in range(count)
-            ]
-        )
-    planes = [[], []]
-    for c in range(0, count, 2):
-        first, second = (grids[0][c], grids[0][c + 1]), (grids[1][c], grids[1][c + 1])
-        if c % comps == 0:
-            first, second = (
-                (first[0], jnp.where(special, second[0], first[1])),
-                (jnp.where(special, first[1], second[0]), second[1]),
-            )
-        planes[0].append(first)
-        planes[1].append(second)
-    near_ref[...] = jnp.concatenate(spectrum(planes[0] + planes[1], n, zh, zr, yb, 2), axis=1)
-    last = pl.num_programs(0) - 1
-
-    @pl.when(step < last)
-    def _():
-        held_ref[step] = near_ref[...]
-        pltpu.make_async_copy(held_ref.at[step], far_ref.at[step], sems.at[step]).start()
-
-    @pl.when(step == last)
-    def _():
-        for i in range(held_ref.shape[0]):
-            pltpu.make_async_copy(held_ref.at[i], far_ref.at[i], sems.at[i]).wait()
+            planes[0].append(first)
+            planes[1].append(second)
+        spectra = jnp.concatenate(spectrum(planes[0] + planes[1], n, zh, zr, yb, 2), axis=1)
+        if step == last:
+            near_ref[...] = spectra
+        else:
+            held_ref[step] = spectra
+            copies[step].start()
+    for copy in copies:
+        copy.wait()
 
 
 def receptor_spectrum(special, blocks_ref, zh, zr, yb, channels, y_parts, z_parts):
@@ -347,11 +344,11 @@
     components = pl.pallas_call(
         forward_x_kernel,
         out_shape=jax.ShapeDtypeStruct((n * SUBLANES, LANES), f32),
-        in_specs=[whole()] * 3,
+        in_specs=[whole()] * 2,
         out_specs=whole(),
         compiler_params=room(60),
         name="forward_x",
-    )(jnp.transpose(receptor_grids, (0, 2, 3, 1)), *(jnp.asarray(m) for m in split_constant(forward_x_matrix(n))))
+    )(jnp.transpose(receptor_grids, (0, 2, 3, 1)), jnp.asarray(np.concatenate(split_constant(forward_x_matrix(n)), axis=0)))
     components, cells = lax.optimization_barrier((components, ligand_cells))
     other = lax.ppermute(cells, "rot", [(i, i ^ 1) for i in range(rots)])
     blocks = lax.all_to_all(components.reshape(devices, rows, LANES), AXES, 0, 0, tiled=True)
@@ -361,7 +358,6 @@
     slabs = max(pairs, VMEM_BYTES // (2 * n * width * 4))
     ligand = pl.pallas_call(
         ligand_kernel,
-        grid=(pairs,),
         out_shape=[
             jax.ShapeDtypeStruct((slabs, 2 * n, width), f32),
             jax.ShapeDtypeStruct((2 * n, width), f32),

time: 99.4 us -> 98.7 us (level)
  no operation moved by 1% of the time
where the time goes in v7:
time: 98.7 us; the launch traced here: 98.4 us
  blocking collectives  51.8 us (52%)
  Pallas kernels  22 us (22%)
  starting transfers between devices  15.2 us (15%)
  waiting for transfers between devices  8.09 us (8%)
    all_to_all x1, blocking collectives, on_device(): got = lax.all_to_all(sent, AXES, 0, 0, tiled=True)  51.8 us
    ppermute x4, waiting for transfers between devices, on_device(): lax.ppermute(best, axis, [(i, i ^ step) for i in range(sizes[axis])])  8.09 us
    all_to_all x1, starting transfers between devices, on_device(): lax.all_to_all(components.reshape(devices, rows, LANES), AXES, 0, 0, tile...  7.32 us
    pallas_call x1, Pallas kernels, on_device(): ligand(place, other, *weights, *matrices)  6.31 us
    pallas_call x1, Pallas kernels, on_device(): ligand(place, ligand_cells, *weights, *matrices)  6.31 us
    ppermute x4, starting transfers between devices, on_device(): lax.ppermute(best, axis, [(i, i ^ step) for i in range(sizes[axis])])  6.05 us
    pallas_call x1, Pallas kernels, on_device(): pl.pallas_call(functools.partial(product_kernel, channels=channels, y_par...  4.61 us
    pallas_call x1, Pallas kernels, on_device(): pl.pallas_call(inverse_x_kernel, out_shape=[jax.ShapeDtypeStruct((rotatio...  2.37 us
  transfers between devices with their start and end apart: 6, of which 4 were waited for; matrix products, arithmetic and copies ran while one was open for 0% of the time, Pallas kernels for 13%

profile of v7, /device:TPU:0, one launch (start us, length us, event | category | flops | bytes accessed | tf_op | source)
XLA Modules:
  0.0 98.4 jit_solution(15357388613890506622)
XLA Ops:
  0.6 0.0 copy-start
  0.6 0.0 copy-start.1
  0.7 0.0 copy-start.2
  0.7 0.0 copy-start.4
  0.7 0.0 copy-start.6
  0.7 0.0 copy-start.5
  0.7 2.4 %forward_x.1 = f32[1024,128]{1,0:T(8,128)} custom-call(f32[1,32,32,128]{3,2,1,0:T(8,128)} %bitcast.10, bf16[256,128]{1,0:T(8,128)(2,1)} %constant.30.clone.both_ref), custom_call_target="tpu_custom_call" | custom-call | tf_op jit(solution)/shard_map/forward_x/pallas_call | solution.py:344
  3.1 7.3 %all-to-all-start = ((f32[32,32,128]{2,1,0:T(8,128)}), f32[32,32,128]{2,1,0:T(8,128)S(1)}, u32[]{:S(2)}, u32[]{:S(2)}) async-start(f32[32,32,128]{2,1,0:T(8,128)} %bitcast.9), calls=%async_computation | async-start | bytes 1048576 | tf_op jit(solution)/shard_map/all_to_all | solution.py:354
  10.4 0.0 copy-done.4
  10.4 1.8 %collective-permute-start = (s32[4,2048]{1,0:T(4,128)S(1)}, s32[4,2048]{1,0:T(4,128)S(1)}, u32[]{:S(2)}, u32[]{:S(2)}) collective-permute-start(s32[4,2048]{1,0:T(4,128)S(1)} %copy-done.4), channel_id=1, source_target_pairs={{0,16},{16,0},{1,17},{17,1},{2,18},{18,2},{3,19},{19,3},{4,20},{20... | collective-permute-start | bytes 98312 | tf_op jit(solution)/shard_map/ppermute | solution.py:353
  12.2 0.0 copy-done
  12.2 0.0 copy-done.1
  12.2 0.0 copy-done.2
  12.2 0.0 copy-done.6
  12.3 0.0 copy-done.5
  12.3 6.3 %ligand.2 = (f32[48,256,1024]{2,1,0:T(8,128)}, f32[256,1024]{1,0:T(8,128)S(1)}) custom-call(s32[1]{0:T(128)} %bitcast.place_ref, s32[4,2048]{1,0:T(4,128)S(1)} %copy-done.4, f32[1,2048]{1,0:T(1,128)S(1)} %bitcast.5, f32[1,2048]{1,0:T(1,128)S(1)} %bitcast.7, bf16[256,256]{1,0:T(8,128)(2,1)S(1)} %copy-done.2, bf16[256,256]{1,0:T(8,128)(2,1)S(1)} %copy-done.1, ...), custom_call_target="tpu_custom_call" | custom-call | tf_op jit(solution)/shard_map/ligand/pallas_call | solution.py:372
  18.6 0.0 collective-permute-done.cells_ref
  18.6 6.3 %ligand.3 = (f32[48,256,1024]{2,1,0:T(8,128)}, f32[256,1024]{1,0:T(8,128)S(1)}) custom-call(s32[1]{0:T(128)} %bitcast.place_ref, s32[4,2048]{1,0:T(4,128)S(1)} %collective-permute-done.cells_ref, f32[1,2048]{1,0:T(1,128)S(1)} %bitcast.6, f32[1,2048]{1,0:T(1,128)S(1)} %bitcast.8, bf16[256,256]{1,0:T(8,128)(2,1)S(1)} %copy-done.2, ...), custom_call_target="tpu_custom_call" | custom-call | tf_op jit(solution)/shard_map/ligand/pallas_call | solution.py:372
  24.9 0.0 all-to-all-done.blocks_ref
  24.9 4.6 %product.1 = f32[32,128,128]{2,1,0:T(8,128)S(1)} custom-call(s32[1]{0:T(128)} %bitcast.place_ref, f32[32,32,128]{2,1,0:T(8,128)S(1)} %all-to-all-done.blocks_ref, f32[48,256,1024]{2,1,0:T(8,128)} %get-tuple-element.11.far_own_ref, f32[256,1024]{1,0:T(8,128)S(1)} %get-tuple-element.12.near_own_ref, f32[48,256,1024]{2,1,0:T(8,128)} %get-tuple-element.14.far_other_ref, ...), custom_call_target="tpu_custom_call" | custom-call | tf_op jit(solution)/shard_map/product/pallas_call | solution.py:374
  29.5 0.0 copy-start.3
  29.6 51.8 %all_to_all.10.blocks_ref = f32[32,128,128]{2,1,0:T(8,128)S(1)} all-to-all(f32[32,128,128]{2,1,0:T(8,128)S(1)} %product.1), channel_id=1, replica_groups=mesh['rot'=2,'py'=4,'pz'=4] {'rot','py','pz'}, dimensions={0} | all-to-all | bytes 4194304 | tf_op jit(solution)/shard_map/all_to_all | solution.py:384
  81.4 2.4 %inverse_x.1 = (f32[4,32,32,128]{3,2,1,0:T(8,128)}, f32[4]{0:T(128)S(1)}) custom-call(f32[32,128,128]{2,1,0:T(8,128)S(1)} %all_to_all.10.blocks_ref, bf16[256,256]{1,0:T(8,128)(2,1)S(1)} %copy-done.3), custom_call_target="tpu_custom_call" | custom-call | tf_op jit(solution)/shard_map/inverse_x/pallas_call | solution.py:386
  83.8 1.7 %collective-permute-start.1 = (f32[4]{0:T(128)S(1)}, f32[4]{0:T(128)S(1)}, u32[]{:S(2)}, u32[]{:S(2)}) collective-permute-start(f32[4]{0:T(128)S(1)} %get-tuple-element.17), channel_id=1, source_target_pairs={{0,4},{4,0},{8,12},{12,8},{1,5},{5,1},{9,13},{13,9},{2,6},{6,2},{1... | collective-permute-start | bytes 56 | tf_op jit(solution)/shard_map/ppermute | solution.py:405
  85.5 0.8 collective-permute-done.1
  86.3 1.5 %collective-permute-start.2 = (f32[4]{0:T(128)S(1)}, f32[4]{0:T(128)S(1)}, u32[]{:S(2)}, u32[]{:S(2)}) collective-permute-start(f32[4]{0:T(128)S(1)} %max.12), channel_id=1, source_target_pairs={{0,8},{4,12},{8,0},{12,4},{1,9},{5,13},{9,1},{13,5},{2,10},{6,14},... | collective-permute-start | bytes 56 | tf_op jit(solution)/shard_map/ppermute | solution.py:405
  87.8 2.1 %collective-permute-done.2 = f32[4]{0:T(128)S(1)} collective-permute-done((f32[4]{0:T(128)S(1)}, f32[4]{0:T(128)S(1)}, u32[]{:S(2)}, u32[]{:S(2)}) %collective-permute-start.2) | collective-permute-done | bytes 48 | tf_op jit(solution)/shard_map/ppermute | solution.py:405
  89.9 1.8 %collective-permute-start.3 = (f32[4]{0:T(128)S(1)}, f32[4]{0:T(128)S(1)}, u32[]{:S(2)}, u32[]{:S(2)}) collective-permute-start(f32[4]{0:T(128)S(1)} %max.13), channel_id=1, source_target_pairs={{0,1},{1,0},{2,3},{3,2},{4,5},{5,4},{6,7},{7,6},{8,9},{9,8},{10,11... | collective-permute-start | bytes 56 | tf_op jit(solution)/shard_map/ppermute | solution.py:405
  91.7 1.8 %collective-permute-done.3 = f32[4]{0:T(128)S(1)} collective-permute-done((f32[4]{0:T(128)S(1)}, f32[4]{0:T(128)S(1)}, u32[]{:S(2)}, u32[]{:S(2)}) %collective-permute-start.3) | collective-permute-done | bytes 48 | tf_op jit(solution)/shard_map/ppermute | solution.py:405
  93.5 1.1 %collective-permute-start.4 = (f32[4]{0:T(128)S(1)}, f32[4]{0:T(128)S(1)}, u32[]{:S(2)}, u32[]{:S(2)}) collective-permute-start(f32[4]{0:T(128)S(1)} %max.14), channel_id=1, source_target_pairs={{0,2},{1,3},{2,0},{3,1},{4,6},{5,7},{6,4},{7,5},{8,10},{9,11},{10,... | collective-permute-start | bytes 56 | tf_op jit(solution)/shard_map/ppermute | solution.py:405
  94.5 3.4 %collective-permute-done.4 = f32[4]{0:T(128)S(1)} collective-permute-done((f32[4]{0:T(128)S(1)}, f32[4]{0:T(128)S(1)}, u32[]{:S(2)}, u32[]{:S(2)}) %collective-permute-start.4) | collective-permute-done | bytes 48 | tf_op jit(solution)/shard_map/ppermute | solution.py:405
  97.9 0.5 max.15
  (4 shorter events, 0.0 us)
Async XLA Ops:
  0.6 11.6 %copy-start = (bf16[512,256]{1,0:T(8,128)(2,1)S(1)}, bf16[512,256]{1,0:T(8,128)(2,1)}, u32[]{:S(2)}) copy-start(bf16[512,256]{1,0:T(8,128)(2,1)} %constant.29.clone.yb) | copy-start | bytes 786436
  0.6 11.6 %copy-start.1 = (bf16[256,256]{1,0:T(8,128)(2,1)S(1)}, bf16[256,256]{1,0:T(8,128)(2,1)}, u32[]{:S(2)}) copy-start(bf16[256,256]{1,0:T(8,128)(2,1)} %constant.28.clone.zr) | copy-start | bytes 393220
  0.7 11.6 %copy-start.2 = (bf16[256,256]{1,0:T(8,128)(2,1)S(1)}, bf16[256,256]{1,0:T(8,128)(2,1)}, u32[]{:S(2)}) copy-start(bf16[256,256]{1,0:T(8,128)(2,1)} %constant.27.clone.zh) | copy-start | bytes 393220
  0.7 9.7 %copy-start.4 = (s32[4,2048]{1,0:T(4,128)S(1)}, s32[4,2048]{1,0:T(4,128)}, u32[]{:S(2)}) copy-start(s32[4,2048]{1,0:T(4,128)} %cells_ref.1) | copy-start | bytes 98308
  0.7 11.6 %copy-start.6 = (f32[2048]{0:T(1024)S(1)}, f32[2048]{0:T(1024)}, u32[]{:S(2)}) copy-start(f32[2048]{0:T(1024)} %param.12) | copy-start | bytes 24580
  0.7 11.6 %copy-start.5 = (f32[2048]{0:T(1024)S(1)}, f32[2048]{0:T(1024)}, u32[]{:S(2)}) copy-start(f32[2048]{0:T(1024)} %param.11) | copy-start | bytes 24580
  3.1 21.8 %all-to-all-start = ((f32[32,32,128]{2,1,0:T(8,128)}), f32[32,32,128]{2,1,0:T(8,128)S(1)}, u32[]{:S(2)}, u32[]{:S(2)}) async-start(f32[32,32,128]{2,1,0:T(8,128)} %bitcast.9), calls=%async_computation | async-start | bytes 1048576 | tf_op jit(solution)/shard_map/all_to_all | solution.py:354
  10.4 8.2 %collective-permute-start = (s32[4,2048]{1,0:T(4,128)S(1)}, s32[4,2048]{1,0:T(4,128)S(1)}, u32[]{:S(2)}, u32[]{:S(2)}) collective-permute-start(s32[4,2048]{1,0:T(4,128)S(1)} %copy-done.4), channel_id=1, source_target_pairs={{0,16},{16,0},{1,17},{17,1},{2,18},{18,2},{3,19},{19,3},{4,20},{20... | collective-permute-start | bytes 98312 | tf_op jit(solution)/shard_map/ppermute | solution.py:353
  29.5 51.9 %copy-start.3 = (bf16[256,256]{1,0:T(8,128)(2,1)S(1)}, bf16[256,256]{1,0:T(8,128)(2,1)}, u32[]{:S(2)}) copy-start(bf16[256,256]{1,0:T(8,128)(2,1)} %constant.31.clone.matrix_ref) | copy-start | bytes 393220
  83.8 2.5 %collective-permute-start.1 = (f32[4]{0:T(128)S(1)}, f32[4]{0:T(128)S(1)}, u32[]{:S(2)}, u32[]{:S(2)}) collective-permute-start(f32[4]{0:T(128)S(1)} %get-tuple-element.17), channel_id=1, source_target_pairs={{0,4},{4,0},{8,12},{12,8},{1,5},{5,1},{9,13},{13,9},{2,6},{6,2},{1... | collective-permute-start | bytes 56 | tf_op jit(solution)/shard_map/ppermute | solution.py:405
  86.3 3.6 %collective-permute-start.2 = (f32[4]{0:T(128)S(1)}, f32[4]{0:T(128)S(1)}, u32[]{:S(2)}, u32[]{:S(2)}) collective-permute-start(f32[4]{0:T(128)S(1)} %max.12), channel_id=1, source_target_pairs={{0,8},{4,12},{8,0},{12,4},{1,9},{5,13},{9,1},{13,5},{2,10},{6,14},... | collective-permute-start | bytes 56 | tf_op jit(solution)/shard_map/ppermute | solution.py:405
  89.9 3.6 %collective-permute-start.3 = (f32[4]{0:T(128)S(1)}, f32[4]{0:T(128)S(1)}, u32[]{:S(2)}, u32[]{:S(2)}) collective-permute-start(f32[4]{0:T(128)S(1)} %max.13), channel_id=1, source_target_pairs={{0,1},{1,0},{2,3},{3,2},{4,5},{5,4},{6,7},{7,6},{8,9},{9,8},{10,11... | collective-permute-start | bytes 56 | tf_op jit(solution)/shard_map/ppermute | solution.py:405
  93.5 4.5 %collective-permute-start.4 = (f32[4]{0:T(128)S(1)}, f32[4]{0:T(128)S(1)}, u32[]{:S(2)}, u32[]{:S(2)}) collective-permute-start(f32[4]{0:T(128)S(1)} %max.14), channel_id=1, source_target_pairs={{0,2},{1,3},{2,0},{3,1},{4,6},{5,7},{6,4},{7,5},{8,10},{9,11},{10,... | collective-permute-start | bytes 56 | tf_op jit(solution)/shard_map/ppermute | solution.py:405
